TPU v7x, 32 devices: a whole 2x2x4 slice. The times are simulated.
32 devices in a mesh: row: 8 (over z, x), col: 4 (over y, core).
Axes of the slice: x: 2, y: 2, z: 4, core: 2. Of those that a mesh axis runs over, the one named last changes fastest.
Arguments:
- object_field: float32 [2, 2, 4096, 2048], P(None, None, 'row', 'col'), may hold values from -5 to 5
- probe_field: float32 [2, 256, 256], replicated, may hold values from -6 to 6
- propagator_phase: float32 [256, 256], replicated, may hold values from -3.140625 to 3.140625
- positions: int32 [8, 4, 4, 2], P('row', 'col'), may hold values from 0 to 511
- counts: int32 [8, 4], P('row', 'col'), may hold values from 2 to 4, as said below
- amplitudes: bfloat16 [8, 4, 4, 256, 256], P('row', 'col'), may hold values from 0.19921875 to 2.5
Outputs:
- object_gradient: float32 [2, 2, 4096, 2048], P(None, None, 'row', 'col')
Inputs may be any that keep to these rules, and one draw needn't show every extreme that they name: `counts`: each tile holds from 2 to 4 live slots; in every draw some tile holds 4 and some tile holds 2.
All inputs are finite; a program needn't handle non-finite values.
Results may differ from a plain program's by a relative error of at most 0.018.
Values sent between devices are 32-bit elements; how exact they have to be, the bound alone decides.
No kernel may reach another device: no remote copies, remote signals or barrier semaphores. Data moves between devices by JAX's collectives and lax.ppermute only.
A program may use at most 128 MiB of HBM per device.

v0:
```python
import functools
import math

import jax
import jax.numpy as jnp
from jax import lax
from jax.experimental import pallas as pl
from jax.experimental.pallas import tpu as pltpu
from jax.sharding import PartitionSpec as P


floor_value = 0.1
lanes = 128


def shifted(block, axis, distance):
    devices = range(lax.axis_size(axis))
    route = [((i - distance) % len(devices), i) for i in devices]
    return lax.ppermute(block, axis, route)


def dft_tables(length):
    indices = jnp.arange(length, dtype=jnp.int32)
    turns = indices[:, None] * indices[None, :] % length
    angles = turns.astype(jnp.float32) * (2.0 * math.pi / length)
    cosine = jnp.cos(angles) / math.sqrt(length)
    sine = jnp.sin(angles) / math.sqrt(length)
    table_a = jnp.concatenate(
        [jnp.concatenate([cosine, sine], 1), jnp.concatenate([-sine, cosine], 1)], 0
    )
    table_b = jnp.concatenate(
        [jnp.concatenate([cosine, -sine], 1), jnp.concatenate([sine, cosine], 1)], 0
    )
    return (table_a.astype(jnp.bfloat16), table_b.astype(jnp.bfloat16))


def transforms(waves, left_table, right_table):
    length = waves[0][0].shape[0]
    stacked = [jnp.concatenate([part.astype(jnp.bfloat16) for part in wave], 0) for wave in waves]
    middles = [jnp.dot(left_table, s, preferred_element_type=jnp.float32) for s in stacked]
    middles = [m.astype(jnp.bfloat16) for m in middles]
    middles = [jnp.concatenate([m[:length], m[length:]], 1) for m in middles]
    results = [jnp.dot(m, right_table, preferred_element_type=jnp.float32) for m in middles]
    return [(r[:, :length], r[:, length:]) for r in results]


def product_of(left, right):
    return left[0] * right[0] - left[1] * right[1], left[0] * right[1] + left[1] * right[0]


def conj_product(left, right):
    return left[0] * right[0] + left[1] * right[1], left[1] * right[0] - left[0] * right[1]


def strip_copies(array, strips, row0, store, sem, outward):
    copies = []
    for s in range(array.shape[0]):
        for c in range(array.shape[1]):
            for k, strip in enumerate(strips):
                whole = array.at[s, c, :, pl.ds(k * lanes, lanes)]
                part = store.at[s, c, strip, pl.ds(row0, array.shape[2]), :]
                source, target = (part, whole) if outward else (whole, part)
                copies.append(pltpu.make_async_copy(source, target, sem))
    return copies


def run_copies(groups):
    copies = [copy for group in groups for copy in group]
    for copy in copies:
        copy.start()
    return copies


def process_slots(wanted, places, count, window, gradient, constants, todo):
    probe_ref, propagator_ref, measured_ref, table_a_ref, table_b_ref = constants
    length = probe_ref.shape[-1]
    halo_strips = length // lanes
    lane = lax.broadcasted_iota(jnp.int32, (length, lanes), 1)

    def pick(slot, found):
        chosen = jnp.logical_and(
            slot < count[0], wanted(places[2 * slot], places[2 * slot + 1])
        )

        @pl.when(chosen)
        def _():
            todo[found] = slot

        return found + chosen.astype(jnp.int32)

    found = lax.fori_loop(0, measured_ref.shape[0], pick, jnp.int32(0))

    def fetch(s, spot):
        row, strip, shift = spot
        back = lax.rem(lanes - shift, lanes)
        out = []
        for c in range(2):
            rolled = [
                pltpu.roll(window[s, c, strip + k, pl.ds(row, length), :], back, 1)
                for k in range(halo_strips + 1)
            ]
            parts = [
                jnp.where(lane < lanes - shift, rolled[k], rolled[k + 1])
                for k in range(halo_strips)
            ]
            out.append(jnp.concatenate(parts, 1))
        return tuple(out)

    def accumulate(s, spot, wave):
        row, strip, shift = spot
        for c in range(2):
            rolled = [
                pltpu.roll(wave[c][:, k * lanes : (k + 1) * lanes], shift, 1)
                for k in range(halo_strips)
            ]
            for k in range(halo_strips + 1):
                if k == 0:
                    part = jnp.where(lane >= shift, rolled[0], 0.0)
                elif k == halo_strips:
                    part = jnp.where(lane < shift, rolled[k - 1], 0.0)
                else:
                    part = jnp.where(lane < shift, rolled[k - 1], rolled[k])
                at = (s, c, strip + k, pl.ds(row, length), slice(None))
                gradient[at] = gradient[at] + part

    def run_slots(slots):
        table_a = table_a_ref[...]
        table_b = table_b_ref[...]
        spots = []
        for slot in slots:
            column = places[2 * slot + 1]
            spots.append((places[2 * slot], column // lanes, lax.rem(column, lanes)))
        probe = (probe_ref[0], probe_ref[1])
        propagator = (propagator_ref[0], propagator_ref[1])
        lits = [product_of(probe, fetch(0, spot)) for spot in spots]
        spreads = transforms(lits, table_a, table_b)
        spreads = transforms([product_of(propagator, w) for w in spreads], table_b, table_a)
        exits = [product_of(spread, fetch(1, spot)) for spread, spot in zip(spreads, spots)]
        fars = transforms(exits, table_a, table_b)
        residuals = []
        for far, slot in zip(fars, slots):
            power = far[0] * far[0] + far[1] * far[1]
            measured = measured_ref[slot].astype(jnp.float32)
            ratio = 1.0 - measured * jnp.minimum(lax.rsqrt(power), 1.0 / floor_value)
            residuals.append((far[0] * ratio, far[1] * ratio))
        backs = transforms(residuals, table_b, table_a)
        for back, spread, spot in zip(backs, spreads, spots):
            accumulate(1, spot, conj_product(back, spread))
        inners = [conj_product(back, fetch(1, spot)) for back, spot in zip(backs, spots)]
        inners = transforms(inners, table_a, table_b)
        firsts = transforms([conj_product(w, propagator) for w in inners], table_b, table_a)
        for first, spot in zip(firsts, spots):
            accumulate(0, spot, conj_product(first, probe))

    def pair(index, carry):
        run_slots([todo[2 * index], todo[2 * index + 1]])
        return carry

    lax.fori_loop(0, found // 2, pair, 0)

    @pl.when(lax.rem(found, 2) == 1)
    def _():
        run_slots([todo[found - 1]])


def sizes(object_shape, length):
    tile = object_shape[-1]
    own = range(tile // lanes)
    near = range(length // lanes)
    far = range(length // lanes, tile // lanes)
    past = range(tile // lanes, (tile + length) // lanes)
    return tile, own, near, far, past


def first_kernel(split, places, count, object_ref, *rest):
    constants, (window, gradient), (todo, sem) = rest[:5], rest[5:7], rest[7:]
    length = constants[0].shape[-1]
    tile, own, _, _, _ = sizes(object_ref.shape, length)
    loads = run_copies([strip_copies(object_ref, own, 0, window, sem, False)])
    gradient[...] = jnp.zeros_like(gradient)
    for copy in loads:
        copy.wait()

    def wanted(row, column):
        return jnp.logical_and(row <= tile - length, column <= tile - length)

    process_slots(wanted, places, count, window, gradient, constants, todo)


def second_kernel(split, places, count, near_ref, far_ref, corner_ref, right_ref, *rest):
    constants, (window, gradient), (todo, sem) = rest[:5], rest[7:9], rest[9:]
    length = constants[0].shape[-1]
    tile, _, near, far, past = sizes((right_ref.shape[2],), length)
    loads = run_copies(
        [
            strip_copies(near_ref, near, tile, window, sem, False),
            strip_copies(far_ref, far, tile, window, sem, False),
            strip_copies(corner_ref, past, tile, window, sem, False),
            strip_copies(right_ref, past, 0, window, sem, False),
        ]
    )
    for copy in loads:
        copy.wait()

    def wanted(row, column):
        early = jnp.logical_and(row <= tile - length, column <= tile - length)
        return jnp.logical_and(row <= tile - length + split, jnp.logical_not(early))

    process_slots(wanted, places, count, window, gradient, constants, todo)


def third_kernel(split, places, count, near_ref, far_ref, corner_ref, *rest):
    constants = rest[:5]
    near_out, far_out, corner_out, window, gradient, todo, sem = rest[7:]
    length = constants[0].shape[-1]
    tile, _, near, far, past = sizes((near_ref.shape[3] + far_ref.shape[3],), length)
    loads = run_copies(
        [
            strip_copies(near_ref, near, tile + split, window, sem, False),
            strip_copies(far_ref, far, tile + split, window, sem, False),
            strip_copies(corner_ref, past, tile + split, window, sem, False),
        ]
    )
    for copy in loads:
        copy.wait()

    def wanted(row, column):
        return row > tile - length + split

    process_slots(wanted, places, count, window, gradient, constants, todo)
    stores = run_copies(
        [
            strip_copies(corner_out, past, tile, gradient, sem, True),
            strip_copies(far_out, far, tile, gradient, sem, True),
            strip_copies(near_out, near, tile, gradient, sem, True),
        ]
    )
    for copy in stores:
        copy.wait()


def own_kernel(gradient, own_out, right_out, sem):
    _, own, _, _, past = sizes(own_out.shape, right_out.shape[-1])
    stores = run_copies(
        [
            strip_copies(right_out, past, 0, gradient, sem, True),
            strip_copies(own_out, own, 0, gradient, sem, True),
        ]
    )
    for copy in stores:
        copy.wait()


def add_kernel(column, gradient_in, piece_ref, gradient_out, held, added, sems):
    del gradient_in
    slices, parts, rows, columns = piece_ref.shape
    planes = [(s, c) for s in range(slices) for c in range(parts)]

    def spot(s, c):
        return gradient_out.at[s, c, pl.ds(0, rows), pl.ds(column, columns)]

    loads, pieces, stores = [], [], []
    for i, (s, c) in enumerate(planes):
        loads.append(pltpu.make_async_copy(spot(s, c), held.at[i], sems.at[0, i]))
        pieces.append(pltpu.make_async_copy(piece_ref.at[s, c], added.at[i], sems.at[1, i]))
        stores.append(pltpu.make_async_copy(held.at[i], spot(s, c), sems.at[2, i]))
        loads[i].start()
        pieces[i].start()
    for i in range(len(planes)):
        loads[i].wait()
        pieces[i].wait()
        held[i] = held[i] + added[i]
        stores[i].start()
    for store in stores:
        store.wait()


def add_piece(gradient, piece, column):
    slices, parts, rows, columns = piece.shape
    planes = slices * parts
    return pl.pallas_call(
        functools.partial(add_kernel, column),
        out_shape=jax.ShapeDtypeStruct(gradient.shape, gradient.dtype),
        in_specs=[any_space] * 2,
        out_specs=any_space,
        scratch_shapes=[pltpu.VMEM((planes, rows, columns), jnp.float32)] * 2
        + [pltpu.SemaphoreType.DMA((3, planes))],
        input_output_aliases={0: 0},
        compiler_params=pltpu.CompilerParams(vmem_limit_bytes=8 * 1024 * 1024),
    )(gradient, piece)


any_space = pl.BlockSpec(memory_space=pl.ANY)
hbm_space = pl.BlockSpec(memory_space=pltpu.HBM)
vmem_space = pl.BlockSpec(memory_space=pltpu.VMEM)
scalar_space = pl.BlockSpec(memory_space=pltpu.SMEM)


def slots_call(body, scalars, pieces, constants, state, state_shapes, out_shapes):
    first = len(scalars) + len(pieces) + len(constants)
    held = [pltpu.with_memory_space_constraint(x, pltpu.VMEM) for x in (*constants, *state)]
    aliases = {first + i: len(out_shapes) + i for i in range(len(state))}
    return pl.pallas_call(
        body,
        out_shape=[jax.ShapeDtypeStruct(s, jnp.float32) for s in out_shapes]
        + [pltpu.VMEM(s, jnp.float32) for s in state_shapes],
        in_specs=[scalar_space] * len(scalars)
        + [any_space if state else hbm_space] * len(pieces)
        + [vmem_space] * len(held),
        out_specs=[any_space] * len(out_shapes) + [vmem_space] * len(state_shapes),
        scratch_shapes=[
            pltpu.SMEM((constants[2].shape[0],), jnp.int32),
            pltpu.SemaphoreType.DMA,
        ],
        input_output_aliases=aliases,
        compiler_params=pltpu.CompilerParams(vmem_limit_bytes=20 * 1024 * 1024),
    )(*scalars, *pieces, *held)


def tile_gradient(object_field, probe_field, propagator_phase, positions, counts, amplitudes):
    length = probe_field.shape[-1]
    tile = object_field.shape[-1]
    split = length // 2
    slices, parts = object_field.shape[:2]
    top_near = object_field[:, :, :split, :length]
    top_far = object_field[:, :, :split, length:]
    top_near, top_far, later = lax.optimization_barrier((top_near, top_far, object_field))
    top_near = shifted(top_near, "row", -1)
    top_far = shifted(top_far, "row", -1)
    bottom_near = later[:, :, split:length, :length]
    bottom_far = later[:, :, split:length, length:]
    right = shifted(later[:, :, :, :length], "col", -1)
    bottom_near = shifted(bottom_near, "row", -1)
    bottom_far = shifted(bottom_far, "row", -1)
    top_corner = shifted(top_near, "col", -1)
    bottom_corner = shifted(bottom_near, "col", -1)
    propagator = jnp.stack([jnp.cos(propagator_phase), jnp.sin(propagator_phase)], 0)
    constants = (probe_field, propagator, amplitudes[0, 0], *dft_tables(length))
    scalars = (positions.reshape(-1), counts.reshape(-1))
    strips = (slices, parts, (tile + length) // lanes, tile + length, lanes)

    def call(kernel, pieces, state, out_shapes):
        body = functools.partial(kernel, split)
        return slots_call(body, scalars, pieces, constants, state, (strips, strips), out_shapes)

    state = call(first_kernel, (object_field,), (), ())
    state = call(second_kernel, (top_near, top_far, top_corner, right), state, ())
    lower_near, lower_far, corner, _, gradient = call(
        third_kernel,
        (bottom_near, bottom_far, bottom_corner),
        state,
        (
            (slices, parts, length, length),
            (slices, parts, length, tile - length),
            (slices, parts, length, length),
        ),
    )
    corner = shifted(corner, "col", 1)
    lower_far = shifted(lower_far, "row", 1)
    own, right = pl.pallas_call(
        own_kernel,
        name="own",
        out_shape=[
            jax.ShapeDtypeStruct(object_field.shape, jnp.float32),
            jax.ShapeDtypeStruct((slices, parts, tile, length), jnp.float32),
        ],
        in_specs=[vmem_space],
        out_specs=[any_space] * 2,
        scratch_shapes=[pltpu.SemaphoreType.DMA],
        compiler_params=pltpu.CompilerParams(vmem_limit_bytes=4 * 1024 * 1024),
    )(pltpu.with_memory_space_constraint(gradient, pltpu.VMEM))
    corner, right = lax.optimization_barrier((corner, right))
    lower_near = shifted(lower_near + corner, "row", 1)
    right = shifted(right, "col", 1)
    gradient = add_piece(own, right, 0)
    gradient = add_piece(gradient, lower_far, length)
    return add_piece(gradient, lower_near, 0)


def solution(mesh):
    return jax.shard_map(
        tile_gradient,
        mesh=mesh,
        in_specs=(
            P(None, None, "row", "col"),
            P(),
            P(),
            P("row", "col", None, None),
            P("row", "col"),
            P("row", "col", None, None, None),
        ),
        out_specs=P(None, None, "row", "col"),
        check_vma=False,
    )
```

profile of v0, /device:TPU:0, one launch (start us, length us, event | category | flops | bytes accessed | tf_op | source)
XLA Modules:
  0.0 130.7 jit_solution(17408943927840491968)
XLA Ops:
  0.0 2.1 %fusion.10 = (f32[2,2,128,256]{3,2,1,0:T(8,128)}, f32[2,2,128,256]{3,2,1,0:T(8,128)S(1)}) fusion(f32[2,2,512,512]{3,2,1,0:T(8,128)} %object_ref.1), kind=kLoop, calls=%fused_computation.23 | loop fusion | bytes 2097152 | tf_op jit(solution)/shard_map/slice | solution.py:326
  2.1 3.1 %slice.19 = f32[2,2,512,256]{3,2,1,0:T(8,128)} slice(f32[2,2,512,512]{3,2,1,0:T(8,128)} %object_ref.1), slice={[0:2], [0:2], [0:512], [0:256]} | slice | bytes 4194304 | tf_op jit(solution)/shard_map/slice | solution.py:332
  5.2 2.4 %collective-permute-start.6 = (f32[2,2,512,256]{3,2,1,0:T(8,128)}, f32[2,2,512,256]{3,2,1,0:T(8,128)S(1)}, u32[]{:S(2)}, u32[]{:S(2)}) collective-permute-start(f32[2,2,512,256]{3,2,1,0:T(8,128)} %slice.19), channel_id=1, source_target_pairs={{1,0},{2,1},{3,2},{0,3},{5,4},{6,5},{7,6},{4,7},{9,8},{10,9},{11,1... | collective-permute-start | bytes 6291464 | tf_op jit(solution)/shard_map/ppermute | solution.py:19
  7.7 4.5 %collective-permute-start.3 = (f32[2,2,128,256]{3,2,1,0:T(8,128)S(1)}, f32[2,2,128,256]{3,2,1,0:T(8,128)}, u32[]{:S(2)}, u32[]{:S(2)}) collective-permute-start(f32[2,2,128,256]{3,2,1,0:T(8,128)S(1)} %get-tuple-element.21), channel_id=1, source_target_pairs={{4,0},{8,4},{12,8},{16,12},{20,16},{24,20},{28,24},{0,28},{5,1},{9... | collective-permute-start | bytes 1572872 | tf_op jit(solution)/shard_map/ppermute | solution.py:19
  12.2 2.1 %fusion.9 = (f32[2,2,128,256]{3,2,1,0:T(8,128)}, f32[2,2,128,256]{3,2,1,0:T(8,128)S(1)}) fusion(f32[2,2,512,512]{3,2,1,0:T(8,128)} %object_ref.1), kind=kLoop, calls=%fused_computation.22 | loop fusion | bytes 2097152 | tf_op jit(solution)/shard_map/slice | solution.py:331
  14.3 0.5 collective-permute-start
  14.8 1.4 %collective-permute-start.4 = (f32[2,2,128,256]{3,2,1,0:T(8,128)}, f32[2,2,128,256]{3,2,1,0:T(8,128)}, u32[]{:S(2)}, u32[]{:S(2)}) collective-permute-start(f32[2,2,128,256]{3,2,1,0:T(8,128)} %get-tuple-element.22), channel_id=1, source_target_pairs={{4,0},{8,4},{12,8},{16,12},{20,16},{24,20},{28,24},{0,28},{5,1},{9... | collective-permute-start | bytes 1572872 | tf_op jit(solution)/shard_map/ppermute | solution.py:19
  16.2 0.5 collective-permute-start.1
  16.7 1.1 negate_convert_fusion
  17.8 6.7 %collective-permute-done.3.near_ref = f32[2,2,128,256]{3,2,1,0:T(8,128)} collective-permute-done((f32[2,2,128,256]{3,2,1,0:T(8,128)S(1)}, f32[2,2,128,256]{3,2,1,0:T(8,128)}, u32[]{:S(2)}, u32[]{:S(2)}) %collective-permute-start.3) | collective-permute-done | bytes 524320 | tf_op jit(solution)/shard_map/ppermute | solution.py:19
  24.5 11.2 %collective-permute-done.near_ref = f32[2,2,128,256]{3,2,1,0:T(8,128)} collective-permute-done((f32[2,2,128,256]{3,2,1,0:T(8,128)S(1)}, f32[2,2,128,256]{3,2,1,0:T(8,128)}, u32[]{:S(2)}, u32[]{:S(2)}) %collective-permute-start) | collective-permute-done | bytes 524320 | tf_op jit(solution)/shard_map/ppermute | solution.py:19
  35.7 1.0 fusion.8
  36.7 0.1 copy.15
  37.6 1.9 %cosine_bitcast_fusion = (f32[1,256,256]{2,1,0:T(8,128)S(1)}, f32[1,256,256]{2,1,0:T(8,128)S(1)}) fusion(f32[256,256]{1,0:T(8,128)} %param.8), kind=kLoop, calls=%fused_computation.19 | loop fusion | bytes 786432 | tf_op jit(solution)/shard_map/stack | solution.py:337
  39.6 2.2 %copy-done = f32[2,2,512,512]{3,2,1,0:T(8,128)S(1)} copy-done((f32[2,2,512,512]{3,2,1,0:T(8,128)S(1)}, f32[2,2,512,512]{3,2,1,0:T(8,128)}, u32[]{:S(2)}) %copy-start) | copy-done | bytes 4194328
  41.8 7.1 %shard_map.64 = (f32[2,2,6,768,128]{4,3,2,1,0:T(8,128)S(1)}, f32[2,2,6,768,128]{4,3,2,1,0:T(8,128)S(1)}) custom-call(s32[8]{0:T(128)S(1)} %reshape.6.places, s32[1]{0:T(128)} %bitcast.6.count, f32[2,2,512,512]{3,2,1,0:T(8,128)S(1)} %copy-done, f32[2,256,256]{2,1,0:T(8,128)S(1)} %copy-done.1, f32[2,256,256]{2,1,0:T(8,128)S(1)} %pad_maximum_fusion.4.rest_1_, ...), custom_call_target="tpu_custom_call" | custom-call | tf_op jit(solution)/shard_map/pallas_call | solution.py:303
  48.9 7.1 %shard_map.65 = (f32[2,2,6,768,128]{4,3,2,1,0:T(8,128)S(1)}, f32[2,2,6,768,128]{4,3,2,1,0:T(8,128)S(1)}) custom-call(s32[8]{0:T(128)S(1)} %reshape.6.places, s32[1]{0:T(128)} %bitcast.7.count, f32[2,2,128,256]{3,2,1,0:T(8,128)} %collective-permute-done.3.near_ref, ...), custom_call_target="tpu_custom_call", output_to_operand_aliasing={{0}: (11, {}), {1}: (12, {})} | custom-call | tf_op jit(solution)/shard_map/pallas_call | solution.py:303
  56.0 0.9 collective-permute-done.1.far_ref
  56.9 2.2 %shard_map.66 = (f32[2,2,256,256]{3,2,1,0:T(8,128)S(1)}, f32[2,2,256,256]{3,2,1,0:T(8,128)S(1)}, f32[2,2,256,256]{3,2,1,0:T(8,128)S(1)}, f32[2,2,6,768,128]{4,3,2,1,0:T(8,128)S(1)}, f32[2,2,6,768,128]{4,3,2,1,0:T(8,128)S(1)}) custom-call(s32[8]{0:T(128)S(1)} %reshape.6.places, s32[1]{0:T(128)} %bitcast.8.count, ...), custom_call_target="tpu_custom_call", output_to_operand_aliasing={{3}: (10, {}), {4}: (11, {})} | custom-call | tf_op jit(solution)/shard_map/pallas_call | solution.py:303
  59.1 3.1 %collective-permute-start.7 = (f32[2,2,256,256]{3,2,1,0:T(8,128)S(1)}, f32[2,2,256,256]{3,2,1,0:T(8,128)S(1)}, u32[]{:S(2)}, u32[]{:S(2)}) collective-permute-start(f32[2,2,256,256]{3,2,1,0:T(8,128)S(1)} %get-tuple-element.29), channel_id=1, source_target_pairs={{3,0},{0,1},{1,2},{2,3},{7,4},{4,5},{5,6},{6,7},{11,8},{8,9},{9,10... | collective-permute-start | bytes 3145736 | tf_op jit(solution)/shard_map/ppermute | solution.py:19
  62.3 2.2 %own.1 = (f32[2,2,512,512]{3,2,1,0:T(8,128)}, f32[2,2,512,256]{3,2,1,0:T(8,128)S(1)}) custom-call(f32[2,2,6,768,128]{4,3,2,1,0:T(8,128)S(1)} %get-tuple-element.27.gradient), custom_call_target="tpu_custom_call" | custom-call | tf_op jit(solution)/shard_map/own/pallas_call | solution.py:360
  64.4 9.0 %collective-permute-done.7 = f32[2,2,256,256]{3,2,1,0:T(8,128)S(1)} collective-permute-done((f32[2,2,256,256]{3,2,1,0:T(8,128)S(1)}, f32[2,2,256,256]{3,2,1,0:T(8,128)S(1)}, u32[]{:S(2)}, u32[]{:S(2)}) %collective-permute-start.7) | collective-permute-done | bytes 1048608 | tf_op jit(solution)/shard_map/ppermute | solution.py:19
  73.4 0.6 collective-permute-start.8
  74.0 4.1 %collective-permute-start.9 = (f32[2,2,256,256]{3,2,1,0:T(8,128)S(1)}, f32[2,2,256,256]{3,2,1,0:T(8,128)S(1)}, u32[]{:S(2)}, u32[]{:S(2)}) collective-permute-start(f32[2,2,256,256]{3,2,1,0:T(8,128)S(1)} %get-tuple-element.32), channel_id=1, source_target_pairs={{28,0},{0,4},{4,8},{8,12},{12,16},{16,20},{20,24},{24,28},{29,1},{... | collective-permute-start | bytes 3145736 | tf_op jit(solution)/shard_map/ppermute | solution.py:19
  78.2 0.1 add.24
  78.3 2.0 %collective-permute-start.10 = (f32[2,2,256,256]{3,2,1,0:T(8,128)S(1)}, f32[2,2,256,256]{3,2,1,0:T(8,128)S(1)}, u32[]{:S(2)}, u32[]{:S(2)}) collective-permute-start(f32[2,2,256,256]{3,2,1,0:T(8,128)S(1)} %add.24), channel_id=1, source_target_pairs={{28,0},{0,4},{4,8},{8,12},{12,16},{16,20},{20,24},{24,28},{29,1},{... | collective-permute-start | bytes 3145736 | tf_op jit(solution)/shard_map/ppermute | solution.py:19
  80.3 18.5 %collective-permute-done.8.piece_ref = f32[2,2,512,256]{3,2,1,0:T(8,128)S(1)} collective-permute-done((f32[2,2,512,256]{3,2,1,0:T(8,128)S(1)}, f32[2,2,512,256]{3,2,1,0:T(8,128)S(1)}, u32[]{:S(2)}, u32[]{:S(2)}) %collective-permute-start.8) | collective-permute-done | bytes 2097184 | tf_op jit(solution)/shard_map/ppermute | solution.py:19
  98.9 2.5 %shard_map.67.gradient_in = f32[2,2,512,512]{3,2,1,0:T(8,128)} custom-call(f32[2,2,512,512]{3,2,1,0:T(8,128)} %get-tuple-element.28.gradient_in, f32[2,2,512,256]{3,2,1,0:T(8,128)S(1)} %collective-permute-done.8.piece_ref), custom_call_target="tpu_custom_call", output_to_operand_aliasing={{}: (0, {})} | custom-call | tf_op jit(solution)/shard_map/pallas_call | solution.py:281
  101.4 4.7 %collective-permute-done.9.piece_ref = f32[2,2,256,256]{3,2,1,0:T(8,128)S(1)} collective-permute-done((f32[2,2,256,256]{3,2,1,0:T(8,128)S(1)}, f32[2,2,256,256]{3,2,1,0:T(8,128)S(1)}, u32[]{:S(2)}, u32[]{:S(2)}) %collective-permute-start.9) | collective-permute-done | bytes 1048608 | tf_op jit(solution)/shard_map/ppermute | solution.py:19
  106.0 2.0 %shard_map.68.gradient_in = f32[2,2,512,512]{3,2,1,0:T(8,128)} custom-call(f32[2,2,512,512]{3,2,1,0:T(8,128)} %shard_map.67.gradient_in, f32[2,2,256,256]{3,2,1,0:T(8,128)S(1)} %collective-permute-done.9.piece_ref), custom_call_target="tpu_custom_call", output_to_operand_aliasing={{}: (0, {})} | custom-call | tf_op jit(solution)/shard_map/pallas_call | solution.py:281
  108.1 20.4 %collective-permute-done.10.piece_ref = f32[2,2,256,256]{3,2,1,0:T(8,128)S(1)} collective-permute-done((f32[2,2,256,256]{3,2,1,0:T(8,128)S(1)}, f32[2,2,256,256]{3,2,1,0:T(8,128)S(1)}, u32[]{:S(2)}, u32[]{:S(2)}) %collective-permute-start.10) | collective-permute-done | bytes 1048608 | tf_op jit(solution)/shard_map/ppermute | solution.py:19
  128.5 2.0 %shard_map.69 = f32[2,2,512,512]{3,2,1,0:T(8,128)} custom-call(f32[2,2,512,512]{3,2,1,0:T(8,128)} %shard_map.68.gradient_in, f32[2,2,256,256]{3,2,1,0:T(8,128)S(1)} %collective-permute-done.10.piece_ref), custom_call_target="tpu_custom_call", output_to_operand_aliasing={{}: (0, {})} | custom-call | tf_op jit(solution)/shard_map/pallas_call | solution.py:281
  (16 shorter events, 0.2 us)
Async XLA Ops:
  0.0 36.7 %copy-start.3 = (s32[1,1,4,2]{2,3,1,0:T(2,128)S(1)}, s32[1,1,4,2]{2,3,1,0:T(2,128)}, u32[]{:S(2)}) copy-start(s32[1,1,4,2]{2,3,1,0:T(2,128)} %param.9) | copy-start | bytes 100
  2.1 37.5 %copy-start.1 = (f32[2,256,256]{2,1,0:T(8,128)S(1)}, f32[2,256,256]{2,1,0:T(8,128)}, u32[]{:S(2)}) copy-start(f32[2,256,256]{2,1,0:T(8,128)} %rest_0_.5) | copy-start | bytes 1572868
  2.1 37.5 %copy-start.2 = (bf16[1,1,4,256,256]{4,3,2,1,0:T(8,128)(2,1)S(1)}, bf16[1,1,4,256,256]{4,3,2,1,0:T(8,128)(2,1)}, u32[]{:S(2)}) copy-start(bf16[1,1,4,256,256]{4,3,2,1,0:T(8,128)(2,1)} %param.11) | copy-start | bytes 1572868
  5.2 43.7 %collective-permute-start.6 = (f32[2,2,512,256]{3,2,1,0:T(8,128)}, f32[2,2,512,256]{3,2,1,0:T(8,128)S(1)}, u32[]{:S(2)}, u32[]{:S(2)}) collective-permute-start(f32[2,2,512,256]{3,2,1,0:T(8,128)} %slice.19), channel_id=1, source_target_pairs={{1,0},{2,1},{3,2},{0,3},{5,4},{6,5},{7,6},{4,7},{9,8},{10,9},{11,1... | collective-permute-start | bytes 6291464 | tf_op jit(solution)/shard_map/ppermute | solution.py:19
  7.7 16.8 %collective-permute-start.3 = (f32[2,2,128,256]{3,2,1,0:T(8,128)S(1)}, f32[2,2,128,256]{3,2,1,0:T(8,128)}, u32[]{:S(2)}, u32[]{:S(2)}) collective-permute-start(f32[2,2,128,256]{3,2,1,0:T(8,128)S(1)} %get-tuple-element.21), channel_id=1, source_target_pairs={{4,0},{8,4},{12,8},{16,12},{20,16},{24,20},{28,24},{0,28},{5,1},{9... | collective-permute-start | bytes 1572872 | tf_op jit(solution)/shard_map/ppermute | solution.py:19
  14.3 21.5 %collective-permute-start = (f32[2,2,128,256]{3,2,1,0:T(8,128)S(1)}, f32[2,2,128,256]{3,2,1,0:T(8,128)}, u32[]{:S(2)}, u32[]{:S(2)}) collective-permute-start(f32[2,2,128,256]{3,2,1,0:T(8,128)S(1)} %get-tuple-element.36), channel_id=1, source_target_pairs={{4,0},{8,4},{12,8},{16,12},{20,16},{24,20},{28,24},{0,28},{5,1},{9... | collective-permute-start | bytes 1572872 | tf_op jit(solution)/shard_map/ppermute | solution.py:19
  14.8 34.1 %collective-permute-start.4 = (f32[2,2,128,256]{3,2,1,0:T(8,128)}, f32[2,2,128,256]{3,2,1,0:T(8,128)}, u32[]{:S(2)}, u32[]{:S(2)}) collective-permute-start(f32[2,2,128,256]{3,2,1,0:T(8,128)} %get-tuple-element.22), channel_id=1, source_target_pairs={{4,0},{8,4},{12,8},{16,12},{20,16},{24,20},{28,24},{0,28},{5,1},{9... | collective-permute-start | bytes 1572872 | tf_op jit(solution)/shard_map/ppermute | solution.py:19
  16.2 40.7 %collective-permute-start.1 = (f32[2,2,128,256]{3,2,1,0:T(8,128)}, f32[2,2,128,256]{3,2,1,0:T(8,128)}, u32[]{:S(2)}, u32[]{:S(2)}) collective-permute-start(f32[2,2,128,256]{3,2,1,0:T(8,128)} %get-tuple-element.35), channel_id=1, source_target_pairs={{4,0},{8,4},{12,8},{16,12},{20,16},{24,20},{28,24},{0,28},{5,1},{9... | collective-permute-start | bytes 1572872 | tf_op jit(solution)/shard_map/ppermute | solution.py:19
  24.5 24.4 %collective-permute-start.5 = (f32[2,2,128,256]{3,2,1,0:T(8,128)}, f32[2,2,128,256]{3,2,1,0:T(8,128)}, u32[]{:S(2)}, u32[]{:S(2)}) collective-permute-start(f32[2,2,128,256]{3,2,1,0:T(8,128)} %collective-permute-done.3.near_ref), channel_id=1, source_target_pairs={{1,0},{2,1},{3,2},{0,3},{5,4},{6,5},{7,6},{4,7},{9,8},{10,9},{11,1... | collective-permute-start | bytes 1572872 | tf_op jit(solution)/shard_map/ppermute | solution.py:19
  35.7 21.2 %collective-permute-start.2 = (f32[2,2,128,256]{3,2,1,0:T(8,128)}, f32[2,2,128,256]{3,2,1,0:T(8,128)}, u32[]{:S(2)}, u32[]{:S(2)}) collective-permute-start(f32[2,2,128,256]{3,2,1,0:T(8,128)} %collective-permute-done.near_ref), channel_id=1, source_target_pairs={{1,0},{2,1},{3,2},{0,3},{5,4},{6,5},{7,6},{4,7},{9,8},{10,9},{11,1... | collective-permute-start | bytes 1572872 | tf_op jit(solution)/shard_map/ppermute | solution.py:19
  39.6 2.2 %copy-start = (f32[2,2,512,512]{3,2,1,0:T(8,128)S(1)}, f32[2,2,512,512]{3,2,1,0:T(8,128)}, u32[]{:S(2)}) copy-start(f32[2,2,512,512]{3,2,1,0:T(8,128)} %object_ref.1) | copy-start | bytes 12582916
  59.1 14.3 %collective-permute-start.7 = (f32[2,2,256,256]{3,2,1,0:T(8,128)S(1)}, f32[2,2,256,256]{3,2,1,0:T(8,128)S(1)}, u32[]{:S(2)}, u32[]{:S(2)}) collective-permute-start(f32[2,2,256,256]{3,2,1,0:T(8,128)S(1)} %get-tuple-element.29), channel_id=1, source_target_pairs={{3,0},{0,1},{1,2},{2,3},{7,4},{4,5},{5,6},{6,7},{11,8},{8,9},{9,10... | collective-permute-start | bytes 3145736 | tf_op jit(solution)/shard_map/ppermute | solution.py:19
  73.4 25.5 %collective-permute-start.8 = (f32[2,2,512,256]{3,2,1,0:T(8,128)S(1)}, f32[2,2,512,256]{3,2,1,0:T(8,128)S(1)}, u32[]{:S(2)}, u32[]{:S(2)}) collective-permute-start(f32[2,2,512,256]{3,2,1,0:T(8,128)S(1)} %get-tuple-element.31), channel_id=1, source_target_pairs={{3,0},{0,1},{1,2},{2,3},{7,4},{4,5},{5,6},{6,7},{11,8},{8,9},{9,10... | collective-permute-start | bytes 6291464 | tf_op jit(solution)/shard_map/ppermute | solution.py:19
  74.0 32.0 %collective-permute-start.9 = (f32[2,2,256,256]{3,2,1,0:T(8,128)S(1)}, f32[2,2,256,256]{3,2,1,0:T(8,128)S(1)}, u32[]{:S(2)}, u32[]{:S(2)}) collective-permute-start(f32[2,2,256,256]{3,2,1,0:T(8,128)S(1)} %get-tuple-element.32), channel_id=1, source_target_pairs={{28,0},{0,4},{4,8},{8,12},{12,16},{16,20},{20,24},{24,28},{29,1},{... | collective-permute-start | bytes 3145736 | tf_op jit(solution)/shard_map/ppermute | solution.py:19
  78.3 50.2 %collective-permute-start.10 = (f32[2,2,256,256]{3,2,1,0:T(8,128)S(1)}, f32[2,2,256,256]{3,2,1,0:T(8,128)S(1)}, u32[]{:S(2)}, u32[]{:S(2)}) collective-permute-start(f32[2,2,256,256]{3,2,1,0:T(8,128)S(1)} %add.24), channel_id=1, source_target_pairs={{28,0},{0,4},{4,8},{8,12},{12,16},{16,20},{20,24},{24,28},{29,1},{... | collective-permute-start | bytes 3145736 | tf_op jit(solution)/shard_map/ppermute | solution.py:19
where the time goes:
time: 131 us
  waiting for transfers between devices  71.4 us (55%)
  Pallas kernels  25.2 us (19%)
  starting transfers between devices  19.3 us (15%)
  local copies, waits for them, and re-layouts  11.5 us (9%)
  other arithmetic  2.34 us (2%)
    ppermute x11, waiting for transfers between devices, shifted(): return lax.ppermute(block, axis, route)  71.4 us
    ppermute x11, starting transfers between devices, shifted(): return lax.ppermute(block, axis, route)  19.3 us
    pallas_call x3, Pallas kernels, slots_call(): pl.pallas_call(body, out_shape=[jax.ShapeDtypeStruct(s, jnp.float32) for...  16.4 us
    pallas_call x3, Pallas kernels, add_piece(): pl.pallas_call(functools.partial(add_kernel, column), out_shape=jax.Shape...  6.6 us
    slice x1, local copies, waits for them, and re-layouts, tile_gradient(): right = shifted(later[:, :, :, :length], 'col', -1)  3.13 us
  transfers between devices with their start and end apart: 11, of which 7 were waited for; matrix products, arithmetic and copies ran while one was open for 5% of the time, Pallas kernels for 16%

commit v1 on v0

v1 whole, which is shorter than its diff:
```python
import functools
import math

import jax
import jax.numpy as jnp
from jax import lax
from jax.experimental import pallas as pl
from jax.experimental.pallas import tpu as pltpu
from jax.sharding import PartitionSpec as P


floor_value = 0.1
lanes = 128


def shifted(block, axis, distance):
    devices = range(lax.axis_size(axis))
    route = [((i - distance) % len(devices), i) for i in devices]
    return lax.ppermute(block, axis, route)


def dft_tables(length):
    indices = jnp.arange(length, dtype=jnp.int32)
    turns = indices[:, None] * indices[None, :] % length
    angles = turns.astype(jnp.float32) * (2.0 * math.pi / length)
    cosine = jnp.cos(angles) / math.sqrt(length)
    sine = jnp.sin(angles) / math.sqrt(length)
    table_a = jnp.concatenate(
        [jnp.concatenate([cosine, sine], 1), jnp.concatenate([-sine, cosine], 1)], 0
    )
    table_b = jnp.concatenate(
        [jnp.concatenate([cosine, -sine], 1), jnp.concatenate([sine, cosine], 1)], 0
    )
    return (table_a.astype(jnp.bfloat16), table_b.astype(jnp.bfloat16))


def sections(stacked, left_table, right_table):
    length = stacked.shape[1]
    middle = jnp.dot(left_table, stacked, preferred_element_type=jnp.float32)
    middle = middle.astype(jnp.bfloat16)
    middle = jnp.concatenate([middle[:length], middle[length:]], 1)
    result = jnp.dot(middle, right_table, preferred_element_type=jnp.float32)
    return result[:, :length], result[:, length:]


def transform(wave, left_table, right_table):
    stacked = jnp.concatenate([part.astype(jnp.bfloat16) for part in wave], 0)
    return sections(stacked, left_table, right_table)


def product_of(left, right):
    return left[0] * right[0] - left[1] * right[1], left[0] * right[1] + left[1] * right[0]


def conj_product(left, right):
    return left[0] * right[0] + left[1] * right[1], left[1] * right[0] - left[0] * right[1]


def strip_copies(array, strips, row0, store, plane, sem, outward):
    copies = []
    for s in range(array.shape[0]):
        for c in range(array.shape[1]):
            for k, strip in enumerate(strips):
                whole = array.at[s, c, :, pl.ds(k * lanes, lanes)]
                part = store.at[plane + s, c, strip, pl.ds(row0, array.shape[2]), :]
                source, target = (part, whole) if outward else (whole, part)
                copies.append(pltpu.make_async_copy(source, target, sem))
    return copies


def run_copies(groups):
    copies = [copy for group in groups for copy in group]
    for copy in copies:
        copy.start()
    return copies


def finish(copies):
    for copy in copies:
        copy.wait()


def patch_spot(places, slot):
    column = places[2 * slot + 1]
    return places[2 * slot], column // lanes, lax.rem(column, lanes)


def fetch(window, s, spot, length):
    row, strip, shift = spot
    back = lax.rem(lanes - shift, lanes)
    lane = lax.broadcasted_iota(jnp.int32, (length, lanes), 1)
    out = []
    for c in range(2):
        rolled = [
            pltpu.roll(window[s, c, strip + k, pl.ds(row, length), :], back, 1)
            for k in range(length // lanes + 1)
        ]
        parts = [
            jnp.where(lane < lanes - shift, rolled[k], rolled[k + 1])
            for k in range(length // lanes)
        ]
        out.append(jnp.concatenate(parts, 1))
    return tuple(out)


def accumulate(gradient, s, spot, wave, length):
    row, strip, shift = spot
    lane = lax.broadcasted_iota(jnp.int32, (length, lanes), 1)
    count = length // lanes
    for c in range(2):
        rolled = [
            pltpu.roll(wave[c][:, k * lanes : (k + 1) * lanes], shift, 1) for k in range(count)
        ]
        for k in range(count + 1):
            if k == 0:
                part = jnp.where(lane >= shift, rolled[0], 0.0)
            elif k == count:
                part = jnp.where(lane < shift, rolled[k - 1], 0.0)
            else:
                part = jnp.where(lane < shift, rolled[k - 1], rolled[k])
            at = (s, c, strip + k, pl.ds(row, length), slice(None))
            gradient[at] = gradient[at] + part


def spread_slot(places, window, constants, spreads, slot):
    probe, propagator, _, table_a, table_b = constants
    length = probe.shape[-1]
    lit = product_of((probe[0], probe[1]), fetch(window, 0, patch_spot(places, slot), length))
    wave = transform(lit, table_a[...], table_b[...])
    wave = product_of((propagator[0], propagator[1]), wave)
    wave = transform(wave, table_b[...], table_a[...])
    spreads[slot, 0] = wave[0]
    spreads[slot, 1] = wave[1]


def back_slot(places, window, gradient, constants, spreads, inners, slot):
    probe, _, measured_ref, table_a, table_b = constants
    length = probe.shape[-1]
    spot = patch_spot(places, slot)
    second = fetch(window, 1, spot, length)
    spread = (spreads[slot, 0], spreads[slot, 1])
    far = transform(product_of(spread, second), table_a[...], table_b[...])
    power = far[0] * far[0] + far[1] * far[1]
    measured = measured_ref[slot].astype(jnp.float32)
    ratio = 1.0 - measured * jnp.minimum(lax.rsqrt(power), 1.0 / floor_value)
    back = transform((far[0] * ratio, far[1] * ratio), table_b[...], table_a[...])
    inner = conj_product(back, second)
    inners[slot, pl.ds(0, length), :] = inner[0].astype(jnp.bfloat16)
    inners[slot, pl.ds(length, length), :] = inner[1].astype(jnp.bfloat16)
    spread = (spreads[slot, 0], spreads[slot, 1])
    accumulate(gradient, 1, spot, conj_product(back, spread), length)


def first_slot(places, gradient, constants, inners, slot):
    probe, propagator, _, table_a, table_b = constants
    length = probe.shape[-1]
    wave = sections(inners[slot], table_a[...], table_b[...])
    wave = conj_product(wave, (propagator[0], propagator[1]))
    wave = transform(wave, table_b[...], table_a[...])
    grad = conj_product(wave, (probe[0], probe[1]))
    accumulate(gradient, 0, patch_spot(places, slot), grad, length)


def each_slot(places, count, tile, length, inside, visit):
    def step(slot, carry):
        within = jnp.logical_and(
            places[2 * slot] <= tile - length, places[2 * slot + 1] <= tile - length
        )
        if inside is None:
            visit(slot)
        else:

            @pl.when(within if inside else jnp.logical_not(within))
            def _():
                visit(slot)

        return carry

    lax.fori_loop(0, count[0], step, 0)


def sizes(tile, length):
    own = range(tile // lanes)
    near = range(length // lanes)
    far = range(length // lanes, tile // lanes)
    past = range(tile // lanes, (tile + length) // lanes)
    return own, near, far, past


def own_slots_kernel(places, count, object_ref, *rest):
    constants, (window, gradient, spreads, inners, sem) = rest[:5], rest[5:]
    length = constants[0].shape[-1]
    tile = object_ref.shape[-1]
    own, _, _, _ = sizes(tile, length)
    loads = run_copies([strip_copies(object_ref, own, 0, window, 0, sem, False)])
    gradient[...] = jnp.zeros_like(gradient)
    finish(loads)

    def visit(slot):
        spread_slot(places, window, constants, spreads, slot)
        back_slot(places, window, gradient, constants, spreads, inners, slot)

    each_slot(places, count, tile, length, True, visit)


def spread_kernel(places, count, near_ref, far_ref, corner_ref, right_ref, *rest):
    constants, (window, gradient, spreads, inners, sem) = rest[:5], rest[9:]
    length = constants[0].shape[-1]
    tile = right_ref.shape[2]
    _, near, far, past = sizes(tile, length)
    finish(
        run_copies(
            [
                strip_copies(near_ref, near, tile, window, 0, sem, False),
                strip_copies(far_ref, far, tile, window, 0, sem, False),
                strip_copies(corner_ref, past, tile, window, 0, sem, False),
                strip_copies(right_ref, past, 0, window, 0, sem, False),
            ]
        )
    )

    def visit(slot):
        spread_slot(places, window, constants, spreads, slot)

    each_slot(places, count, tile, length, False, visit)


def load_kernel(near_ref, corner_ref, right_ref, window_in, window, sem):
    del window_in
    length = near_ref.shape[3]
    tile = right_ref.shape[2]
    _, near, _, past = sizes(tile, length)
    finish(
        run_copies(
            [
                strip_copies(near_ref, near, tile, window, 1, sem, False),
                strip_copies(corner_ref, past, tile, window, 1, sem, False),
                strip_copies(right_ref, past, 0, window, 1, sem, False),
            ]
        )
    )


def back_kernel(places, count, far_ref, *rest):
    constants = rest[:5]
    near_out, far_out, corner_out, window, gradient, spreads, inners, sem = rest[9:]
    length = constants[0].shape[-1]
    tile = length + far_ref.shape[3]
    _, near, far, past = sizes(tile, length)
    finish(run_copies([strip_copies(far_ref, far, tile, window, 1, sem, False)]))

    def visit(slot):
        back_slot(places, window, gradient, constants, spreads, inners, slot)

    each_slot(places, count, tile, length, False, visit)
    finish(
        run_copies(
            [
                strip_copies(corner_out, past, tile, gradient, 1, sem, True),
                strip_copies(far_out, far, tile, gradient, 1, sem, True),
                strip_copies(near_out, near, tile, gradient, 1, sem, True),
            ]
        )
    )


def first_kernel(places, count, *rest):
    constants = rest[:5]
    near_out, far_out, corner_out, _, gradient, _, inners, sem = rest[9:]
    length = constants[0].shape[-1]
    tile = length + far_out.shape[3]
    _, near, far, past = sizes(tile, length)

    def visit(slot):
        first_slot(places, gradient, constants, inners, slot)

    each_slot(places, count, tile, length, None, visit)
    finish(
        run_copies(
            [
                strip_copies(corner_out, past, tile, gradient, 0, sem, True),
                strip_copies(far_out, far, tile, gradient, 0, sem, True),
                strip_copies(near_out, near, tile, gradient, 0, sem, True),
            ]
        )
    )


def own_kernel(gradient, own_out, right_out, sem):
    tile = own_out.shape[-1]
    own, _, _, past = sizes(tile, right_out.shape[-1])
    finish(
        run_copies(
            [
                strip_copies(right_out, past, 0, gradient, 0, sem, True),
                strip_copies(own_out, own, 0, gradient, 0, sem, True),
            ]
        )
    )


def add_kernel(plane, column, gradient_in, piece_ref, gradient_out, held, added, sems):
    del gradient_in
    slices, parts, rows, columns = piece_ref.shape
    planes = [(s, c) for s in range(slices) for c in range(parts)]

    def spot(s, c):
        return gradient_out.at[plane + s, c, pl.ds(0, rows), pl.ds(column, columns)]

    loads, pieces, stores = [], [], []
    for i, (s, c) in enumerate(planes):
        loads.append(pltpu.make_async_copy(spot(s, c), held.at[i], sems.at[0, i]))
        pieces.append(pltpu.make_async_copy(piece_ref.at[s, c], added.at[i], sems.at[1, i]))
        stores.append(pltpu.make_async_copy(held.at[i], spot(s, c), sems.at[2, i]))
        loads[i].start()
        pieces[i].start()
    for i in range(len(planes)):
        loads[i].wait()
        pieces[i].wait()
        held[i] = held[i] + added[i]
        stores[i].start()
    finish(stores)


def add_piece(gradient, piece, plane, column):
    slices, parts, rows, columns = piece.shape
    planes = slices * parts
    return pl.pallas_call(
        functools.partial(add_kernel, plane, column),
        out_shape=jax.ShapeDtypeStruct(gradient.shape, gradient.dtype),
        in_specs=[any_space] * 2,
        out_specs=any_space,
        scratch_shapes=[pltpu.VMEM((planes, rows, columns), jnp.float32)] * 2
        + [pltpu.SemaphoreType.DMA((3, planes))],
        input_output_aliases={0: 0},
        compiler_params=pltpu.CompilerParams(vmem_limit_bytes=8 * 1024 * 1024),
    )(gradient, piece)


def in_vmem(x):
    return pltpu.with_memory_space_constraint(x, pltpu.VMEM)


any_space = pl.BlockSpec(memory_space=pl.ANY)
hbm_space = pl.BlockSpec(memory_space=pltpu.HBM)
vmem_space = pl.BlockSpec(memory_space=pltpu.VMEM)
scalar_space = pl.BlockSpec(memory_space=pltpu.SMEM)


def slots_call(body, scalars, pieces, constants, state, state_types, out_shapes):
    first = len(scalars) + len(pieces) + len(constants)
    aliases = {first + i: len(out_shapes) + i for i in range(len(state))}
    return pl.pallas_call(
        body,
        out_shape=[jax.ShapeDtypeStruct(s, jnp.float32) for s in out_shapes] + state_types,
        in_specs=[scalar_space] * len(scalars)
        + [any_space if state else hbm_space] * len(pieces)
        + [vmem_space] * (len(constants) + len(state)),
        out_specs=[any_space] * len(out_shapes) + [vmem_space] * len(state_types),
        scratch_shapes=[pltpu.SemaphoreType.DMA],
        input_output_aliases=aliases,
        compiler_params=pltpu.CompilerParams(vmem_limit_bytes=20 * 1024 * 1024),
    )(*scalars, *pieces, *[in_vmem(x) for x in (*constants, *state)])


def tile_gradient(object_field, probe_field, propagator_phase, positions, counts, amplitudes):
    length = probe_field.shape[-1]
    tile = object_field.shape[-1]
    slices, parts = object_field.shape[:2]
    slots = positions.shape[-2]

    near0 = object_field[:1, :, :length, :length]
    near0, source = lax.optimization_barrier((near0, object_field))
    near0 = shifted(near0, "row", -1)
    right0 = source[:1, :, :, :length]
    far0 = source[:1, :, :length, length:]
    right0, far0, source = lax.optimization_barrier((right0, far0, source))
    right0 = shifted(right0, "col", -1)
    far0 = shifted(far0, "row", -1)
    near1 = shifted(source[1:, :, :length, :length], "row", -1)
    far1 = shifted(source[1:, :, :length, length:], "row", -1)
    right1 = shifted(source[1:, :, :, :length], "col", -1)
    corner0 = shifted(near0, "col", -1)
    corner1 = shifted(near1, "col", -1)

    propagator = jnp.stack([jnp.cos(propagator_phase), jnp.sin(propagator_phase)], 0)
    constants = (probe_field, propagator, amplitudes[0, 0], *dft_tables(length))
    scalars = (positions.reshape(-1), counts.reshape(-1))
    strips = (slices, parts, (tile + length) // lanes, tile + length, lanes)
    state_types = [
        pltpu.VMEM(strips, jnp.float32),
        pltpu.VMEM(strips, jnp.float32),
        pltpu.VMEM((slots, parts, length, length), jnp.float32),
        pltpu.VMEM((slots, parts * length, length), jnp.bfloat16),
    ]
    piece_shapes = (
        (1, parts, length, length),
        (1, parts, length, tile - length),
        (1, parts, length, length),
    )

    def call(kernel, pieces, state, out_shapes):
        return slots_call(kernel, scalars, pieces, constants, state, state_types, out_shapes)

    state = call(own_slots_kernel, (object_field,), (), ())
    state = call(spread_kernel, (near0, far0, corner0, right0), state, ())
    window, *others = state
    window = pl.pallas_call(
        load_kernel,
        name="load_halo",
        out_shape=state_types[0],
        in_specs=[any_space] * 3 + [vmem_space],
        out_specs=vmem_space,
        scratch_shapes=[pltpu.SemaphoreType.DMA],
        input_output_aliases={3: 0},
        compiler_params=pltpu.CompilerParams(vmem_limit_bytes=4 * 1024 * 1024),
    )(near1, corner1, right1, in_vmem(window))
    near1, far1, corner1, *state = call(back_kernel, (far1,), (window, *others), piece_shapes)
    corner1 = shifted(corner1, "col", 1)
    far1 = shifted(far1, "row", 1)
    near0, far0, corner0, window, gradient, *_ = call(first_kernel, (), state, piece_shapes)
    near1 = shifted(near1 + corner1, "row", 1)
    corner0 = shifted(corner0, "col", 1)
    far0 = shifted(far0, "row", 1)
    own, right = pl.pallas_call(
        own_kernel,
        name="own",
        out_shape=[
            jax.ShapeDtypeStruct(object_field.shape, jnp.float32),
            jax.ShapeDtypeStruct((slices, parts, tile, length), jnp.float32),
        ],
        in_specs=[vmem_space],
        out_specs=[any_space] * 2,
        scratch_shapes=[pltpu.SemaphoreType.DMA],
        compiler_params=pltpu.CompilerParams(vmem_limit_bytes=4 * 1024 * 1024),
    )(in_vmem(gradient))
    corner0, right = lax.optimization_barrier((corner0, right))
    near0 = shifted(near0 + corner0, "row", 1)
    right = shifted(right, "col", 1)
    result = add_piece(own, far1, 1, length)
    result = add_piece(result, near1, 1, 0)
    result = add_piece(result, right, 0, 0)
    result = add_piece(result, far0, 0, length)
    return add_piece(result, near0, 0, 0)


def solution(mesh):
    return jax.shard_map(
        tile_gradient,
        mesh=mesh,
        in_specs=(
            P(None, None, "row", "col"),
            P(),
            P(),
            P("row", "col", None, None),
            P("row", "col"),
            P("row", "col", None, None, None),
        ),
        out_specs=P(None, None, "row", "col"),
        check_vma=False,
    )
```

time: 131 us -> 153 us (1.17)
  Pallas kernels: 25.2 us -> 38.2 us
  waiting for transfers between devices: 71.4 us -> 77.7 us
  local copies, waits for them, and re-layouts: 11.5 us -> 13.9 us
    pallas_call x3 -> x4, Pallas kernels: 16.4 us -> 25 us  [slots_call(): pl.pallas_call(body, out_shape=[jax.ShapeDtypeStruct(s, jnp.float32) for...]
    ppermute x11 -> x15, waiting for transfers between devices: 71.4 us -> 77.7 us  [shifted(): return lax.ppermute(block, axis, route)]
    pallas_call x3 -> x6, Pallas kernels: 6.6 us -> 11.1 us  [the longest x5 9.79 us: add_piece(): pl.pallas_call(functools.partial(add_kernel, plane, column), out_shape=ja...]
    slice x3 -> x5, local copies, waits for them, and re-layouts: 7.3 us -> 8.83 us  [the longest x1 2.28 us: tile_gradient(): right0 = source[:1, :, :, :length]]
    unnamed x9 -> x13, local copies, waits for them, and re-layouts: 2.29 us -> 3.12 us
    ppermute x11 -> x15, starting transfers between devices: 19.3 us -> 19.5 us  [shifted(): return lax.ppermute(block, axis, route)]
  transfers between devices with their start and end apart: 11 -> 15, of which waited for: 7 -> 8; matrix products, arithmetic and copies ran while one was open for 5% -> 6% of each run, Pallas kernels for 16% -> 16%
where the time goes in v1:
time: 153 us
  waiting for transfers between devices  77.7 us (51%)
  Pallas kernels  38.2 us (25%)
  starting transfers between devices  19.5 us (13%)
  local copies, waits for them, and re-layouts  13.9 us (9%)
  other arithmetic  2.34 us (2%)
    ppermute x15, waiting for transfers between devices, shifted(): return lax.ppermute(block, axis, route)  77.7 us
    pallas_call x4, Pallas kernels, slots_call(): pl.pallas_call(body, out_shape=[jax.ShapeDtypeStruct(s, jnp.float32) for...  25 us
    ppermute x15, starting transfers between devices, shifted(): return lax.ppermute(block, axis, route)  19.5 us
    pallas_call x5, Pallas kernels, add_piece(): pl.pallas_call(functools.partial(add_kernel, plane, column), out_shape=ja...  9.79 us
    unnamed x13, local copies, waits for them, and re-layouts  3.12 us
  transfers between devices with their start and end apart: 15, of which 8 were waited for; matrix products, arithmetic and copies ran while one was open for 6% of the time, Pallas kernels for 16%

profile of v1, /device:TPU:0, one launch (start us, length us, event | category | flops | bytes accessed | tf_op | source)
XLA Modules:
  0.0 152.6 jit_solution(2873785299683159802)
XLA Ops:
  0.0 1.1 slice.18
  1.1 2.3 %slice.19 = f32[1,2,512,256]{3,2,1,0:T(8,128)} slice(f32[2,2,512,512]{3,2,1,0:T(8,128)} %object_ref.1), slice={[0:1], [0:2], [0:512], [0:256]} | slice | bytes 2097152 | tf_op jit(solution)/shard_map/slice | solution.py:375
  3.4 1.1 slice.20
  4.5 6.1 %collective-permute-start.5 = (f32[1,2,256,256]{3,2,1,0:T(8,128)S(1)}, f32[1,2,256,256]{3,2,1,0:T(8,128)S(1)}, u32[]{:S(2)}, u32[]{:S(2)}) collective-permute-start(f32[1,2,256,256]{3,2,1,0:T(8,128)S(1)} %slice.20), channel_id=1, source_target_pairs={{4,0},{8,4},{12,8},{16,12},{20,16},{24,20},{28,24},{0,28},{5,1},{9... | collective-permute-start | bytes 1572872 | tf_op jit(solution)/shard_map/ppermute | solution.py:19
  11.1 2.1 %fusion.9 = (f32[1,2,256,256]{3,2,1,0:T(8,128)S(1)}, f32[1,2,256,256]{3,2,1,0:T(8,128)}) fusion(f32[2,2,512,512]{3,2,1,0:T(8,128)} %object_ref.1), kind=kLoop, calls=%fused_computation.22 | loop fusion | bytes 2097152 | tf_op jit(solution)/shard_map/slice | solution.py:380
  13.2 1.4 collective-permute-start.1
  14.7 2.3 %slice.23 = f32[1,2,512,256]{3,2,1,0:T(8,128)} slice(f32[2,2,512,512]{3,2,1,0:T(8,128)} %object_ref.1), slice={[1:2], [0:2], [0:512], [0:256]} | slice | bytes 2097152 | tf_op jit(solution)/shard_map/slice | solution.py:382
  17.0 1.5 collective-permute-start.3
  18.5 1.1 negate_convert_fusion
  19.6 3.3 %collective-permute-done.5.far_ref = f32[1,2,256,256]{3,2,1,0:T(8,128)S(1)} collective-permute-done((f32[1,2,256,256]{3,2,1,0:T(8,128)S(1)}, f32[1,2,256,256]{3,2,1,0:T(8,128)S(1)}, u32[]{:S(2)}, u32[]{:S(2)}) %collective-permute-start.5) | collective-permute-done | bytes 524320 | tf_op jit(solution)/shard_map/ppermute | solution.py:19
  23.7 5.2 %collective-permute-start = (f32[1,2,256,256]{3,2,1,0:T(8,128)}, f32[1,2,256,256]{3,2,1,0:T(8,128)}, u32[]{:S(2)}, u32[]{:S(2)}) collective-permute-start(f32[1,2,256,256]{3,2,1,0:T(8,128)} %get-tuple-element.62), channel_id=1, source_target_pairs={{4,0},{8,4},{12,8},{16,12},{20,16},{24,20},{28,24},{0,28},{5,1},{9... | collective-permute-start | bytes 1572872 | tf_op jit(solution)/shard_map/ppermute | solution.py:19
  28.8 5.3 %collective-permute-done.4.near_ref = f32[1,2,256,256]{3,2,1,0:T(8,128)} collective-permute-done((f32[1,2,256,256]{3,2,1,0:T(8,128)S(1)}, f32[1,2,256,256]{3,2,1,0:T(8,128)}, u32[]{:S(2)}, u32[]{:S(2)}) %collective-permute-start.4) | collective-permute-done | bytes 524320 | tf_op jit(solution)/shard_map/ppermute | solution.py:19
  34.1 11.2 %collective-permute-done.1.near_ref = f32[1,2,256,256]{3,2,1,0:T(8,128)} collective-permute-done((f32[1,2,256,256]{3,2,1,0:T(8,128)S(1)}, f32[1,2,256,256]{3,2,1,0:T(8,128)}, u32[]{:S(2)}, u32[]{:S(2)}) %collective-permute-start.1) | collective-permute-done | bytes 524320 | tf_op jit(solution)/shard_map/ppermute | solution.py:19
  47.2 1.9 %cosine_bitcast_fusion = (f32[1,256,256]{2,1,0:T(8,128)S(1)}, f32[1,256,256]{2,1,0:T(8,128)S(1)}) fusion(f32[256,256]{1,0:T(8,128)} %param.8), kind=kLoop, calls=%fused_computation.19 | loop fusion | bytes 786432 | tf_op jit(solution)/shard_map/stack | solution.py:386
  49.2 2.2 %copy-done = f32[2,2,512,512]{3,2,1,0:T(8,128)S(1)} copy-done((f32[2,2,512,512]{3,2,1,0:T(8,128)S(1)}, f32[2,2,512,512]{3,2,1,0:T(8,128)}, u32[]{:S(2)}) %copy-start) | copy-done | bytes 4194328
  51.4 8.0 %shard_map.64 = (f32[2,2,6,768,128]{4,3,2,1,0:T(8,128)S(1)}, f32[2,2,6,768,128]{4,3,2,1,0:T(8,128)S(1)}, f32[4,2,256,256]{3,2,1,0:T(8,128)S(1)}, bf16[4,512,256]{2,1,0:T(8,128)(2,1)S(1)}) custom-call(s32[8]{0:T(128)S(1)} %reshape.6.places, s32[1]{0:T(128)} %bitcast.6.count, f32[2,2,512,512]{3,2,1,0:T(8,128)S(1)} %copy-done, f32[2,256,256]{2,1,0:T(8,128)S(1)} %copy-done.1, ...), custom_call_target="tpu_custom_call" | custom-call | tf_op jit(solution)/shard_map/pallas_call | solution.py:353
  59.4 5.0 %shard_map.65 = (f32[2,2,6,768,128]{4,3,2,1,0:T(8,128)S(1)}, f32[2,2,6,768,128]{4,3,2,1,0:T(8,128)S(1)}, f32[4,2,256,256]{3,2,1,0:T(8,128)S(1)}, bf16[4,512,256]{2,1,0:T(8,128)(2,1)S(1)}) custom-call(s32[8]{0:T(128)S(1)} %reshape.6.places, s32[1]{0:T(128)} %bitcast.7.count, ...), custom_call_target="tpu_custom_call", output_to_operand_aliasing={{0}: (11, {}), {1}: (12, {}), {2}: (13, {}), {3}: (14, {})} | custom-call | tf_op jit(solution)/shard_map/pallas_call | solution.py:353
  64.5 1.3 load_halo.1.rest_5_
  65.8 5.4 %shard_map.66 = (f32[1,2,256,256]{3,2,1,0:T(8,128)S(1)}, f32[1,2,256,256]{3,2,1,0:T(8,128)S(1)}, f32[1,2,256,256]{3,2,1,0:T(8,128)S(1)}, f32[2,2,6,768,128]{4,3,...) custom-call(s32[8]{0:T(128)S(1)} %reshape.6.places, ...), custom_call_target="tpu_custom_call", output_to_operand_aliasing={{3}: (8, {}), {4}: (9, {}), {5}: (10, {}), {6}: (11, {})} | custom-call | tf_op jit(solution)/shard_map/pallas_call | solution.py:353
  71.2 6.6 %shard_map.67 = (f32[1,2,256,256]{3,2,1,0:T(8,128)S(1)}, f32[1,2,256,256]{3,2,1,0:T(8,128)S(1)}, f32[1,2,256,256]{3,2,1,0:T(8,128)S(1)}, f32[2,2,6,768,128]{4,3,...) custom-call(s32[8]{0:T(128)S(1)} %reshape.6.places, ...), custom_call_target="tpu_custom_call", output_to_operand_aliasing={{3}: (7, {}), {4}: (8, {}), {5}: (9, {}), {6}: (10, {})} | custom-call | tf_op jit(solution)/shard_map/pallas_call | solution.py:353
  77.9 2.2 %own.1 = (f32[2,2,512,512]{3,2,1,0:T(8,128)}, f32[2,2,512,256]{3,2,1,0:T(8,128)S(1)}) custom-call(f32[2,2,6,768,128]{4,3,2,1,0:T(8,128)S(1)} %get-tuple-element.50.gradient), custom_call_target="tpu_custom_call" | custom-call | tf_op jit(solution)/shard_map/own/pallas_call | solution.py:425
  80.0 6.4 %collective-permute-done.11 = f32[1,2,256,256]{3,2,1,0:T(8,128)S(1)} collective-permute-done((f32[1,2,256,256]{3,2,1,0:T(8,128)S(1)}, f32[1,2,256,256]{3,2,1,0:T(8,128)S(1)}, u32[]{:S(2)}, u32[]{:S(2)}) %collective-permute-start.11) | collective-permute-done | bytes 524320 | tf_op jit(solution)/shard_map/ppermute | solution.py:19
  87.4 30.2 %collective-permute-done.9 = f32[1,2,256,256]{3,2,1,0:T(8,128)S(1)} collective-permute-done((f32[1,2,256,256]{3,2,1,0:T(8,128)S(1)}, f32[1,2,256,256]{3,2,1,0:T(8,128)S(1)}, u32[]{:S(2)}, u32[]{:S(2)}) %collective-permute-start.9) | collective-permute-done | bytes 524320 | tf_op jit(solution)/shard_map/ppermute | solution.py:19
  118.7 2.7 %collective-permute-start.14 = (f32[1,2,256,256]{3,2,1,0:T(8,128)S(1)}, f32[1,2,256,256]{3,2,1,0:T(8,128)S(1)}, u32[]{:S(2)}, u32[]{:S(2)}) collective-permute-start(f32[1,2,256,256]{3,2,1,0:T(8,128)S(1)} %add.28), channel_id=1, source_target_pairs={{28,0},{0,4},{4,8},{8,12},{12,16},{16,20},{20,24},{24,28},{29,1},{... | collective-permute-start | bytes 1572872 | tf_op jit(solution)/shard_map/ppermute | solution.py:19
  121.4 1.8 %shard_map.68.gradient_in = f32[2,2,512,512]{3,2,1,0:T(8,128)} custom-call(f32[2,2,512,512]{3,2,1,0:T(8,128)} %get-tuple-element.51.gradient_in, f32[1,2,256,256]{3,2,1,0:T(8,128)S(1)} %collective-permute-done.8.piece_ref), custom_call_target="tpu_custom_call", output_to_operand_aliasing={{}: (0, {})} | custom-call | tf_op jit(solution)/shard_map/pallas_call | solution.py:328
  123.2 12.8 %collective-permute-done.10.piece_ref = f32[1,2,256,256]{3,2,1,0:T(8,128)S(1)} collective-permute-done((f32[1,2,256,256]{3,2,1,0:T(8,128)S(1)}, f32[1,2,256,256]{3,2,1,0:T(8,128)S(1)}, u32[]{:S(2)}, u32[]{:S(2)}) %collective-permute-start.10) | collective-permute-done | bytes 524320 | tf_op jit(solution)/shard_map/ppermute | solution.py:19
  136.0 1.8 %shard_map.69.gradient_in = f32[2,2,512,512]{3,2,1,0:T(8,128)} custom-call(f32[2,2,512,512]{3,2,1,0:T(8,128)} %shard_map.68.gradient_in, f32[1,2,256,256]{3,2,1,0:T(8,128)S(1)} %collective-permute-done.10.piece_ref), custom_call_target="tpu_custom_call", output_to_operand_aliasing={{}: (0, {})} | custom-call | tf_op jit(solution)/shard_map/pallas_call | solution.py:328
  137.9 2.5 %shard_map.70.gradient_in = f32[2,2,512,512]{3,2,1,0:T(8,128)} custom-call(f32[2,2,512,512]{3,2,1,0:T(8,128)} %shard_map.69.gradient_in, f32[2,2,512,256]{3,2,1,0:T(8,128)S(1)} %collective-permute-done.12.piece_ref), custom_call_target="tpu_custom_call", output_to_operand_aliasing={{}: (0, {})} | custom-call | tf_op jit(solution)/shard_map/pallas_call | solution.py:328
  140.4 4.8 %collective-permute-done.13.piece_ref = f32[1,2,256,256]{3,2,1,0:T(8,128)S(1)} collective-permute-done((f32[1,2,256,256]{3,2,1,0:T(8,128)S(1)}, f32[1,2,256,256]{3,2,1,0:T(8,128)S(1)}, u32[]{:S(2)}, u32[]{:S(2)}) %collective-permute-start.13) | collective-permute-done | bytes 524320 | tf_op jit(solution)/shard_map/ppermute | solution.py:19
  145.2 1.8 %shard_map.71.gradient_in = f32[2,2,512,512]{3,2,1,0:T(8,128)} custom-call(f32[2,2,512,512]{3,2,1,0:T(8,128)} %shard_map.70.gradient_in, f32[1,2,256,256]{3,2,1,0:T(8,128)S(1)} %collective-permute-done.13.piece_ref), custom_call_target="tpu_custom_call", output_to_operand_aliasing={{}: (0, {})} | custom-call | tf_op jit(solution)/shard_map/pallas_call | solution.py:328
  147.0 3.8 %collective-permute-done.14.piece_ref = f32[1,2,256,256]{3,2,1,0:T(8,128)S(1)} collective-permute-done((f32[1,2,256,256]{3,2,1,0:T(8,128)S(1)}, f32[1,2,256,256]{3,2,1,0:T(8,128)S(1)}, u32[]{:S(2)}, u32[]{:S(2)}) %collective-permute-start.14) | collective-permute-done | bytes 524320 | tf_op jit(solution)/shard_map/ppermute | solution.py:19
  150.8 1.8 %shard_map.72 = f32[2,2,512,512]{3,2,1,0:T(8,128)} custom-call(f32[2,2,512,512]{3,2,1,0:T(8,128)} %shard_map.71.gradient_in, f32[1,2,256,256]{3,2,1,0:T(8,128)S(1)} %collective-permute-done.14.piece_ref), custom_call_target="tpu_custom_call", output_to_operand_aliasing={{}: (0, {})} | custom-call | tf_op jit(solution)/shard_map/pallas_call | solution.py:328
  (35 shorter events, 4.9 us)
Async XLA Ops:
  0.0 46.3 %copy-start.5 = (s32[1,1,4,2]{2,3,1,0:T(2,128)S(1)}, s32[1,1,4,2]{2,3,1,0:T(2,128)}, u32[]{:S(2)}) copy-start(s32[1,1,4,2]{2,3,1,0:T(2,128)} %param.9) | copy-start | bytes 100
  4.5 44.7 %copy-start.1 = (f32[2,256,256]{2,1,0:T(8,128)S(1)}, f32[2,256,256]{2,1,0:T(8,128)}, u32[]{:S(2)}) copy-start(f32[2,256,256]{2,1,0:T(8,128)} %rest_0_.7) | copy-start | bytes 1572868
  4.5 44.7 %copy-start.2 = (bf16[1,1,4,256,256]{4,3,2,1,0:T(8,128)(2,1)S(1)}, bf16[1,1,4,256,256]{4,3,2,1,0:T(8,128)(2,1)}, u32[]{:S(2)}) copy-start(bf16[1,1,4,256,256]{4,3,2,1,0:T(8,128)(2,1)} %param.11) | copy-start | bytes 1572868
  4.5 18.4 %collective-permute-start.5 = (f32[1,2,256,256]{3,2,1,0:T(8,128)S(1)}, f32[1,2,256,256]{3,2,1,0:T(8,128)S(1)}, u32[]{:S(2)}, u32[]{:S(2)}) collective-permute-start(f32[1,2,256,256]{3,2,1,0:T(8,128)S(1)} %slice.20), channel_id=1, source_target_pairs={{4,0},{8,4},{12,8},{16,12},{20,16},{24,20},{28,24},{0,28},{5,1},{9... | collective-permute-start | bytes 1572872 | tf_op jit(solution)/shard_map/ppermute | solution.py:19
  10.6 23.5 %collective-permute-start.4 = (f32[1,2,256,256]{3,2,1,0:T(8,128)S(1)}, f32[1,2,256,256]{3,2,1,0:T(8,128)}, u32[]{:S(2)}, u32[]{:S(2)}) collective-permute-start(f32[1,2,256,256]{3,2,1,0:T(8,128)S(1)} %slice.18), channel_id=1, source_target_pairs={{4,0},{8,4},{12,8},{16,12},{20,16},{24,20},{28,24},{0,28},{5,1},{9... | collective-permute-start | bytes 1572872 | tf_op jit(solution)/shard_map/ppermute | solution.py:19
  13.2 32.1 %collective-permute-start.1 = (f32[1,2,256,256]{3,2,1,0:T(8,128)S(1)}, f32[1,2,256,256]{3,2,1,0:T(8,128)}, u32[]{:S(2)}, u32[]{:S(2)}) collective-permute-start(f32[1,2,256,256]{3,2,1,0:T(8,128)S(1)} %get-tuple-element.61), channel_id=1, source_target_pairs={{4,0},{8,4},{12,8},{16,12},{20,16},{24,20},{28,24},{0,28},{5,1},{9... | collective-permute-start | bytes 1572872 | tf_op jit(solution)/shard_map/ppermute | solution.py:19
  14.6 44.8 %collective-permute-start.7 = (f32[1,2,512,256]{3,2,1,0:T(8,128)}, f32[1,2,512,256]{3,2,1,0:T(8,128)S(1)}, u32[]{:S(2)}, u32[]{:S(2)}) collective-permute-start(f32[1,2,512,256]{3,2,1,0:T(8,128)} %slice.19), channel_id=1, source_target_pairs={{1,0},{2,1},{3,2},{0,3},{5,4},{6,5},{7,6},{4,7},{9,8},{10,9},{11,1... | collective-permute-start | bytes 3145736 | tf_op jit(solution)/shard_map/ppermute | solution.py:19
  17.0 47.6 %collective-permute-start.3 = (f32[1,2,512,256]{3,2,1,0:T(8,128)}, f32[1,2,512,256]{3,2,1,0:T(8,128)S(1)}, u32[]{:S(2)}, u32[]{:S(2)}) collective-permute-start(f32[1,2,512,256]{3,2,1,0:T(8,128)} %slice.23), channel_id=1, source_target_pairs={{1,0},{2,1},{3,2},{0,3},{5,4},{6,5},{7,6},{4,7},{9,8},{10,9},{11,1... | collective-permute-start | bytes 3145736 | tf_op jit(solution)/shard_map/ppermute | solution.py:19
  22.9 0.8 copy-start.3
  23.7 42.2 %collective-permute-start = (f32[1,2,256,256]{3,2,1,0:T(8,128)}, f32[1,2,256,256]{3,2,1,0:T(8,128)}, u32[]{:S(2)}, u32[]{:S(2)}) collective-permute-start(f32[1,2,256,256]{3,2,1,0:T(8,128)} %get-tuple-element.62), channel_id=1, source_target_pairs={{4,0},{8,4},{12,8},{16,12},{20,16},{24,20},{28,24},{0,28},{5,1},{9... | collective-permute-start | bytes 1572872 | tf_op jit(solution)/shard_map/ppermute | solution.py:19
  34.1 25.3 %collective-permute-start.6 = (f32[1,2,256,256]{3,2,1,0:T(8,128)}, f32[1,2,256,256]{3,2,1,0:T(8,128)}, u32[]{:S(2)}, u32[]{:S(2)}) collective-permute-start(f32[1,2,256,256]{3,2,1,0:T(8,128)} %collective-permute-done.4.near_ref), channel_id=1, source_target_pairs={{1,0},{2,1},{3,2},{0,3},{5,4},{6,5},{7,6},{4,7},{9,8},{10,9},{11,1... | collective-permute-start | bytes 1572872 | tf_op jit(solution)/shard_map/ppermute | solution.py:19
  45.3 19.2 %collective-permute-start.2 = (f32[1,2,256,256]{3,2,1,0:T(8,128)}, f32[1,2,256,256]{3,2,1,0:T(8,128)}, u32[]{:S(2)}, u32[]{:S(2)}) collective-permute-start(f32[1,2,256,256]{3,2,1,0:T(8,128)} %collective-permute-done.1.near_ref), channel_id=1, source_target_pairs={{1,0},{2,1},{3,2},{0,3},{5,4},{6,5},{7,6},{4,7},{9,8},{10,9},{11,1... | collective-permute-start | bytes 1572872 | tf_op jit(solution)/shard_map/ppermute | solution.py:19
  49.1 10.3 %copy-start.4 = (f32[1,2,256,256]{3,2,1,0:T(8,128)S(1)}, f32[1,2,256,256]{3,2,1,0:T(8,128)}, u32[]{:S(2)}) copy-start(f32[1,2,256,256]{3,2,1,0:T(8,128)} %copy-done.3) | copy-start | bytes 1572868
  49.2 2.2 %copy-start = (f32[2,2,512,512]{3,2,1,0:T(8,128)S(1)}, f32[2,2,512,512]{3,2,1,0:T(8,128)}, u32[]{:S(2)}) copy-start(f32[2,2,512,512]{3,2,1,0:T(8,128)} %object_ref.1) | copy-start | bytes 12582916
  77.8 8.7 %collective-permute-start.11 = (f32[1,2,256,256]{3,2,1,0:T(8,128)S(1)}, f32[1,2,256,256]{3,2,1,0:T(8,128)S(1)}, u32[]{:S(2)}, u32[]{:S(2)}) collective-permute-start(f32[1,2,256,256]{3,2,1,0:T(8,128)S(1)} %get-tuple-element.55), channel_id=1, source_target_pairs={{3,0},{0,1},{1,2},{2,3},{7,4},{4,5},{5,6},{6,7},{11,8},{8,9},{9,10... | collective-permute-start | bytes 1572872 | tf_op jit(solution)/shard_map/ppermute | solution.py:19
  86.5 51.4 %collective-permute-start.12 = (f32[2,2,512,256]{3,2,1,0:T(8,128)S(1)}, f32[2,2,512,256]{3,2,1,0:T(8,128)S(1)}, u32[]{:S(2)}, u32[]{:S(2)}) collective-permute-start(f32[2,2,512,256]{3,2,1,0:T(8,128)S(1)} %get-tuple-element.57), channel_id=1, source_target_pairs={{3,0},{0,1},{1,2},{2,3},{7,4},{4,5},{5,6},{6,7},{11,8},{8,9},{9,10... | collective-permute-start | bytes 6291464 | tf_op jit(solution)/shard_map/ppermute | solution.py:19
  86.5 31.1 %collective-permute-start.9 = (f32[1,2,256,256]{3,2,1,0:T(8,128)S(1)}, f32[1,2,256,256]{3,2,1,0:T(8,128)S(1)}, u32[]{:S(2)}, u32[]{:S(2)}) collective-permute-start(f32[1,2,256,256]{3,2,1,0:T(8,128)S(1)} %get-tuple-element.54), channel_id=1, source_target_pairs={{3,0},{0,1},{1,2},{2,3},{7,4},{4,5},{5,6},{6,7},{11,8},{8,9},{9,10... | collective-permute-start | bytes 1572872 | tf_op jit(solution)/shard_map/ppermute | solution.py:19
  86.5 34.9 %collective-permute-start.8 = (f32[1,2,256,256]{3,2,1,0:T(8,128)S(1)}, f32[1,2,256,256]{3,2,1,0:T(8,128)S(1)}, u32[]{:S(2)}, u32[]{:S(2)}) collective-permute-start(f32[1,2,256,256]{3,2,1,0:T(8,128)S(1)} %get-tuple-element.52), channel_id=1, source_target_pairs={{28,0},{0,4},{4,8},{8,12},{12,16},{16,20},{20,24},{24,28},{29,1},{... | collective-permute-start | bytes 1572872 | tf_op jit(solution)/shard_map/ppermute | solution.py:19
  117.6 18.4 %collective-permute-start.10 = (f32[1,2,256,256]{3,2,1,0:T(8,128)S(1)}, f32[1,2,256,256]{3,2,1,0:T(8,128)S(1)}, u32[]{:S(2)}, u32[]{:S(2)}) collective-permute-start(f32[1,2,256,256]{3,2,1,0:T(8,128)S(1)} %add.27), channel_id=1, source_target_pairs={{28,0},{0,4},{4,8},{8,12},{12,16},{16,20},{20,24},{24,28},{29,1},{... | collective-permute-start | bytes 1572872 | tf_op jit(solution)/shard_map/ppermute | solution.py:19
  118.6 26.6 %collective-permute-start.13 = (f32[1,2,256,256]{3,2,1,0:T(8,128)S(1)}, f32[1,2,256,256]{3,2,1,0:T(8,128)S(1)}, u32[]{:S(2)}, u32[]{:S(2)}) collective-permute-start(f32[1,2,256,256]{3,2,1,0:T(8,128)S(1)} %get-tuple-element.58), channel_id=1, source_target_pairs={{28,0},{0,4},{4,8},{8,12},{12,16},{16,20},{20,24},{24,28},{29,1},{... | collective-permute-start | bytes 1572872 | tf_op jit(solution)/shard_map/ppermute | solution.py:19
  118.7 32.0 %collective-permute-start.14 = (f32[1,2,256,256]{3,2,1,0:T(8,128)S(1)}, f32[1,2,256,256]{3,2,1,0:T(8,128)S(1)}, u32[]{:S(2)}, u32[]{:S(2)}) collective-permute-start(f32[1,2,256,256]{3,2,1,0:T(8,128)S(1)} %add.28), channel_id=1, source_target_pairs={{28,0},{0,4},{4,8},{8,12},{12,16},{16,20},{20,24},{24,28},{29,1},{... | collective-permute-start | bytes 1572872 | tf_op jit(solution)/shard_map/ppermute | solution.py:19

commit v2 on v1

--- a/solution.py
+++ b/solution.py
@@ -3,6 +3,7 @@
 
 import jax
 import jax.numpy as jnp
+import numpy as np
 from jax import lax
 from jax.experimental import pallas as pl
 from jax.experimental.pallas import tpu as pltpu
@@ -20,31 +21,33 @@
 
 
 def dft_tables(length):
-    indices = jnp.arange(length, dtype=jnp.int32)
+    indices = np.arange(length, dtype=np.int32)
     turns = indices[:, None] * indices[None, :] % length
-    angles = turns.astype(jnp.float32) * (2.0 * math.pi / length)
-    cosine = jnp.cos(angles) / math.sqrt(length)
-    sine = jnp.sin(angles) / math.sqrt(length)
-    table_a = jnp.concatenate(
-        [jnp.concatenate([cosine, sine], 1), jnp.concatenate([-sine, cosine], 1)], 0
-    )
-    table_b = jnp.concatenate(
-        [jnp.concatenate([cosine, -sine], 1), jnp.concatenate([sine, cosine], 1)], 0
-    )
-    return (table_a.astype(jnp.bfloat16), table_b.astype(jnp.bfloat16))
+    angles = turns.astype(np.float32) * np.float32(2.0 * math.pi / length)
+    cosine = np.cos(angles) / np.float32(math.sqrt(length))
+    sine = np.sin(angles) / np.float32(math.sqrt(length))
+    table_a = np.block([[cosine, sine], [-sine, cosine]])
+    table_b = np.block([[cosine, -sine], [sine, cosine]])
+    return (jnp.asarray(table_a, jnp.bfloat16), jnp.asarray(table_b, jnp.bfloat16))
 
 
 def sections(stacked, left_table, right_table):
-    length = stacked.shape[1]
-    middle = jnp.dot(left_table, stacked, preferred_element_type=jnp.float32)
-    middle = middle.astype(jnp.bfloat16)
-    middle = jnp.concatenate([middle[:length], middle[length:]], 1)
-    result = jnp.dot(middle, right_table, preferred_element_type=jnp.float32)
-    return result[:, :length], result[:, length:]
-
-
-def transform(wave, left_table, right_table):
-    stacked = jnp.concatenate([part.astype(jnp.bfloat16) for part in wave], 0)
+    length = stacked[0].shape[1]
+    middle = [
+        jnp.dot(left_table, wave, preferred_element_type=jnp.float32).astype(jnp.bfloat16)
+        for wave in stacked
+    ]
+    middle = [jnp.concatenate([wave[:length], wave[length:]], 1) for wave in middle]
+    result = [
+        jnp.dot(wave, right_table, preferred_element_type=jnp.float32) for wave in middle
+    ]
+    return [(wave[:, :length], wave[:, length:]) for wave in result]
+
+
+def transforms(waves, left_table, right_table):
+    stacked = [
+        jnp.concatenate([part.astype(jnp.bfloat16) for part in wave], 0) for wave in waves
+    ]
     return sections(stacked, left_table, right_table)
 
 
@@ -122,61 +125,87 @@
             gradient[at] = gradient[at] + part
 
 
-def spread_slot(places, window, constants, spreads, slot):
+def spread_slots(places, window, constants, spreads, slots):
     probe, propagator, _, table_a, table_b = constants
     length = probe.shape[-1]
-    lit = product_of((probe[0], probe[1]), fetch(window, 0, patch_spot(places, slot), length))
-    wave = transform(lit, table_a[...], table_b[...])
-    wave = product_of((propagator[0], propagator[1]), wave)
-    wave = transform(wave, table_b[...], table_a[...])
-    spreads[slot, 0] = wave[0]
-    spreads[slot, 1] = wave[1]
-
-
-def back_slot(places, window, gradient, constants, spreads, inners, slot):
+    waves = [
+        product_of((probe[0], probe[1]), fetch(window, 0, patch_spot(places, slot), length))
+        for slot in slots
+    ]
+    waves = transforms(waves, table_a[...], table_b[...])
+    waves = [product_of((propagator[0], propagator[1]), wave) for wave in waves]
+    waves = transforms(waves, table_b[...], table_a[...])
+    for wave, slot in zip(waves, slots):
+        spreads[slot, 0] = wave[0]
+        spreads[slot, 1] = wave[1]
+
+
+def back_slots(places, window, gradient, constants, spreads, inners, slots):
     probe, _, measured_ref, table_a, table_b = constants
     length = probe.shape[-1]
-    spot = patch_spot(places, slot)
-    second = fetch(window, 1, spot, length)
-    spread = (spreads[slot, 0], spreads[slot, 1])
-    far = transform(product_of(spread, second), table_a[...], table_b[...])
-    power = far[0] * far[0] + far[1] * far[1]
-    measured = measured_ref[slot].astype(jnp.float32)
-    ratio = 1.0 - measured * jnp.minimum(lax.rsqrt(power), 1.0 / floor_value)
-    back = transform((far[0] * ratio, far[1] * ratio), table_b[...], table_a[...])
-    inner = conj_product(back, second)
-    inners[slot, pl.ds(0, length), :] = inner[0].astype(jnp.bfloat16)
-    inners[slot, pl.ds(length, length), :] = inner[1].astype(jnp.bfloat16)
-    spread = (spreads[slot, 0], spreads[slot, 1])
-    accumulate(gradient, 1, spot, conj_product(back, spread), length)
-
-
-def first_slot(places, gradient, constants, inners, slot):
+    spots = [patch_spot(places, slot) for slot in slots]
+    waves = [
+        product_of((spreads[slot, 0], spreads[slot, 1]), fetch(window, 1, spot, length))
+        for slot, spot in zip(slots, spots)
+    ]
+    residuals = []
+    for far, slot in zip(transforms(waves, table_a[...], table_b[...]), slots):
+        power = far[0] * far[0] + far[1] * far[1]
+        measured = measured_ref[slot].astype(jnp.float32)
+        ratio = 1.0 - measured * jnp.minimum(lax.rsqrt(power), 1.0 / floor_value)
+        residuals.append((far[0] * ratio, far[1] * ratio))
+    backs = transforms(residuals, table_b[...], table_a[...])
+    for back, slot, spot in zip(backs, slots, spots):
+        inner = conj_product(back, fetch(window, 1, spot, length))
+        inners[slot, pl.ds(0, length), :] = inner[0].astype(jnp.bfloat16)
+        inners[slot, pl.ds(length, length), :] = inner[1].astype(jnp.bfloat16)
+        spread = (spreads[slot, 0], spreads[slot, 1])
+        accumulate(gradient, 1, spot, conj_product(back, spread), length)
+
+
+def first_slots(places, gradient, constants, inners, slots):
     probe, propagator, _, table_a, table_b = constants
     length = probe.shape[-1]
-    wave = sections(inners[slot], table_a[...], table_b[...])
-    wave = conj_product(wave, (propagator[0], propagator[1]))
-    wave = transform(wave, table_b[...], table_a[...])
-    grad = conj_product(wave, (probe[0], probe[1]))
-    accumulate(gradient, 0, patch_spot(places, slot), grad, length)
-
-
-def each_slot(places, count, tile, length, inside, visit):
-    def step(slot, carry):
-        within = jnp.logical_and(
-            places[2 * slot] <= tile - length, places[2 * slot + 1] <= tile - length
-        )
-        if inside is None:
-            visit(slot)
-        else:
-
-            @pl.when(within if inside else jnp.logical_not(within))
+    waves = sections([inners[slot] for slot in slots], table_a[...], table_b[...])
+    waves = [conj_product(wave, (propagator[0], propagator[1])) for wave in waves]
+    waves = transforms(waves, table_b[...], table_a[...])
+    for wave, slot in zip(waves, slots):
+        grad = conj_product(wave, (probe[0], probe[1]))
+        accumulate(gradient, 0, patch_spot(places, slot), grad, length)
+
+
+def visit_slots(places, count, slots, limit, inside, todo, exact, visit):
+    def pick(slot, found):
+        within = jnp.logical_and(places[2 * slot] <= limit, places[2 * slot + 1] <= limit)
+        chosen = slot < count[0]
+        if inside is not None:
+            chosen = jnp.logical_and(chosen, within == inside)
+
+        @pl.when(chosen)
+        def _():
+            todo[found] = slot
+
+        return found + chosen.astype(jnp.int32)
+
+    found = lax.fori_loop(0, slots, pick, jnp.int32(0))
+    if exact:
+        for size in range(1, slots + 1):
+
+            @pl.when(found == size)
             def _():
-                visit(slot)
-
+                visit([todo[i] for i in range(size)])
+
+        return
+
+    def pair(index, carry):
+        visit([todo[2 * index], todo[2 * index + 1]])
         return carry
 
-    lax.fori_loop(0, count[0], step, 0)
+    lax.fori_loop(0, found // 2, pair, 0)
+
+    @pl.when(lax.rem(found, 2) == 1)
+    def _():
+        visit([todo[found - 1]])
 
 
 def sizes(tile, length):
@@ -187,8 +216,52 @@
     return own, near, far, past
 
 
+def from_strips(out, strips, row0, store, plane):
+    for c in range(out.shape[1]):
+        for k, strip in enumerate(strips):
+            out[0, c, :, pl.ds(k * lanes, lanes)] = store[
+                plane, c, strip, pl.ds(row0, out.shape[2]), :
+            ]
+
+
+def into_strips(piece, strips, row0, store, plane):
+    for c in range(piece.shape[1]):
+        for k, strip in enumerate(strips):
+            store[plane, c, strip, pl.ds(row0, piece.shape[2]), :] = piece[
+                0, c, :, pl.ds(k * lanes, lanes)
+            ]
+
+
+def pack_kernel(corners, object_ref, *rest):
+    outs, sem = rest[:-1], rest[-1]
+    copies = []
+    for (s, row, column), out in zip(corners, outs):
+        for c in range(out.shape[1]):
+            piece = object_ref.at[
+                s, c, pl.ds(row, out.shape[2]), pl.ds(column, out.shape[3])
+            ]
+            copies.append(pltpu.make_async_copy(piece, out.at[0, c], sem))
+    for copy in copies:
+        copy.start()
+    finish(copies)
+
+
+def pack(object_field, pieces):
+    return pl.pallas_call(
+        functools.partial(pack_kernel, [piece[:3] for piece in pieces]),
+        out_shape=[
+            jax.ShapeDtypeStruct((1, object_field.shape[1], *piece[3:]), jnp.float32)
+            for piece in pieces
+        ],
+        in_specs=[hbm_space],
+        out_specs=[any_space] * len(pieces),
+        scratch_shapes=[pltpu.SemaphoreType.DMA],
+        compiler_params=pltpu.CompilerParams(vmem_limit_bytes=1024 * 1024),
+    )(in_hbm(object_field))
+
+
 def own_slots_kernel(places, count, object_ref, *rest):
-    constants, (window, gradient, spreads, inners, sem) = rest[:5], rest[5:]
+    constants, (window, gradient, spreads, inners, todo, sem) = rest[:5], rest[5:]
     length = constants[0].shape[-1]
     tile = object_ref.shape[-1]
     own, _, _, _ = sizes(tile, length)
@@ -196,15 +269,17 @@
     gradient[...] = jnp.zeros_like(gradient)
     finish(loads)
 
-    def visit(slot):
-        spread_slot(places, window, constants, spreads, slot)
-        back_slot(places, window, gradient, constants, spreads, inners, slot)
-
-    each_slot(places, count, tile, length, True, visit)
+    def visit(slots):
+        spread_slots(places, window, constants, spreads, slots)
+        back_slots(places, window, gradient, constants, spreads, inners, slots)
+
+    visit_slots(
+        places, count, inners.shape[0], tile - length, True, todo, False, visit
+    )
 
 
 def spread_kernel(places, count, near_ref, far_ref, corner_ref, right_ref, *rest):
-    constants, (window, gradient, spreads, inners, sem) = rest[:5], rest[9:]
+    constants, (window, gradient, spreads, inners, todo, sem) = rest[:5], rest[9:]
     length = constants[0].shape[-1]
     tile = right_ref.shape[2]
     _, near, far, past = sizes(tile, length)
@@ -219,10 +294,12 @@
         )
     )
 
-    def visit(slot):
-        spread_slot(places, window, constants, spreads, slot)
-
-    each_slot(places, count, tile, length, False, visit)
+    def visit(slots):
+        spread_slots(places, window, constants, spreads, slots)
+
+    visit_slots(
+        places, count, inners.shape[0], tile - length, False, todo, False, visit
+    )
 
 
 def load_kernel(near_ref, corner_ref, right_ref, window_in, window, sem):
@@ -243,47 +320,39 @@
 
 def back_kernel(places, count, far_ref, *rest):
     constants = rest[:5]
-    near_out, far_out, corner_out, window, gradient, spreads, inners, sem = rest[9:]
+    near_out, far_out, corner_out, window, gradient, spreads, inners, todo, _ = rest[9:]
     length = constants[0].shape[-1]
     tile = length + far_ref.shape[3]
     _, near, far, past = sizes(tile, length)
-    finish(run_copies([strip_copies(far_ref, far, tile, window, 1, sem, False)]))
-
-    def visit(slot):
-        back_slot(places, window, gradient, constants, spreads, inners, slot)
-
-    each_slot(places, count, tile, length, False, visit)
-    finish(
-        run_copies(
-            [
-                strip_copies(corner_out, past, tile, gradient, 1, sem, True),
-                strip_copies(far_out, far, tile, gradient, 1, sem, True),
-                strip_copies(near_out, near, tile, gradient, 1, sem, True),
-            ]
-        )
-    )
+    into_strips(far_ref, far, tile, window, 1)
+
+    def visit(slots):
+        back_slots(places, window, gradient, constants, spreads, inners, slots)
+
+    visit_slots(
+        places, count, inners.shape[0], tile - length, False, todo, True, visit
+    )
+    from_strips(corner_out, past, tile, gradient, 1)
+    from_strips(far_out, far, tile, gradient, 1)
+    from_strips(near_out, near, tile, gradient, 1)
 
 
 def first_kernel(places, count, *rest):
     constants = rest[:5]
-    near_out, far_out, corner_out, _, gradient, _, inners, sem = rest[9:]
+    near_out, far_out, corner_out, _, gradient, _, inners, todo, _ = rest[9:]
     length = constants[0].shape[-1]
     tile = length + far_out.shape[3]
     _, near, far, past = sizes(tile, length)
 
-    def visit(slot):
-        first_slot(places, gradient, constants, inners, slot)
-
-    each_slot(places, count, tile, length, None, visit)
-    finish(
-        run_copies(
-            [
-                strip_copies(corner_out, past, tile, gradient, 0, sem, True),
-                strip_copies(far_out, far, tile, gradient, 0, sem, True),
-                strip_copies(near_out, near, tile, gradient, 0, sem, True),
-            ]
-        )
-    )
+    def visit(slots):
+        first_slots(places, gradient, constants, inners, slots)
+
+    visit_slots(
+        places, count, inners.shape[0], tile - length, None, todo, False, visit
+    )
+    from_strips(corner_out, past, tile, gradient, 0)
+    from_strips(far_out, far, tile, gradient, 0)
+    from_strips(near_out, near, tile, gradient, 0)
 
 
 def own_kernel(gradient, own_out, right_out, sem):
@@ -337,6 +406,10 @@
     )(gradient, piece)
 
 
+def in_hbm(x):
+    return pltpu.with_memory_space_constraint(x, pltpu.HBM)
+
+
 def in_vmem(x):
     return pltpu.with_memory_space_constraint(x, pltpu.VMEM)
 
@@ -350,14 +423,21 @@
 def slots_call(body, scalars, pieces, constants, state, state_types, out_shapes):
     first = len(scalars) + len(pieces) + len(constants)
     aliases = {first + i: len(out_shapes) + i for i in range(len(state))}
+    close = bool(out_shapes)
+    if close:
+        pieces = [in_vmem(piece) for piece in pieces]
+    piece_space = vmem_space if close else any_space if state else hbm_space
     return pl.pallas_call(
         body,
-        out_shape=[jax.ShapeDtypeStruct(s, jnp.float32) for s in out_shapes] + state_types,
+        out_shape=[pltpu.VMEM(s, jnp.float32) for s in out_shapes] + state_types,
         in_specs=[scalar_space] * len(scalars)
-        + [any_space if state else hbm_space] * len(pieces)
+        + [piece_space] * len(pieces)
         + [vmem_space] * (len(constants) + len(state)),
-        out_specs=[any_space] * len(out_shapes) + [vmem_space] * len(state_types),
-        scratch_shapes=[pltpu.SemaphoreType.DMA],
+        out_specs=[vmem_space] * (len(out_shapes) + len(state_types)),
+        scratch_shapes=[
+            pltpu.SMEM((constants[2].shape[0],), jnp.int32),
+            pltpu.SemaphoreType.DMA,
+        ],
         input_output_aliases=aliases,
         compiler_params=pltpu.CompilerParams(vmem_limit_bytes=20 * 1024 * 1024),
     )(*scalars, *pieces, *[in_vmem(x) for x in (*constants, *state)])
@@ -369,17 +449,24 @@
     slices, parts = object_field.shape[:2]
     slots = positions.shape[-2]
 
-    near0 = object_field[:1, :, :length, :length]
-    near0, source = lax.optimization_barrier((near0, object_field))
+    rest = tile - length
+    (near0,) = pack(object_field, [(0, 0, 0, length, length)])
+    right0, far0, near1, far1, right1 = pack(
+        object_field,
+        [
+            (0, 0, 0, tile, length),
+            (0, 0, length, length, rest),
+            (1, 0, 0, length, length),
+            (1, 0, length, length, rest),
+            (1, 0, 0, tile, length),
+        ],
+    )
     near0 = shifted(near0, "row", -1)
-    right0 = source[:1, :, :, :length]
-    far0 = source[:1, :, :length, length:]
-    right0, far0, source = lax.optimization_barrier((right0, far0, source))
     right0 = shifted(right0, "col", -1)
     far0 = shifted(far0, "row", -1)
-    near1 = shifted(source[1:, :, :length, :length], "row", -1)
-    far1 = shifted(source[1:, :, :length, length:], "row", -1)
-    right1 = shifted(source[1:, :, :, :length], "col", -1)
+    near1 = shifted(near1, "row", -1)
+    far1 = shifted(far1, "row", -1)
+    right1 = shifted(right1, "col", -1)
     corner0 = shifted(near0, "col", -1)
     corner1 = shifted(near1, "col", -1)
 
@@ -402,7 +489,7 @@
     def call(kernel, pieces, state, out_shapes):
         return slots_call(kernel, scalars, pieces, constants, state, state_types, out_shapes)
 
-    state = call(own_slots_kernel, (object_field,), (), ())
+    state = call(own_slots_kernel, (in_hbm(object_field),), (), ())
     state = call(spread_kernel, (near0, far0, corner0, right0), state, ())
     window, *others = state
     window = pl.pallas_call(

time: 153 us -> 226 us (1.48)
  Pallas kernels: 38.2 us -> 114 us
  waiting for transfers between devices: 77.7 us -> 93.8 us
  local copies, waits for them, and re-layouts: 13.9 us -> 1.98 us
  starting transfers between devices: 19.5 us -> 14.5 us
    pallas_call x4 -> x6, Pallas kernels: 25 us -> 101 us  [the longest x2 81.6 us: pack(): pl.pallas_call(functools.partial(pack_kernel, [piece[:3] for piece in pie...]
    ppermute x15, waiting for transfers between devices: 77.7 us -> 93.8 us  [shifted(): return lax.ppermute(block, axis, route)]
    slice x5 -> x0, local copies, waits for them, and re-layouts: 8.83 us -> none  [the longest x1 2.28 us: tile_gradient(): right0 = source[:1, :, :, :length]]
    ppermute x15, starting transfers between devices: 19.5 us -> 14.5 us  [shifted(): return lax.ppermute(block, axis, route)]
  transfers between devices with their start and end apart: 15 -> 15, of which waited for: 8 -> 8; matrix products, arithmetic and copies ran while one was open for 6% -> 1% of each run, Pallas kernels for 16% -> 11%
where the time goes in v2:
time: 226 us
  Pallas kernels  114 us (50%)
  waiting for transfers between devices  93.8 us (42%)
  starting transfers between devices  14.5 us (6%)
    ppermute x15, waiting for transfers between devices, shifted(): return lax.ppermute(block, axis, route)  93.8 us
    pallas_call x2, Pallas kernels, pack(): pl.pallas_call(functools.partial(pack_kernel, [piece[:3] for piece in pie...  81.6 us
    pallas_call x4, Pallas kernels, slots_call(): pl.pallas_call(body, out_shape=[pltpu.VMEM(s, jnp.float32) for s in out_s...  19.2 us
    ppermute x15, starting transfers between devices, shifted(): return lax.ppermute(block, axis, route)  14.5 us
    pallas_call x5, Pallas kernels, add_piece(): pl.pallas_call(functools.partial(add_kernel, plane, column), out_shape=ja...  9.8 us
  transfers between devices with their start and end apart: 15, of which 8 were waited for; matrix products, arithmetic and copies ran while one was open for 1% of the time, Pallas kernels for 11%

profile of v2, /device:TPU:0, one launch (start us, length us, event | category | flops | bytes accessed | tf_op | source)
XLA Modules:
  0.0 225.6 jit_solution(5866975836481257536)
XLA Ops:
  0.0 80.5 %shard_map.82 = (f32[1,2,512,256]{3,2,1,0:T(8,128)}, f32[1,2,256,256]{3,2,1,0:T(8,128)S(1)}, f32[1,2,256,256]{3,2,1,0:T(8,128)S(1)}, f32[1,2,256,256]{3,2,1,0:T(8,128)}, f32[1,2,512,256]{3,2,1,0:T(8,128)}) custom-call(f32[2,2,512,512]{3,2,1,0:T(8,128)} %object_ref.5), custom_call_target="tpu_custom_call" | custom-call | tf_op jit(solution)/shard_map/pallas_call | solution.py:250
  80.6 2.5 %collective-permute-start.7 = (f32[1,2,512,256]{3,2,1,0:T(8,128)}, f32[1,2,512,256]{3,2,1,0:T(8,128)}, u32[]{:S(2)}, u32[]{:S(2)}) collective-permute-start(f32[1,2,512,256]{3,2,1,0:T(8,128)} %get-tuple-element.37), channel_id=1, source_target_pairs={{1,0},{2,1},{3,2},{0,3},{5,4},{6,5},{7,6},{4,7},{9,8},{10,9},{11,1... | collective-permute-start | bytes 3145736 | tf_op jit(solution)/shard_map/ppermute | solution.py:20
  83.1 1.0 shard_map.83
  84.1 4.6 %collective-permute-start.4 = (f32[1,2,256,256]{3,2,1,0:T(8,128)S(1)}, f32[1,2,256,256]{3,2,1,0:T(8,128)}, u32[]{:S(2)}, u32[]{:S(2)}) collective-permute-start(f32[1,2,256,256]{3,2,1,0:T(8,128)S(1)} %shard_map.83), channel_id=1, source_target_pairs={{4,0},{8,4},{12,8},{16,12},{20,16},{24,20},{28,24},{0,28},{5,1},{9... | collective-permute-start | bytes 1572872 | tf_op jit(solution)/shard_map/ppermute | solution.py:20
  88.7 0.5 collective-permute-start.1
  89.2 0.1 collective-permute-start.3
  89.3 1.4 collective-permute-start.5
  90.7 10.3 %collective-permute-done.4.near_ref = f32[1,2,256,256]{3,2,1,0:T(8,128)} collective-permute-done((f32[1,2,256,256]{3,2,1,0:T(8,128)S(1)}, f32[1,2,256,256]{3,2,1,0:T(8,128)}, u32[]{:S(2)}, u32[]{:S(2)}) %collective-permute-start.4) | collective-permute-done | bytes 524320 | tf_op jit(solution)/shard_map/ppermute | solution.py:20
  101.0 11.2 %collective-permute-done.1.near_ref = f32[1,2,256,256]{3,2,1,0:T(8,128)} collective-permute-done((f32[1,2,256,256]{3,2,1,0:T(8,128)S(1)}, f32[1,2,256,256]{3,2,1,0:T(8,128)}, u32[]{:S(2)}, u32[]{:S(2)}) %collective-permute-start.1) | collective-permute-done | bytes 524320 | tf_op jit(solution)/shard_map/ppermute | solution.py:20
  112.2 9.8 %collective-permute-done.5.far_ref = f32[1,2,256,256]{3,2,1,0:T(8,128)S(1)} collective-permute-done((f32[1,2,256,256]{3,2,1,0:T(8,128)S(1)}, f32[1,2,256,256]{3,2,1,0:T(8,128)S(1)}, u32[]{:S(2)}, u32[]{:S(2)}) %collective-permute-start.5) | collective-permute-done | bytes 524320 | tf_op jit(solution)/shard_map/ppermute | solution.py:20
  122.1 0.8 copy-done.4
  122.9 5.2 %collective-permute-start = (f32[1,2,256,256]{3,2,1,0:T(8,128)}, f32[1,2,256,256]{3,2,1,0:T(8,128)}, u32[]{:S(2)}, u32[]{:S(2)}) collective-permute-start(f32[1,2,256,256]{3,2,1,0:T(8,128)} %get-tuple-element.33), channel_id=1, source_target_pairs={{4,0},{8,4},{12,8},{16,12},{20,16},{24,20},{28,24},{0,28},{5,1},{9... | collective-permute-start | bytes 1572872 | tf_op jit(solution)/shard_map/ppermute | solution.py:20
  128.0 0.1 copy.28
  128.1 0.1 reshape.6.places
  128.9 1.0 cosine_bitcast_fusion
  130.0 7.3 %shard_map.84 = (f32[2,2,6,768,128]{4,3,2,1,0:T(8,128)S(1)}, f32[2,2,6,768,128]{4,3,2,1,0:T(8,128)S(1)}, f32[4,2,256,256]{3,2,1,0:T(8,128)S(1)}, bf16[4,512,256]{2,1,0:T(8,128)(2,1)S(1)}) custom-call(s32[8]{0:T(128)S(1)} %reshape.6.places, s32[1]{0:T(128)} %bitcast.6.count, f32[2,2,512,512]{3,2,1,0:T(8,128)} %object_ref.5, f32[2,256,256]{2,1,0:T(8,128)S(1)} %copy-done, ...), custom_call_target="tpu_custom_call" | custom-call | tf_op jit(solution)/shard_map/pallas_call | solution.py:430
  137.3 4.0 %shard_map.85 = (f32[2,2,6,768,128]{4,3,2,1,0:T(8,128)S(1)}, f32[2,2,6,768,128]{4,3,2,1,0:T(8,128)S(1)}, f32[4,2,256,256]{3,2,1,0:T(8,128)S(1)}, bf16[4,512,256]{2,1,0:T(8,128)(2,1)S(1)}) custom-call(s32[8]{0:T(128)S(1)} %reshape.6.places, s32[1]{0:T(128)} %bitcast.7.count, ...), custom_call_target="tpu_custom_call", output_to_operand_aliasing={{0}: (11, {}), {1}: (12, {}), {2}: (13, {}), {3}: (14, {})} | custom-call | tf_op jit(solution)/shard_map/pallas_call | solution.py:430
  141.4 1.3 load_halo.1.rest_5_
  142.7 3.9 %shard_map.86 = (f32[1,2,256,256]{3,2,1,0:T(8,128)S(1)}, f32[1,2,256,256]{3,2,1,0:T(8,128)S(1)}, f32[1,2,256,256]{3,2,1,0:T(8,128)S(1)}, f32[2,2,6,768,128]{4,3,...) custom-call(s32[8]{0:T(128)S(1)} %reshape.6.places, ...), custom_call_target="tpu_custom_call", output_to_operand_aliasing={{3}: (8, {}), {4}: (9, {}), {5}: (10, {}), {6}: (11, {})} | custom-call | tf_op jit(solution)/shard_map/pallas_call | solution.py:430
  146.6 3.9 %shard_map.87 = (f32[1,2,256,256]{3,2,1,0:T(8,128)S(1)}, f32[1,2,256,256]{3,2,1,0:T(8,128)S(1)}, f32[1,2,256,256]{3,2,1,0:T(8,128)S(1)}, f32[2,2,6,768,128]{4,3,...) custom-call(s32[8]{0:T(128)S(1)} %reshape.6.places, ...), custom_call_target="tpu_custom_call", output_to_operand_aliasing={{3}: (7, {}), {4}: (8, {}), {5}: (9, {}), {6}: (10, {})} | custom-call | tf_op jit(solution)/shard_map/pallas_call | solution.py:430
  150.6 2.2 own.1
  152.7 6.4 %collective-permute-done.11 = f32[1,2,256,256]{3,2,1,0:T(8,128)S(1)} collective-permute-done((f32[1,2,256,256]{3,2,1,0:T(8,128)S(1)}, f32[1,2,256,256]{3,2,1,0:T(8,128)S(1)}, u32[]{:S(2)}, u32[]{:S(2)}) %collective-permute-start.11) | collective-permute-done | bytes 524320 | tf_op jit(solution)/shard_map/ppermute | solution.py:20
  159.2 31.1 %collective-permute-done.9 = f32[1,2,256,256]{3,2,1,0:T(8,128)S(1)} collective-permute-done((f32[1,2,256,256]{3,2,1,0:T(8,128)S(1)}, f32[1,2,256,256]{3,2,1,0:T(8,128)S(1)}, u32[]{:S(2)}, u32[]{:S(2)}) %collective-permute-start.9) | collective-permute-done | bytes 524320 | tf_op jit(solution)/shard_map/ppermute | solution.py:20
  190.5 0.1 add.7
  190.6 1.8 shard_map.88.gradient_in
  192.4 15.4 %collective-permute-done.10.piece_ref = f32[1,2,256,256]{3,2,1,0:T(8,128)S(1)} collective-permute-done((f32[1,2,256,256]{3,2,1,0:T(8,128)S(1)}, f32[1,2,256,256]{3,2,1,0:T(8,128)S(1)}, u32[]{:S(2)}, u32[]{:S(2)}) %collective-permute-start.10) | collective-permute-done | bytes 524320 | tf_op jit(solution)/shard_map/ppermute | solution.py:20
  207.9 1.8 shard_map.89.gradient_in
  209.7 2.5 %shard_map.90.gradient_in = f32[2,2,512,512]{3,2,1,0:T(8,128)} custom-call(f32[2,2,512,512]{3,2,1,0:T(8,128)} %shard_map.89.gradient_in, f32[2,2,512,256]{3,2,1,0:T(8,128)S(1)} %collective-permute-done.12.piece_ref), custom_call_target="tpu_custom_call", output_to_operand_aliasing={{}: (0, {})} | custom-call | tf_op jit(solution)/shard_map/pallas_call | solution.py:397
  212.2 5.8 %collective-permute-done.13.piece_ref = f32[1,2,256,256]{3,2,1,0:T(8,128)S(1)} collective-permute-done((f32[1,2,256,256]{3,2,1,0:T(8,128)S(1)}, f32[1,2,256,256]{3,2,1,0:T(8,128)S(1)}, u32[]{:S(2)}, u32[]{:S(2)}) %collective-permute-start.13) | collective-permute-done | bytes 524320 | tf_op jit(solution)/shard_map/ppermute | solution.py:20
  218.0 1.8 shard_map.91.gradient_in
  219.8 3.8 %collective-permute-done.14.piece_ref = f32[1,2,256,256]{3,2,1,0:T(8,128)S(1)} collective-permute-done((f32[1,2,256,256]{3,2,1,0:T(8,128)S(1)}, f32[1,2,256,256]{3,2,1,0:T(8,128)S(1)}, u32[]{:S(2)}, u32[]{:S(2)}) %collective-permute-start.14) | collective-permute-done | bytes 524320 | tf_op jit(solution)/shard_map/ppermute | solution.py:20
  223.6 1.8 shard_map.92
  (33 shorter events, 0.4 us)
Async XLA Ops:
  0.0 128.0 %copy-start.7 = (s32[1,1,4,2]{2,3,1,0:T(2,128)S(1)}, s32[1,1,4,2]{2,3,1,0:T(2,128)}, u32[]{:S(2)}) copy-start(s32[1,1,4,2]{2,3,1,0:T(2,128)} %param.11) | copy-start | bytes 100
  0.0 128.9 %copy-start.6 = (f32[256,256]{1,0:T(8,128)S(1)}, f32[256,256]{1,0:T(8,128)}, u32[]{:S(2)}) copy-start(f32[256,256]{1,0:T(8,128)} %param.10) | copy-start | bytes 786436
  80.5 49.4 %copy-start = (f32[2,256,256]{2,1,0:T(8,128)S(1)}, f32[2,256,256]{2,1,0:T(8,128)}, u32[]{:S(2)}) copy-start(f32[2,256,256]{2,1,0:T(8,128)} %rest_0_.7) | copy-start | bytes 1572868
  80.5 49.4 %copy-start.1 = (bf16[1,1,4,256,256]{4,3,2,1,0:T(8,128)(2,1)S(1)}, bf16[1,1,4,256,256]{4,3,2,1,0:T(8,128)(2,1)}, u32[]{:S(2)}) copy-start(bf16[1,1,4,256,256]{4,3,2,1,0:T(8,128)(2,1)} %param.13) | copy-start | bytes 1572868
  80.6 49.4 %copy-start.2 = (bf16[512,512]{1,0:T(8,128)(2,1)S(1)}, bf16[512,512]{1,0:T(8,128)(2,1)}, u32[]{:S(2)}) copy-start(bf16[512,512]{1,0:T(8,128)(2,1)} %constant.4.clone.rest_3_) | copy-start | bytes 1572868
  80.6 49.4 %copy-start.3 = (bf16[512,512]{1,0:T(8,128)(2,1)S(1)}, bf16[512,512]{1,0:T(8,128)(2,1)}, u32[]{:S(2)}) copy-start(bf16[512,512]{1,0:T(8,128)(2,1)} %constant.5.clone.rest_4_) | copy-start | bytes 1572868
  80.6 56.7 %collective-permute-start.7 = (f32[1,2,512,256]{3,2,1,0:T(8,128)}, f32[1,2,512,256]{3,2,1,0:T(8,128)}, u32[]{:S(2)}, u32[]{:S(2)}) collective-permute-start(f32[1,2,512,256]{3,2,1,0:T(8,128)} %get-tuple-element.37), channel_id=1, source_target_pairs={{1,0},{2,1},{3,2},{0,3},{5,4},{6,5},{7,6},{4,7},{9,8},{10,9},{11,1... | collective-permute-start | bytes 3145736 | tf_op jit(solution)/shard_map/ppermute | solution.py:20
  84.1 16.9 %collective-permute-start.4 = (f32[1,2,256,256]{3,2,1,0:T(8,128)S(1)}, f32[1,2,256,256]{3,2,1,0:T(8,128)}, u32[]{:S(2)}, u32[]{:S(2)}) collective-permute-start(f32[1,2,256,256]{3,2,1,0:T(8,128)S(1)} %shard_map.83), channel_id=1, source_target_pairs={{4,0},{8,4},{12,8},{16,12},{20,16},{24,20},{28,24},{0,28},{5,1},{9... | collective-permute-start | bytes 1572872 | tf_op jit(solution)/shard_map/ppermute | solution.py:20
  88.7 23.5 %collective-permute-start.1 = (f32[1,2,256,256]{3,2,1,0:T(8,128)S(1)}, f32[1,2,256,256]{3,2,1,0:T(8,128)}, u32[]{:S(2)}, u32[]{:S(2)}) collective-permute-start(f32[1,2,256,256]{3,2,1,0:T(8,128)S(1)} %get-tuple-element.34), channel_id=1, source_target_pairs={{4,0},{8,4},{12,8},{16,12},{20,16},{24,20},{28,24},{0,28},{5,1},{9... | collective-permute-start | bytes 1572872 | tf_op jit(solution)/shard_map/ppermute | solution.py:20
  89.2 52.1 %collective-permute-start.3 = (f32[1,2,512,256]{3,2,1,0:T(8,128)}, f32[1,2,512,256]{3,2,1,0:T(8,128)S(1)}, u32[]{:S(2)}, u32[]{:S(2)}) collective-permute-start(f32[1,2,512,256]{3,2,1,0:T(8,128)} %get-tuple-element.35), channel_id=1, source_target_pairs={{1,0},{2,1},{3,2},{0,3},{5,4},{6,5},{7,6},{4,7},{9,8},{10,9},{11,1... | collective-permute-start | bytes 3145736 | tf_op jit(solution)/shard_map/ppermute | solution.py:20
  89.3 32.7 %collective-permute-start.5 = (f32[1,2,256,256]{3,2,1,0:T(8,128)S(1)}, f32[1,2,256,256]{3,2,1,0:T(8,128)S(1)}, u32[]{:S(2)}, u32[]{:S(2)}) collective-permute-start(f32[1,2,256,256]{3,2,1,0:T(8,128)S(1)} %get-tuple-element.36), channel_id=1, source_target_pairs={{4,0},{8,4},{12,8},{16,12},{20,16},{24,20},{28,24},{0,28},{5,1},{9... | collective-permute-start | bytes 1572872 | tf_op jit(solution)/shard_map/ppermute | solution.py:20
  101.0 36.3 %collective-permute-start.6 = (f32[1,2,256,256]{3,2,1,0:T(8,128)}, f32[1,2,256,256]{3,2,1,0:T(8,128)}, u32[]{:S(2)}, u32[]{:S(2)}) collective-permute-start(f32[1,2,256,256]{3,2,1,0:T(8,128)} %collective-permute-done.4.near_ref), channel_id=1, source_target_pairs={{1,0},{2,1},{3,2},{0,3},{5,4},{6,5},{7,6},{4,7},{9,8},{10,9},{11,1... | collective-permute-start | bytes 1572872 | tf_op jit(solution)/shard_map/ppermute | solution.py:20
  112.2 29.1 %collective-permute-start.2 = (f32[1,2,256,256]{3,2,1,0:T(8,128)}, f32[1,2,256,256]{3,2,1,0:T(8,128)}, u32[]{:S(2)}, u32[]{:S(2)}) collective-permute-start(f32[1,2,256,256]{3,2,1,0:T(8,128)} %collective-permute-done.1.near_ref), channel_id=1, source_target_pairs={{1,0},{2,1},{3,2},{0,3},{5,4},{6,5},{7,6},{4,7},{9,8},{10,9},{11,1... | collective-permute-start | bytes 1572872 | tf_op jit(solution)/shard_map/ppermute | solution.py:20
  122.1 0.8 copy-start.4
  122.9 19.8 %collective-permute-start = (f32[1,2,256,256]{3,2,1,0:T(8,128)}, f32[1,2,256,256]{3,2,1,0:T(8,128)}, u32[]{:S(2)}, u32[]{:S(2)}) collective-permute-start(f32[1,2,256,256]{3,2,1,0:T(8,128)} %get-tuple-element.33), channel_id=1, source_target_pairs={{4,0},{8,4},{12,8},{16,12},{20,16},{24,20},{28,24},{0,28},{5,1},{9... | collective-permute-start | bytes 1572872 | tf_op jit(solution)/shard_map/ppermute | solution.py:20
  128.9 8.4 %copy-start.5 = (f32[1,2,256,256]{3,2,1,0:T(8,128)S(1)}, f32[1,2,256,256]{3,2,1,0:T(8,128)}, u32[]{:S(2)}) copy-start(f32[1,2,256,256]{3,2,1,0:T(8,128)} %copy-done.4) | copy-start | bytes 1572868
  150.5 8.7 %collective-permute-start.11 = (f32[1,2,256,256]{3,2,1,0:T(8,128)S(1)}, f32[1,2,256,256]{3,2,1,0:T(8,128)S(1)}, u32[]{:S(2)}, u32[]{:S(2)}) collective-permute-start(f32[1,2,256,256]{3,2,1,0:T(8,128)S(1)} %get-tuple-element.55), channel_id=1, source_target_pairs={{3,0},{0,1},{1,2},{2,3},{7,4},{4,5},{5,6},{6,7},{11,8},{8,9},{9,10... | collective-permute-start | bytes 1572872 | tf_op jit(solution)/shard_map/ppermute | solution.py:20
  159.2 50.5 %collective-permute-start.12 = (f32[2,2,512,256]{3,2,1,0:T(8,128)S(1)}, f32[2,2,512,256]{3,2,1,0:T(8,128)S(1)}, u32[]{:S(2)}, u32[]{:S(2)}) collective-permute-start(f32[2,2,512,256]{3,2,1,0:T(8,128)S(1)} %get-tuple-element.57), channel_id=1, source_target_pairs={{3,0},{0,1},{1,2},{2,3},{7,4},{4,5},{5,6},{6,7},{11,8},{8,9},{9,10... | collective-permute-start | bytes 6291464 | tf_op jit(solution)/shard_map/ppermute | solution.py:20
  159.2 31.1 %collective-permute-start.9 = (f32[1,2,256,256]{3,2,1,0:T(8,128)S(1)}, f32[1,2,256,256]{3,2,1,0:T(8,128)S(1)}, u32[]{:S(2)}, u32[]{:S(2)}) collective-permute-start(f32[1,2,256,256]{3,2,1,0:T(8,128)S(1)} %get-tuple-element.54), channel_id=1, source_target_pairs={{3,0},{0,1},{1,2},{2,3},{7,4},{4,5},{5,6},{6,7},{11,8},{8,9},{9,10... | collective-permute-start | bytes 1572872 | tf_op jit(solution)/shard_map/ppermute | solution.py:20
  159.2 31.4 %collective-permute-start.8 = (f32[1,2,256,256]{3,2,1,0:T(8,128)S(1)}, f32[1,2,256,256]{3,2,1,0:T(8,128)S(1)}, u32[]{:S(2)}, u32[]{:S(2)}) collective-permute-start(f32[1,2,256,256]{3,2,1,0:T(8,128)S(1)} %get-tuple-element.52), channel_id=1, source_target_pairs={{28,0},{0,4},{4,8},{8,12},{12,16},{16,20},{20,24},{24,28},{29,1},{... | collective-permute-start | bytes 1572872 | tf_op jit(solution)/shard_map/ppermute | solution.py:20
  190.3 17.5 %collective-permute-start.10 = (f32[1,2,256,256]{3,2,1,0:T(8,128)S(1)}, f32[1,2,256,256]{3,2,1,0:T(8,128)S(1)}, u32[]{:S(2)}, u32[]{:S(2)}) collective-permute-start(f32[1,2,256,256]{3,2,1,0:T(8,128)S(1)} %add.6), channel_id=1, source_target_pairs={{28,0},{0,4},{4,8},{8,12},{12,16},{16,20},{20,24},{24,28},{29,1},{... | collective-permute-start | bytes 1572872 | tf_op jit(solution)/shard_map/ppermute | solution.py:20
  190.4 27.6 %collective-permute-start.13 = (f32[1,2,256,256]{3,2,1,0:T(8,128)S(1)}, f32[1,2,256,256]{3,2,1,0:T(8,128)S(1)}, u32[]{:S(2)}, u32[]{:S(2)}) collective-permute-start(f32[1,2,256,256]{3,2,1,0:T(8,128)S(1)} %get-tuple-element.58), channel_id=1, source_target_pairs={{28,0},{0,4},{4,8},{8,12},{12,16},{16,20},{20,24},{24,28},{29,1},{... | collective-permute-start | bytes 1572872 | tf_op jit(solution)/shard_map/ppermute | solution.py:20
  190.5 33.1 %collective-permute-start.14 = (f32[1,2,256,256]{3,2,1,0:T(8,128)S(1)}, f32[1,2,256,256]{3,2,1,0:T(8,128)S(1)}, u32[]{:S(2)}, u32[]{:S(2)}) collective-permute-start(f32[1,2,256,256]{3,2,1,0:T(8,128)S(1)} %add.7), channel_id=1, source_target_pairs={{28,0},{0,4},{4,8},{8,12},{12,16},{16,20},{20,24},{24,28},{29,1},{... | collective-permute-start | bytes 1572872 | tf_op jit(solution)/shard_map/ppermute | solution.py:20

commit v3 on v2

--- a/solution.py
+++ b/solution.py
@@ -217,11 +217,12 @@
 
 
 def from_strips(out, strips, row0, store, plane):
-    for c in range(out.shape[1]):
-        for k, strip in enumerate(strips):
-            out[0, c, :, pl.ds(k * lanes, lanes)] = store[
-                plane, c, strip, pl.ds(row0, out.shape[2]), :
-            ]
+    for s in range(out.shape[0]):
+        for c in range(out.shape[1]):
+            for k, strip in enumerate(strips):
+                out[s, c, :, pl.ds(k * lanes, lanes)] = store[
+                    plane + s, c, strip, pl.ds(row0, out.shape[2]), :
+                ]
 
 
 def into_strips(piece, strips, row0, store, plane):
@@ -250,13 +251,13 @@
     return pl.pallas_call(
         functools.partial(pack_kernel, [piece[:3] for piece in pieces]),
         out_shape=[
-            jax.ShapeDtypeStruct((1, object_field.shape[1], *piece[3:]), jnp.float32)
+            pltpu.VMEM((1, object_field.shape[1], *piece[3:]), jnp.float32)
             for piece in pieces
         ],
         in_specs=[hbm_space],
-        out_specs=[any_space] * len(pieces),
+        out_specs=[vmem_space] * len(pieces),
         scratch_shapes=[pltpu.SemaphoreType.DMA],
-        compiler_params=pltpu.CompilerParams(vmem_limit_bytes=1024 * 1024),
+        compiler_params=pltpu.CompilerParams(vmem_limit_bytes=6 * 1024 * 1024),
     )(in_hbm(object_field))
 
 
@@ -339,7 +340,8 @@
 
 def first_kernel(places, count, *rest):
     constants = rest[:5]
-    near_out, far_out, corner_out, _, gradient, _, inners, todo, _ = rest[9:]
+    near_out, far_out, corner_out, right_out = rest[9:13]
+    _, gradient, _, inners, todo, _ = rest[13:]
     length = constants[0].shape[-1]
     tile = length + far_out.shape[3]
     _, near, far, past = sizes(tile, length)
@@ -353,19 +355,12 @@
     from_strips(corner_out, past, tile, gradient, 0)
     from_strips(far_out, far, tile, gradient, 0)
     from_strips(near_out, near, tile, gradient, 0)
-
-
-def own_kernel(gradient, own_out, right_out, sem):
+    from_strips(right_out, past, 0, gradient, 0)
+
+
+def own_kernel(gradient, own_out, sem):
     tile = own_out.shape[-1]
-    own, _, _, past = sizes(tile, right_out.shape[-1])
-    finish(
-        run_copies(
-            [
-                strip_copies(right_out, past, 0, gradient, 0, sem, True),
-                strip_copies(own_out, own, 0, gradient, 0, sem, True),
-            ]
-        )
-    )
+    finish(run_copies([strip_copies(own_out, range(tile // lanes), 0, gradient, 0, sem, True)]))
 
 
 def add_kernel(plane, column, gradient_in, piece_ref, gradient_out, held, added, sems):
@@ -404,6 +399,28 @@
         input_output_aliases={0: 0},
         compiler_params=pltpu.CompilerParams(vmem_limit_bytes=8 * 1024 * 1024),
     )(gradient, piece)
+
+
+def corner_copies(gradient, held, sem, outward):
+    copies = []
+    for c in range(held.shape[1]):
+        part = gradient.at[0, c, pl.ds(0, held.shape[2]), pl.ds(0, held.shape[3])]
+        source, target = (held.at[0, c], part) if outward else (part, held.at[0, c])
+        copies.append(pltpu.make_async_copy(source, target, sem))
+    return copies
+
+
+def hold_kernel(gradient, held, sem):
+    finish(run_copies([corner_copies(gradient, held, sem, False)]))
+
+
+def last_kernel(gradient_in, held, piece, gradient, total, sem):
+    del gradient_in
+    stores = corner_copies(gradient, total, sem, True)
+    for c, store in enumerate(stores):
+        total[0, c] = held[0, c] + piece[0, c]
+        store.start()
+    finish(stores)
 
 
 def in_hbm(x):
@@ -505,30 +522,46 @@
     near1, far1, corner1, *state = call(back_kernel, (far1,), (window, *others), piece_shapes)
     corner1 = shifted(corner1, "col", 1)
     far1 = shifted(far1, "row", 1)
-    near0, far0, corner0, window, gradient, *_ = call(first_kernel, (), state, piece_shapes)
+    near0, far0, corner0, right, window, gradient, *_ = call(
+        first_kernel, (), state, (*piece_shapes, (slices, parts, tile, length))
+    )
     near1 = shifted(near1 + corner1, "row", 1)
     corner0 = shifted(corner0, "col", 1)
+    right = shifted(right, "col", 1)
     far0 = shifted(far0, "row", 1)
-    own, right = pl.pallas_call(
+    own = pl.pallas_call(
         own_kernel,
         name="own",
-        out_shape=[
-            jax.ShapeDtypeStruct(object_field.shape, jnp.float32),
-            jax.ShapeDtypeStruct((slices, parts, tile, length), jnp.float32),
-        ],
+        out_shape=jax.ShapeDtypeStruct(object_field.shape, jnp.float32),
         in_specs=[vmem_space],
-        out_specs=[any_space] * 2,
+        out_specs=any_space,
         scratch_shapes=[pltpu.SemaphoreType.DMA],
-        compiler_params=pltpu.CompilerParams(vmem_limit_bytes=4 * 1024 * 1024),
+        compiler_params=pltpu.CompilerParams(vmem_limit_bytes=1024 * 1024),
     )(in_vmem(gradient))
-    corner0, right = lax.optimization_barrier((corner0, right))
     near0 = shifted(near0 + corner0, "row", 1)
-    right = shifted(right, "col", 1)
     result = add_piece(own, far1, 1, length)
     result = add_piece(result, near1, 1, 0)
     result = add_piece(result, right, 0, 0)
     result = add_piece(result, far0, 0, length)
-    return add_piece(result, near0, 0, 0)
+    held = pl.pallas_call(
+        hold_kernel,
+        name="hold",
+        out_shape=pltpu.VMEM(near0.shape, jnp.float32),
+        in_specs=[any_space],
+        out_specs=vmem_space,
+        scratch_shapes=[pltpu.SemaphoreType.DMA],
+        compiler_params=pltpu.CompilerParams(vmem_limit_bytes=2 * 1024 * 1024),
+    )(in_hbm(result))
+    return pl.pallas_call(
+        last_kernel,
+        name="add_near0",
+        out_shape=jax.ShapeDtypeStruct(result.shape, jnp.float32),
+        in_specs=[any_space, vmem_space, vmem_space],
+        out_specs=any_space,
+        scratch_shapes=[pltpu.VMEM(near0.shape, jnp.float32), pltpu.SemaphoreType.DMA],
+        input_output_aliases={0: 0},
+        compiler_params=pltpu.CompilerParams(vmem_limit_bytes=2 * 1024 * 1024),
+    )(result, in_vmem(held), in_vmem(near0))
 
 
 def solution(mesh):

time: 226 us -> 135 us (0.60)
  Pallas kernels: 114 us -> 37.1 us
  waiting for transfers between devices: 93.8 us -> 79.1 us
    pallas_call x2, Pallas kernels: 81.6 us -> 4.6 us  [pack(): pl.pallas_call(functools.partial(pack_kernel, [piece[:3] for piece in pie...]
    ppermute x15, waiting for transfers between devices: 93.8 us -> 79.1 us  [shifted(): return lax.ppermute(block, axis, route)]
    pallas_call x5 -> x4, Pallas kernels: 9.8 us -> 7.98 us  [add_piece(): pl.pallas_call(functools.partial(add_kernel, plane, column), out_shape=ja...]
  transfers between devices with their start and end apart: 15 -> 15, of which waited for: 8 -> 8; matrix products, arithmetic and copies ran while one was open for 1% -> 1% of each run, Pallas kernels for 11% -> 20%
where the time goes in v3:
time: 135 us; the launch traced here: 134 us
  waiting for transfers between devices  79.1 us (59%)
  Pallas kernels  37.1 us (27%)
  starting transfers between devices  15 us (11%)
  local copies, waits for them, and re-layouts  1.98 us (1%)
    ppermute x15, waiting for transfers between devices, shifted(): return lax.ppermute(block, axis, route)  79.1 us
    pallas_call x4, Pallas kernels, slots_call(): pl.pallas_call(body, out_shape=[pltpu.VMEM(s, jnp.float32) for s in out_s...  19.3 us
    ppermute x15, starting transfers between devices, shifted(): return lax.ppermute(block, axis, route)  15 us
    pallas_call x4, Pallas kernels, add_piece(): pl.pallas_call(functools.partial(add_kernel, plane, column), out_shape=ja...  7.98 us
    pallas_call x2, Pallas kernels, pack(): pl.pallas_call(functools.partial(pack_kernel, [piece[:3] for piece in pie...  4.6 us
  transfers between devices with their start and end apart: 15, of which 8 were waited for; matrix products, arithmetic and copies ran while one was open for 1% of the time, Pallas kernels for 20%

profile of v3, /device:TPU:0, one launch (start us, length us, event | category | flops | bytes accessed | tf_op | source)
XLA Modules:
  0.0 134.4 jit_solution(2975189618312586737)
XLA Ops:
  0.0 1.1 shard_map.83
  1.1 6.1 %collective-permute-start.4 = (f32[1,2,256,256]{3,2,1,0:T(8,128)S(1)}, f32[1,2,256,256]{3,2,1,0:T(8,128)}, u32[]{:S(2)}, u32[]{:S(2)}) collective-permute-start(f32[1,2,256,256]{3,2,1,0:T(8,128)S(1)} %shard_map.83), channel_id=1, source_target_pairs={{4,0},{8,4},{12,8},{16,12},{20,16},{24,20},{28,24},{0,28},{5,1},{9... | collective-permute-start | bytes 1572872 | tf_op jit(solution)/shard_map/ppermute | solution.py:20
  7.2 3.5 %shard_map.82 = (f32[1,2,512,256]{3,2,1,0:T(8,128)}, f32[1,2,256,256]{3,2,1,0:T(8,128)S(1)}, f32[1,2,256,256]{3,2,1,0:T(8,128)S(1)}, f32[1,2,256,256]{3,2,1,0:T(8,128)}, f32[1,2,512,256]{3,2,1,0:T(8,128)}) custom-call(f32[2,2,512,512]{3,2,1,0:T(8,128)} %object_ref.5), custom_call_target="tpu_custom_call" | custom-call | tf_op jit(solution)/shard_map/pallas_call | solution.py:251
  10.7 0.7 collective-permute-start.7
  11.5 0.7 collective-permute-start.1
  12.2 0.5 collective-permute-start.3
  12.7 1.4 %collective-permute-start.5 = (f32[1,2,256,256]{3,2,1,0:T(8,128)S(1)}, f32[1,2,256,256]{3,2,1,0:T(8,128)S(1)}, u32[]{:S(2)}, u32[]{:S(2)}) collective-permute-start(f32[1,2,256,256]{3,2,1,0:T(8,128)S(1)} %get-tuple-element.33), channel_id=1, source_target_pairs={{4,0},{8,4},{12,8},{16,12},{20,16},{24,20},{28,24},{0,28},{5,1},{9... | collective-permute-start | bytes 1572872 | tf_op jit(solution)/shard_map/ppermute | solution.py:20
  14.0 5.5 %collective-permute-done.4.near_ref = f32[1,2,256,256]{3,2,1,0:T(8,128)} collective-permute-done((f32[1,2,256,256]{3,2,1,0:T(8,128)S(1)}, f32[1,2,256,256]{3,2,1,0:T(8,128)}, u32[]{:S(2)}, u32[]{:S(2)}) %collective-permute-start.4) | collective-permute-done | bytes 524320 | tf_op jit(solution)/shard_map/ppermute | solution.py:20
  19.5 11.2 %collective-permute-done.1.near_ref = f32[1,2,256,256]{3,2,1,0:T(8,128)} collective-permute-done((f32[1,2,256,256]{3,2,1,0:T(8,128)S(1)}, f32[1,2,256,256]{3,2,1,0:T(8,128)}, u32[]{:S(2)}, u32[]{:S(2)}) %collective-permute-start.1) | collective-permute-done | bytes 524320 | tf_op jit(solution)/shard_map/ppermute | solution.py:20
  30.8 10.1 %collective-permute-done.5.far_ref = f32[1,2,256,256]{3,2,1,0:T(8,128)S(1)} collective-permute-done((f32[1,2,256,256]{3,2,1,0:T(8,128)S(1)}, f32[1,2,256,256]{3,2,1,0:T(8,128)S(1)}, u32[]{:S(2)}, u32[]{:S(2)}) %collective-permute-start.5) | collective-permute-done | bytes 524320 | tf_op jit(solution)/shard_map/ppermute | solution.py:20
  40.9 0.8 copy-done.4
  41.7 5.2 %collective-permute-start = (f32[1,2,256,256]{3,2,1,0:T(8,128)}, f32[1,2,256,256]{3,2,1,0:T(8,128)}, u32[]{:S(2)}, u32[]{:S(2)}) collective-permute-start(f32[1,2,256,256]{3,2,1,0:T(8,128)} %get-tuple-element.30), channel_id=1, source_target_pairs={{4,0},{8,4},{12,8},{16,12},{20,16},{24,20},{28,24},{0,28},{5,1},{9... | collective-permute-start | bytes 1572872 | tf_op jit(solution)/shard_map/ppermute | solution.py:20
  47.5 0.1 copy.28
  47.6 0.1 reshape.6.places
  47.7 0.9 cosine_bitcast_fusion
  48.7 7.3 %shard_map.84 = (f32[2,2,6,768,128]{4,3,2,1,0:T(8,128)S(1)}, f32[2,2,6,768,128]{4,3,2,1,0:T(8,128)S(1)}, f32[4,2,256,256]{3,2,1,0:T(8,128)S(1)}, bf16[4,512,256]{2,1,0:T(8,128)(2,1)S(1)}) custom-call(s32[8]{0:T(128)S(1)} %reshape.6.places, s32[1]{0:T(128)} %bitcast.6.count, f32[2,2,512,512]{3,2,1,0:T(8,128)} %object_ref.5, f32[2,256,256]{2,1,0:T(8,128)S(1)} %copy-done, ...), custom_call_target="tpu_custom_call" | custom-call | tf_op jit(solution)/shard_map/pallas_call | solution.py:447
  56.1 4.0 %shard_map.85 = (f32[2,2,6,768,128]{4,3,2,1,0:T(8,128)S(1)}, f32[2,2,6,768,128]{4,3,2,1,0:T(8,128)S(1)}, f32[4,2,256,256]{3,2,1,0:T(8,128)S(1)}, bf16[4,512,256]{2,1,0:T(8,128)(2,1)S(1)}) custom-call(s32[8]{0:T(128)S(1)} %reshape.6.places, s32[1]{0:T(128)} %bitcast.7.count, ...), custom_call_target="tpu_custom_call", output_to_operand_aliasing={{0}: (11, {}), {1}: (12, {}), {2}: (13, {}), {3}: (14, {})} | custom-call | tf_op jit(solution)/shard_map/pallas_call | solution.py:447
  60.2 1.3 load_halo.1.rest_5_
  61.5 3.9 %shard_map.86 = (f32[1,2,256,256]{3,2,1,0:T(8,128)S(1)}, f32[1,2,256,256]{3,2,1,0:T(8,128)S(1)}, f32[1,2,256,256]{3,2,1,0:T(8,128)S(1)}, f32[2,2,6,768,128]{4,3,...) custom-call(s32[8]{0:T(128)S(1)} %reshape.6.places, ...), custom_call_target="tpu_custom_call", output_to_operand_aliasing={{3}: (8, {}), {4}: (9, {}), {5}: (10, {}), {6}: (11, {})} | custom-call | tf_op jit(solution)/shard_map/pallas_call | solution.py:447
  65.3 4.1 %shard_map.87 = (f32[1,2,256,256]{3,2,1,0:T(8,128)S(1)}, f32[1,2,256,256]{3,2,1,0:T(8,128)S(1)}, f32[1,2,256,256]{3,2,1,0:T(8,128)S(1)}, f32[2,2,512,256]{3,2,1,...) custom-call(s32[8]{0:T(128)S(1)} %reshape.6.places, ...), custom_call_target="tpu_custom_call", output_to_operand_aliasing={{4}: (7, {}), {5}: (8, {}), {6}: (9, {}), {7}: (10, {})} | custom-call | tf_op jit(solution)/shard_map/pallas_call | solution.py:447
  69.7 30.9 %collective-permute-done.9 = f32[1,2,256,256]{3,2,1,0:T(8,128)S(1)} collective-permute-done((f32[1,2,256,256]{3,2,1,0:T(8,128)S(1)}, f32[1,2,256,256]{3,2,1,0:T(8,128)S(1)}, u32[]{:S(2)}, u32[]{:S(2)}) %collective-permute-start.9) | collective-permute-done | bytes 524320 | tf_op jit(solution)/shard_map/ppermute | solution.py:20
  100.8 5.4 %collective-permute-done.13 = f32[1,2,256,256]{3,2,1,0:T(8,128)S(1)} collective-permute-done((f32[1,2,256,256]{3,2,1,0:T(8,128)S(1)}, f32[1,2,256,256]{3,2,1,0:T(8,128)S(1)}, u32[]{:S(2)}, u32[]{:S(2)}) %collective-permute-start.13) | collective-permute-done | bytes 524320 | tf_op jit(solution)/shard_map/ppermute | solution.py:20
  106.3 2.0 %own.1.gradient_in = f32[2,2,512,512]{3,2,1,0:T(8,128)} custom-call(f32[2,2,6,768,128]{4,3,2,1,0:T(8,128)S(1)} %get-tuple-element.47.gradient), custom_call_target="tpu_custom_call" | custom-call | tf_op jit(solution)/shard_map/own/pallas_call | solution.py:532
  108.4 1.8 %shard_map.88.gradient_in = f32[2,2,512,512]{3,2,1,0:T(8,128)} custom-call(f32[2,2,512,512]{3,2,1,0:T(8,128)} %own.1.gradient_in, f32[1,2,256,256]{3,2,1,0:T(8,128)S(1)} %collective-permute-done.8.piece_ref), custom_call_target="tpu_custom_call", output_to_operand_aliasing={{}: (0, {})} | custom-call | tf_op jit(solution)/shard_map/pallas_call | solution.py:392
  110.2 8.0 %collective-permute-done.10.piece_ref = f32[1,2,256,256]{3,2,1,0:T(8,128)S(1)} collective-permute-done((f32[1,2,256,256]{3,2,1,0:T(8,128)S(1)}, f32[1,2,256,256]{3,2,1,0:T(8,128)S(1)}, u32[]{:S(2)}, u32[]{:S(2)}) %collective-permute-start.10) | collective-permute-done | bytes 524320 | tf_op jit(solution)/shard_map/ppermute | solution.py:20
  118.2 1.8 %shard_map.89.gradient_in = f32[2,2,512,512]{3,2,1,0:T(8,128)} custom-call(f32[2,2,512,512]{3,2,1,0:T(8,128)} %shard_map.88.gradient_in, f32[1,2,256,256]{3,2,1,0:T(8,128)S(1)} %collective-permute-done.10.piece_ref), custom_call_target="tpu_custom_call", output_to_operand_aliasing={{}: (0, {})} | custom-call | tf_op jit(solution)/shard_map/pallas_call | solution.py:392
  120.0 2.5 %shard_map.90.gradient_in = f32[2,2,512,512]{3,2,1,0:T(8,128)} custom-call(f32[2,2,512,512]{3,2,1,0:T(8,128)} %shard_map.89.gradient_in, f32[2,2,512,256]{3,2,1,0:T(8,128)S(1)} %collective-permute-done.11.piece_ref), custom_call_target="tpu_custom_call", output_to_operand_aliasing={{}: (0, {})} | custom-call | tf_op jit(solution)/shard_map/pallas_call | solution.py:392
  122.6 5.2 %collective-permute-done.12.piece_ref = f32[1,2,256,256]{3,2,1,0:T(8,128)S(1)} collective-permute-done((f32[1,2,256,256]{3,2,1,0:T(8,128)S(1)}, f32[1,2,256,256]{3,2,1,0:T(8,128)S(1)}, u32[]{:S(2)}, u32[]{:S(2)}) %collective-permute-start.12) | collective-permute-done | bytes 524320 | tf_op jit(solution)/shard_map/ppermute | solution.py:20
  127.8 1.8 %shard_map.91.gradient.gradient_in = f32[2,2,512,512]{3,2,1,0:T(8,128)} custom-call(f32[2,2,512,512]{3,2,1,0:T(8,128)} %shard_map.90.gradient_in, f32[1,2,256,256]{3,2,1,0:T(8,128)S(1)} %collective-permute-done.12.piece_ref), custom_call_target="tpu_custom_call", output_to_operand_aliasing={{}: (0, {})} | custom-call | tf_op jit(solution)/shard_map/pallas_call | solution.py:392
  129.6 1.0 hold.1.held
  130.7 2.7 %collective-permute-done.14.piece = f32[1,2,256,256]{3,2,1,0:T(8,128)S(1)} collective-permute-done((f32[1,2,256,256]{3,2,1,0:T(8,128)S(1)}, f32[1,2,256,256]{3,2,1,0:T(8,128)S(1)}, u32[]{:S(2)}, u32[]{:S(2)}) %collective-permute-start.14) | collective-permute-done | bytes 524320 | tf_op jit(solution)/shard_map/ppermute | solution.py:20
  133.4 0.8 add_near0.1
  (34 shorter events, 0.6 us)
Async XLA Ops:
  0.0 47.5 %copy-start.7 = (s32[1,1,4,2]{2,3,1,0:T(2,128)S(1)}, s32[1,1,4,2]{2,3,1,0:T(2,128)}, u32[]{:S(2)}) copy-start(s32[1,1,4,2]{2,3,1,0:T(2,128)} %param.11) | copy-start | bytes 100
  0.0 47.7 %copy-start.6 = (f32[256,256]{1,0:T(8,128)S(1)}, f32[256,256]{1,0:T(8,128)}, u32[]{:S(2)}) copy-start(f32[256,256]{1,0:T(8,128)} %param.10) | copy-start | bytes 786436
  1.1 47.6 %copy-start = (f32[2,256,256]{2,1,0:T(8,128)S(1)}, f32[2,256,256]{2,1,0:T(8,128)}, u32[]{:S(2)}) copy-start(f32[2,256,256]{2,1,0:T(8,128)} %rest_0_.7) | copy-start | bytes 1572868
  1.1 47.6 %copy-start.1 = (bf16[1,1,4,256,256]{4,3,2,1,0:T(8,128)(2,1)S(1)}, bf16[1,1,4,256,256]{4,3,2,1,0:T(8,128)(2,1)}, u32[]{:S(2)}) copy-start(bf16[1,1,4,256,256]{4,3,2,1,0:T(8,128)(2,1)} %param.13) | copy-start | bytes 1572868
  1.1 47.6 %copy-start.2 = (bf16[512,512]{1,0:T(8,128)(2,1)S(1)}, bf16[512,512]{1,0:T(8,128)(2,1)}, u32[]{:S(2)}) copy-start(bf16[512,512]{1,0:T(8,128)(2,1)} %constant.5.clone.rest_4_) | copy-start | bytes 1572868
  1.1 47.6 %copy-start.3 = (bf16[512,512]{1,0:T(8,128)(2,1)S(1)}, bf16[512,512]{1,0:T(8,128)(2,1)}, u32[]{:S(2)}) copy-start(bf16[512,512]{1,0:T(8,128)(2,1)} %constant.4.clone.rest_3_) | copy-start | bytes 1572868
  1.1 18.4 %collective-permute-start.4 = (f32[1,2,256,256]{3,2,1,0:T(8,128)S(1)}, f32[1,2,256,256]{3,2,1,0:T(8,128)}, u32[]{:S(2)}, u32[]{:S(2)}) collective-permute-start(f32[1,2,256,256]{3,2,1,0:T(8,128)S(1)} %shard_map.83), channel_id=1, source_target_pairs={{4,0},{8,4},{12,8},{16,12},{20,16},{24,20},{28,24},{0,28},{5,1},{9... | collective-permute-start | bytes 1572872 | tf_op jit(solution)/shard_map/ppermute | solution.py:20
  10.7 45.4 %collective-permute-start.7 = (f32[1,2,512,256]{3,2,1,0:T(8,128)}, f32[1,2,512,256]{3,2,1,0:T(8,128)}, u32[]{:S(2)}, u32[]{:S(2)}) collective-permute-start(f32[1,2,512,256]{3,2,1,0:T(8,128)} %get-tuple-element.34), channel_id=1, source_target_pairs={{1,0},{2,1},{3,2},{0,3},{5,4},{6,5},{7,6},{4,7},{9,8},{10,9},{11,1... | collective-permute-start | bytes 3145736 | tf_op jit(solution)/shard_map/ppermute | solution.py:20
  11.5 19.3 %collective-permute-start.1 = (f32[1,2,256,256]{3,2,1,0:T(8,128)S(1)}, f32[1,2,256,256]{3,2,1,0:T(8,128)}, u32[]{:S(2)}, u32[]{:S(2)}) collective-permute-start(f32[1,2,256,256]{3,2,1,0:T(8,128)S(1)} %get-tuple-element.31), channel_id=1, source_target_pairs={{4,0},{8,4},{12,8},{16,12},{20,16},{24,20},{28,24},{0,28},{5,1},{9... | collective-permute-start | bytes 1572872 | tf_op jit(solution)/shard_map/ppermute | solution.py:20
  12.2 48.0 %collective-permute-start.3 = (f32[1,2,512,256]{3,2,1,0:T(8,128)}, f32[1,2,512,256]{3,2,1,0:T(8,128)S(1)}, u32[]{:S(2)}, u32[]{:S(2)}) collective-permute-start(f32[1,2,512,256]{3,2,1,0:T(8,128)} %get-tuple-element.32), channel_id=1, source_target_pairs={{1,0},{2,1},{3,2},{0,3},{5,4},{6,5},{7,6},{4,7},{9,8},{10,9},{11,1... | collective-permute-start | bytes 3145736 | tf_op jit(solution)/shard_map/ppermute | solution.py:20
  12.7 28.2 %collective-permute-start.5 = (f32[1,2,256,256]{3,2,1,0:T(8,128)S(1)}, f32[1,2,256,256]{3,2,1,0:T(8,128)S(1)}, u32[]{:S(2)}, u32[]{:S(2)}) collective-permute-start(f32[1,2,256,256]{3,2,1,0:T(8,128)S(1)} %get-tuple-element.33), channel_id=1, source_target_pairs={{4,0},{8,4},{12,8},{16,12},{20,16},{24,20},{28,24},{0,28},{5,1},{9... | collective-permute-start | bytes 1572872 | tf_op jit(solution)/shard_map/ppermute | solution.py:20
  19.5 36.6 %collective-permute-start.6 = (f32[1,2,256,256]{3,2,1,0:T(8,128)}, f32[1,2,256,256]{3,2,1,0:T(8,128)}, u32[]{:S(2)}, u32[]{:S(2)}) collective-permute-start(f32[1,2,256,256]{3,2,1,0:T(8,128)} %collective-permute-done.4.near_ref), channel_id=1, source_target_pairs={{1,0},{2,1},{3,2},{0,3},{5,4},{6,5},{7,6},{4,7},{9,8},{10,9},{11,1... | collective-permute-start | bytes 1572872 | tf_op jit(solution)/shard_map/ppermute | solution.py:20
  30.7 29.4 %collective-permute-start.2 = (f32[1,2,256,256]{3,2,1,0:T(8,128)}, f32[1,2,256,256]{3,2,1,0:T(8,128)}, u32[]{:S(2)}, u32[]{:S(2)}) collective-permute-start(f32[1,2,256,256]{3,2,1,0:T(8,128)} %collective-permute-done.1.near_ref), channel_id=1, source_target_pairs={{1,0},{2,1},{3,2},{0,3},{5,4},{6,5},{7,6},{4,7},{9,8},{10,9},{11,1... | collective-permute-start | bytes 1572872 | tf_op jit(solution)/shard_map/ppermute | solution.py:20
  40.9 0.8 copy-start.4
  41.7 19.8 %collective-permute-start = (f32[1,2,256,256]{3,2,1,0:T(8,128)}, f32[1,2,256,256]{3,2,1,0:T(8,128)}, u32[]{:S(2)}, u32[]{:S(2)}) collective-permute-start(f32[1,2,256,256]{3,2,1,0:T(8,128)} %get-tuple-element.30), channel_id=1, source_target_pairs={{4,0},{8,4},{12,8},{16,12},{20,16},{24,20},{28,24},{0,28},{5,1},{9... | collective-permute-start | bytes 1572872 | tf_op jit(solution)/shard_map/ppermute | solution.py:20
  47.7 8.4 %copy-start.5 = (f32[1,2,256,256]{3,2,1,0:T(8,128)S(1)}, f32[1,2,256,256]{3,2,1,0:T(8,128)}, u32[]{:S(2)}) copy-start(f32[1,2,256,256]{3,2,1,0:T(8,128)} %copy-done.4) | copy-start | bytes 1572868
  69.5 50.6 %collective-permute-start.11 = (f32[2,2,512,256]{3,2,1,0:T(8,128)S(1)}, f32[2,2,512,256]{3,2,1,0:T(8,128)S(1)}, u32[]{:S(2)}, u32[]{:S(2)}) collective-permute-start(f32[2,2,512,256]{3,2,1,0:T(8,128)S(1)} %get-tuple-element.51), channel_id=1, source_target_pairs={{3,0},{0,1},{1,2},{2,3},{7,4},{4,5},{5,6},{6,7},{11,8},{8,9},{9,10... | collective-permute-start | bytes 6291464 | tf_op jit(solution)/shard_map/ppermute | solution.py:20
  69.5 31.1 %collective-permute-start.9 = (f32[1,2,256,256]{3,2,1,0:T(8,128)S(1)}, f32[1,2,256,256]{3,2,1,0:T(8,128)S(1)}, u32[]{:S(2)}, u32[]{:S(2)}) collective-permute-start(f32[1,2,256,256]{3,2,1,0:T(8,128)S(1)} %get-tuple-element.50), channel_id=1, source_target_pairs={{3,0},{0,1},{1,2},{2,3},{7,4},{4,5},{5,6},{6,7},{11,8},{8,9},{9,10... | collective-permute-start | bytes 1572872 | tf_op jit(solution)/shard_map/ppermute | solution.py:20
  69.6 36.6 %collective-permute-start.13 = (f32[1,2,256,256]{3,2,1,0:T(8,128)S(1)}, f32[1,2,256,256]{3,2,1,0:T(8,128)S(1)}, u32[]{:S(2)}, u32[]{:S(2)}) collective-permute-start(f32[1,2,256,256]{3,2,1,0:T(8,128)S(1)} %get-tuple-element.54), channel_id=1, source_target_pairs={{3,0},{0,1},{1,2},{2,3},{7,4},{4,5},{5,6},{6,7},{11,8},{8,9},{9,10... | collective-permute-start | bytes 1572872 | tf_op jit(solution)/shard_map/ppermute | solution.py:20
  69.7 38.7 %collective-permute-start.8 = (f32[1,2,256,256]{3,2,1,0:T(8,128)S(1)}, f32[1,2,256,256]{3,2,1,0:T(8,128)S(1)}, u32[]{:S(2)}, u32[]{:S(2)}) collective-permute-start(f32[1,2,256,256]{3,2,1,0:T(8,128)S(1)} %get-tuple-element.48), channel_id=1, source_target_pairs={{28,0},{0,4},{4,8},{8,12},{12,16},{16,20},{20,24},{24,28},{29,1},{... | collective-permute-start | bytes 1572872 | tf_op jit(solution)/shard_map/ppermute | solution.py:20
  100.7 17.5 %collective-permute-start.10 = (f32[1,2,256,256]{3,2,1,0:T(8,128)S(1)}, f32[1,2,256,256]{3,2,1,0:T(8,128)S(1)}, u32[]{:S(2)}, u32[]{:S(2)}) collective-permute-start(f32[1,2,256,256]{3,2,1,0:T(8,128)S(1)} %add.6), channel_id=1, source_target_pairs={{28,0},{0,4},{4,8},{8,12},{12,16},{16,20},{20,24},{24,28},{29,1},{... | collective-permute-start | bytes 1572872 | tf_op jit(solution)/shard_map/ppermute | solution.py:20
  100.7 27.1 %collective-permute-start.12 = (f32[1,2,256,256]{3,2,1,0:T(8,128)S(1)}, f32[1,2,256,256]{3,2,1,0:T(8,128)S(1)}, u32[]{:S(2)}, u32[]{:S(2)}) collective-permute-start(f32[1,2,256,256]{3,2,1,0:T(8,128)S(1)} %get-tuple-element.52), channel_id=1, source_target_pairs={{28,0},{0,4},{4,8},{8,12},{12,16},{16,20},{20,24},{24,28},{29,1},{... | collective-permute-start | bytes 1572872 | tf_op jit(solution)/shard_map/ppermute | solution.py:20
  106.3 27.1 %collective-permute-start.14 = (f32[1,2,256,256]{3,2,1,0:T(8,128)S(1)}, f32[1,2,256,256]{3,2,1,0:T(8,128)S(1)}, u32[]{:S(2)}, u32[]{:S(2)}) collective-permute-start(f32[1,2,256,256]{3,2,1,0:T(8,128)S(1)} %add.7), channel_id=1, source_target_pairs={{28,0},{0,4},{4,8},{8,12},{12,16},{16,20},{20,24},{24,28},{29,1},{... | collective-permute-start | bytes 1572872 | tf_op jit(solution)/shard_map/ppermute | solution.py:20

commit v4 on v3

--- a/solution.py
+++ b/solution.py
@@ -233,6 +233,11 @@
             ]
 
 
+def pack_near_kernel(object_ref, start, out, sem):
+    del start
+    finish(run_copies([corner_copies(object_ref, out, sem, False)]))
+
+
 def pack_kernel(corners, object_ref, *rest):
     outs, sem = rest[:-1], rest[-1]
     copies = []
@@ -467,7 +472,16 @@
     slots = positions.shape[-2]
 
     rest = tile - length
-    (near0,) = pack(object_field, [(0, 0, 0, length, length)])
+    near0 = pl.pallas_call(
+        pack_near_kernel,
+        name="pack0",
+        out_shape=pltpu.VMEM((1, parts, length, length), jnp.float32),
+        in_specs=[hbm_space, vmem_space],
+        out_specs=vmem_space,
+        scratch_shapes=[pltpu.SemaphoreType.DMA],
+        input_output_aliases={1: 0},
+        compiler_params=pltpu.CompilerParams(vmem_limit_bytes=1024 * 1024),
+    )(in_hbm(object_field), in_vmem(jnp.zeros((1, parts, length, length), jnp.float32)))
     right0, far0, near1, far1, right1 = pack(
         object_field,
         [
@@ -511,7 +525,7 @@
     window, *others = state
     window = pl.pallas_call(
         load_kernel,
-        name="load_halo",
+        name="load",
         out_shape=state_types[0],
         in_specs=[any_space] * 3 + [vmem_space],
         out_specs=vmem_space,
@@ -531,7 +545,7 @@
     far0 = shifted(far0, "row", 1)
     own = pl.pallas_call(
         own_kernel,
-        name="own",
+        name="store",
         out_shape=jax.ShapeDtypeStruct(object_field.shape, jnp.float32),
         in_specs=[vmem_space],
         out_specs=any_space,
@@ -554,7 +568,7 @@
     )(in_hbm(result))
     return pl.pallas_call(
         last_kernel,
-        name="add_near0",
+        name="addn0",
         out_shape=jax.ShapeDtypeStruct(result.shape, jnp.float32),
         in_specs=[any_space, vmem_space, vmem_space],
         out_specs=any_space,

time: 135 us -> 135 us (level)
    pallas_call x3 -> x4, Pallas kernels: 4.13 us -> 5.21 us  [the longest x1 2 us: tile_gradient(): pl.pallas_call(own_kernel, name='store', out_shape=jax.ShapeDtypeStruct(o...]
    pallas_call x2 -> x1, Pallas kernels: 4.6 us -> 3.52 us  [pack(): pl.pallas_call(functools.partial(pack_kernel, [piece[:3] for piece in pie...]
where the time goes in v4:
time: 135 us; the launch traced here: 134 us
  waiting for transfers between devices  79.1 us (59%)
  Pallas kernels  37.1 us (27%)
  starting transfers between devices  15 us (11%)
  local copies, waits for them, and re-layouts  2.02 us (1%)
    ppermute x15, waiting for transfers between devices, shifted(): return lax.ppermute(block, axis, route)  79.1 us
    pallas_call x4, Pallas kernels, slots_call(): pl.pallas_call(body, out_shape=[pltpu.VMEM(s, jnp.float32) for s in out_s...  19.3 us
    ppermute x15, starting transfers between devices, shifted(): return lax.ppermute(block, axis, route)  15 us
    pallas_call x4, Pallas kernels, add_piece(): pl.pallas_call(functools.partial(add_kernel, plane, column), out_shape=ja...  7.98 us
    pallas_call x1, Pallas kernels, pack(): pl.pallas_call(functools.partial(pack_kernel, [piece[:3] for piece in pie...  3.52 us
  transfers between devices with their start and end apart: 15, of which 8 were waited for; matrix products, arithmetic and copies ran while one was open for 1% of the time, Pallas kernels for 20%

profile of v4, /device:TPU:0, one launch (start us, length us, event | category | flops | bytes accessed | tf_op | source)
XLA Modules:
  0.0 134.5 jit_solution(13702248265707437026)
XLA Ops:
  0.1 1.1 pack0.1
  1.2 6.1 %collective-permute-start.4 = (f32[1,2,256,256]{3,2,1,0:T(8,128)S(1)}, f32[1,2,256,256]{3,2,1,0:T(8,128)}, u32[]{:S(2)}, u32[]{:S(2)}) collective-permute-start(f32[1,2,256,256]{3,2,1,0:T(8,128)S(1)} %pack0.1), channel_id=1, source_target_pairs={{4,0},{8,4},{12,8},{16,12},{20,16},{24,20},{28,24},{0,28},{5,1},{9... | collective-permute-start | bytes 1572872 | tf_op jit(solution)/shard_map/ppermute | solution.py:20
  7.3 3.5 %shard_map.82 = (f32[1,2,512,256]{3,2,1,0:T(8,128)}, f32[1,2,256,256]{3,2,1,0:T(8,128)S(1)}, f32[1,2,256,256]{3,2,1,0:T(8,128)S(1)}, f32[1,2,256,256]{3,2,1,0:T(8,128)}, f32[1,2,512,256]{3,2,1,0:T(8,128)}) custom-call(f32[2,2,512,512]{3,2,1,0:T(8,128)} %object_ref.5), custom_call_target="tpu_custom_call" | custom-call | tf_op jit(solution)/shard_map/pallas_call | solution.py:256
  10.8 0.7 collective-permute-start.7
  11.5 0.7 collective-permute-start.1
  12.2 0.5 collective-permute-start.3
  12.7 1.4 %collective-permute-start.5 = (f32[1,2,256,256]{3,2,1,0:T(8,128)S(1)}, f32[1,2,256,256]{3,2,1,0:T(8,128)S(1)}, u32[]{:S(2)}, u32[]{:S(2)}) collective-permute-start(f32[1,2,256,256]{3,2,1,0:T(8,128)S(1)} %get-tuple-element.33), channel_id=1, source_target_pairs={{4,0},{8,4},{12,8},{16,12},{20,16},{24,20},{28,24},{0,28},{5,1},{9... | collective-permute-start | bytes 1572872 | tf_op jit(solution)/shard_map/ppermute | solution.py:20
  14.1 5.5 %collective-permute-done.4.near_ref = f32[1,2,256,256]{3,2,1,0:T(8,128)} collective-permute-done((f32[1,2,256,256]{3,2,1,0:T(8,128)S(1)}, f32[1,2,256,256]{3,2,1,0:T(8,128)}, u32[]{:S(2)}, u32[]{:S(2)}) %collective-permute-start.4) | collective-permute-done | bytes 524320 | tf_op jit(solution)/shard_map/ppermute | solution.py:20
  19.6 11.2 %collective-permute-done.1.near_ref = f32[1,2,256,256]{3,2,1,0:T(8,128)} collective-permute-done((f32[1,2,256,256]{3,2,1,0:T(8,128)S(1)}, f32[1,2,256,256]{3,2,1,0:T(8,128)}, u32[]{:S(2)}, u32[]{:S(2)}) %collective-permute-start.1) | collective-permute-done | bytes 524320 | tf_op jit(solution)/shard_map/ppermute | solution.py:20
  30.8 10.1 %collective-permute-done.5.far_ref = f32[1,2,256,256]{3,2,1,0:T(8,128)S(1)} collective-permute-done((f32[1,2,256,256]{3,2,1,0:T(8,128)S(1)}, f32[1,2,256,256]{3,2,1,0:T(8,128)S(1)}, u32[]{:S(2)}, u32[]{:S(2)}) %collective-permute-start.5) | collective-permute-done | bytes 524320 | tf_op jit(solution)/shard_map/ppermute | solution.py:20
  40.9 0.8 copy-done.4
  41.7 5.2 %collective-permute-start = (f32[1,2,256,256]{3,2,1,0:T(8,128)}, f32[1,2,256,256]{3,2,1,0:T(8,128)}, u32[]{:S(2)}, u32[]{:S(2)}) collective-permute-start(f32[1,2,256,256]{3,2,1,0:T(8,128)} %get-tuple-element.30), channel_id=1, source_target_pairs={{4,0},{8,4},{12,8},{16,12},{20,16},{24,20},{28,24},{0,28},{5,1},{9... | collective-permute-start | bytes 1572872 | tf_op jit(solution)/shard_map/ppermute | solution.py:20
  47.6 0.1 copy.29
  47.7 0.1 reshape.6.places
  47.8 0.9 cosine_bitcast_fusion
  48.8 7.3 %shard_map.83 = (f32[2,2,6,768,128]{4,3,2,1,0:T(8,128)S(1)}, f32[2,2,6,768,128]{4,3,2,1,0:T(8,128)S(1)}, f32[4,2,256,256]{3,2,1,0:T(8,128)S(1)}, bf16[4,512,256]{2,1,0:T(8,128)(2,1)S(1)}) custom-call(s32[8]{0:T(128)S(1)} %reshape.6.places, s32[1]{0:T(128)} %bitcast.6.count, f32[2,2,512,512]{3,2,1,0:T(8,128)} %object_ref.5, f32[2,256,256]{2,1,0:T(8,128)S(1)} %copy-done, ...), custom_call_target="tpu_custom_call" | custom-call | tf_op jit(solution)/shard_map/pallas_call | solution.py:452
  56.2 4.0 %shard_map.84 = (f32[2,2,6,768,128]{4,3,2,1,0:T(8,128)S(1)}, f32[2,2,6,768,128]{4,3,2,1,0:T(8,128)S(1)}, f32[4,2,256,256]{3,2,1,0:T(8,128)S(1)}, bf16[4,512,256]{2,1,0:T(8,128)(2,1)S(1)}) custom-call(s32[8]{0:T(128)S(1)} %reshape.6.places, s32[1]{0:T(128)} %bitcast.7.count, ...), custom_call_target="tpu_custom_call", output_to_operand_aliasing={{0}: (11, {}), {1}: (12, {}), {2}: (13, {}), {3}: (14, {})} | custom-call | tf_op jit(solution)/shard_map/pallas_call | solution.py:452
  60.2 1.3 load.1.rest_5_
  61.5 3.9 %shard_map.85 = (f32[1,2,256,256]{3,2,1,0:T(8,128)S(1)}, f32[1,2,256,256]{3,2,1,0:T(8,128)S(1)}, f32[1,2,256,256]{3,2,1,0:T(8,128)S(1)}, f32[2,2,6,768,128]{4,3,...) custom-call(s32[8]{0:T(128)S(1)} %reshape.6.places, ...), custom_call_target="tpu_custom_call", output_to_operand_aliasing={{3}: (8, {}), {4}: (9, {}), {5}: (10, {}), {6}: (11, {})} | custom-call | tf_op jit(solution)/shard_map/pallas_call | solution.py:452
  65.4 4.1 %shard_map.86 = (f32[1,2,256,256]{3,2,1,0:T(8,128)S(1)}, f32[1,2,256,256]{3,2,1,0:T(8,128)S(1)}, f32[1,2,256,256]{3,2,1,0:T(8,128)S(1)}, f32[2,2,512,256]{3,2,1,...) custom-call(s32[8]{0:T(128)S(1)} %reshape.6.places, ...), custom_call_target="tpu_custom_call", output_to_operand_aliasing={{4}: (7, {}), {5}: (8, {}), {6}: (9, {}), {7}: (10, {})} | custom-call | tf_op jit(solution)/shard_map/pallas_call | solution.py:452
  69.8 30.9 %collective-permute-done.9 = f32[1,2,256,256]{3,2,1,0:T(8,128)S(1)} collective-permute-done((f32[1,2,256,256]{3,2,1,0:T(8,128)S(1)}, f32[1,2,256,256]{3,2,1,0:T(8,128)S(1)}, u32[]{:S(2)}, u32[]{:S(2)}) %collective-permute-start.9) | collective-permute-done | bytes 524320 | tf_op jit(solution)/shard_map/ppermute | solution.py:20
  100.8 5.4 %collective-permute-done.13 = f32[1,2,256,256]{3,2,1,0:T(8,128)S(1)} collective-permute-done((f32[1,2,256,256]{3,2,1,0:T(8,128)S(1)}, f32[1,2,256,256]{3,2,1,0:T(8,128)S(1)}, u32[]{:S(2)}, u32[]{:S(2)}) %collective-permute-start.13) | collective-permute-done | bytes 524320 | tf_op jit(solution)/shard_map/ppermute | solution.py:20
  106.4 2.0 %store.1.gradient_in = f32[2,2,512,512]{3,2,1,0:T(8,128)} custom-call(f32[2,2,6,768,128]{4,3,2,1,0:T(8,128)S(1)} %get-tuple-element.47.gradient), custom_call_target="tpu_custom_call" | custom-call | tf_op jit(solution)/shard_map/store/pallas_call | solution.py:546
  108.4 1.8 %shard_map.87.gradient_in = f32[2,2,512,512]{3,2,1,0:T(8,128)} custom-call(f32[2,2,512,512]{3,2,1,0:T(8,128)} %store.1.gradient_in, f32[1,2,256,256]{3,2,1,0:T(8,128)S(1)} %collective-permute-done.8.piece_ref), custom_call_target="tpu_custom_call", output_to_operand_aliasing={{}: (0, {})} | custom-call | tf_op jit(solution)/shard_map/pallas_call | solution.py:397
  110.2 8.0 %collective-permute-done.10.piece_ref = f32[1,2,256,256]{3,2,1,0:T(8,128)S(1)} collective-permute-done((f32[1,2,256,256]{3,2,1,0:T(8,128)S(1)}, f32[1,2,256,256]{3,2,1,0:T(8,128)S(1)}, u32[]{:S(2)}, u32[]{:S(2)}) %collective-permute-start.10) | collective-permute-done | bytes 524320 | tf_op jit(solution)/shard_map/ppermute | solution.py:20
  118.2 1.8 %shard_map.88.gradient_in = f32[2,2,512,512]{3,2,1,0:T(8,128)} custom-call(f32[2,2,512,512]{3,2,1,0:T(8,128)} %shard_map.87.gradient_in, f32[1,2,256,256]{3,2,1,0:T(8,128)S(1)} %collective-permute-done.10.piece_ref), custom_call_target="tpu_custom_call", output_to_operand_aliasing={{}: (0, {})} | custom-call | tf_op jit(solution)/shard_map/pallas_call | solution.py:397
  120.1 2.5 %shard_map.89.gradient_in = f32[2,2,512,512]{3,2,1,0:T(8,128)} custom-call(f32[2,2,512,512]{3,2,1,0:T(8,128)} %shard_map.88.gradient_in, f32[2,2,512,256]{3,2,1,0:T(8,128)S(1)} %collective-permute-done.11.piece_ref), custom_call_target="tpu_custom_call", output_to_operand_aliasing={{}: (0, {})} | custom-call | tf_op jit(solution)/shard_map/pallas_call | solution.py:397
  122.6 5.2 %collective-permute-done.12.piece_ref = f32[1,2,256,256]{3,2,1,0:T(8,128)S(1)} collective-permute-done((f32[1,2,256,256]{3,2,1,0:T(8,128)S(1)}, f32[1,2,256,256]{3,2,1,0:T(8,128)S(1)}, u32[]{:S(2)}, u32[]{:S(2)}) %collective-permute-start.12) | collective-permute-done | bytes 524320 | tf_op jit(solution)/shard_map/ppermute | solution.py:20
  127.9 1.8 %shard_map.90.gradient.gradient_in = f32[2,2,512,512]{3,2,1,0:T(8,128)} custom-call(f32[2,2,512,512]{3,2,1,0:T(8,128)} %shard_map.89.gradient_in, f32[1,2,256,256]{3,2,1,0:T(8,128)S(1)} %collective-permute-done.12.piece_ref), custom_call_target="tpu_custom_call", output_to_operand_aliasing={{}: (0, {})} | custom-call | tf_op jit(solution)/shard_map/pallas_call | solution.py:397
  129.7 1.0 hold.1.held
  130.7 2.7 %collective-permute-done.14.piece = f32[1,2,256,256]{3,2,1,0:T(8,128)S(1)} collective-permute-done((f32[1,2,256,256]{3,2,1,0:T(8,128)S(1)}, f32[1,2,256,256]{3,2,1,0:T(8,128)S(1)}, u32[]{:S(2)}, u32[]{:S(2)}) %collective-permute-start.14) | collective-permute-done | bytes 524320 | tf_op jit(solution)/shard_map/ppermute | solution.py:20
  133.5 0.8 addn0.1
  (35 shorter events, 0.7 us)
Async XLA Ops:
  0.0 47.5 %copy-start.7 = (s32[1,1,4,2]{2,3,1,0:T(2,128)S(1)}, s32[1,1,4,2]{2,3,1,0:T(2,128)}, u32[]{:S(2)}) copy-start(s32[1,1,4,2]{2,3,1,0:T(2,128)} %param.11) | copy-start | bytes 100
  0.1 47.7 %copy-start.6 = (f32[256,256]{1,0:T(8,128)S(1)}, f32[256,256]{1,0:T(8,128)}, u32[]{:S(2)}) copy-start(f32[256,256]{1,0:T(8,128)} %param.10) | copy-start | bytes 786436
  1.2 47.6 %copy-start = (f32[2,256,256]{2,1,0:T(8,128)S(1)}, f32[2,256,256]{2,1,0:T(8,128)}, u32[]{:S(2)}) copy-start(f32[2,256,256]{2,1,0:T(8,128)} %rest_0_.7) | copy-start | bytes 1572868
  1.2 47.6 %copy-start.1 = (bf16[1,1,4,256,256]{4,3,2,1,0:T(8,128)(2,1)S(1)}, bf16[1,1,4,256,256]{4,3,2,1,0:T(8,128)(2,1)}, u32[]{:S(2)}) copy-start(bf16[1,1,4,256,256]{4,3,2,1,0:T(8,128)(2,1)} %param.13) | copy-start | bytes 1572868
  1.2 47.6 %copy-start.2 = (bf16[512,512]{1,0:T(8,128)(2,1)S(1)}, bf16[512,512]{1,0:T(8,128)(2,1)}, u32[]{:S(2)}) copy-start(bf16[512,512]{1,0:T(8,128)(2,1)} %constant.7.clone.rest_4_) | copy-start | bytes 1572868
  1.2 47.6 %copy-start.3 = (bf16[512,512]{1,0:T(8,128)(2,1)S(1)}, bf16[512,512]{1,0:T(8,128)(2,1)}, u32[]{:S(2)}) copy-start(bf16[512,512]{1,0:T(8,128)(2,1)} %constant.6.clone.rest_3_) | copy-start | bytes 1572868
  1.2 18.4 %collective-permute-start.4 = (f32[1,2,256,256]{3,2,1,0:T(8,128)S(1)}, f32[1,2,256,256]{3,2,1,0:T(8,128)}, u32[]{:S(2)}, u32[]{:S(2)}) collective-permute-start(f32[1,2,256,256]{3,2,1,0:T(8,128)S(1)} %pack0.1), channel_id=1, source_target_pairs={{4,0},{8,4},{12,8},{16,12},{20,16},{24,20},{28,24},{0,28},{5,1},{9... | collective-permute-start | bytes 1572872 | tf_op jit(solution)/shard_map/ppermute | solution.py:20
  10.8 45.4 %collective-permute-start.7 = (f32[1,2,512,256]{3,2,1,0:T(8,128)}, f32[1,2,512,256]{3,2,1,0:T(8,128)}, u32[]{:S(2)}, u32[]{:S(2)}) collective-permute-start(f32[1,2,512,256]{3,2,1,0:T(8,128)} %get-tuple-element.34), channel_id=1, source_target_pairs={{1,0},{2,1},{3,2},{0,3},{5,4},{6,5},{7,6},{4,7},{9,8},{10,9},{11,1... | collective-permute-start | bytes 3145736 | tf_op jit(solution)/shard_map/ppermute | solution.py:20
  11.5 19.3 %collective-permute-start.1 = (f32[1,2,256,256]{3,2,1,0:T(8,128)S(1)}, f32[1,2,256,256]{3,2,1,0:T(8,128)}, u32[]{:S(2)}, u32[]{:S(2)}) collective-permute-start(f32[1,2,256,256]{3,2,1,0:T(8,128)S(1)} %get-tuple-element.31), channel_id=1, source_target_pairs={{4,0},{8,4},{12,8},{16,12},{20,16},{24,20},{28,24},{0,28},{5,1},{9... | collective-permute-start | bytes 1572872 | tf_op jit(solution)/shard_map/ppermute | solution.py:20
  12.2 48.0 %collective-permute-start.3 = (f32[1,2,512,256]{3,2,1,0:T(8,128)}, f32[1,2,512,256]{3,2,1,0:T(8,128)S(1)}, u32[]{:S(2)}, u32[]{:S(2)}) collective-permute-start(f32[1,2,512,256]{3,2,1,0:T(8,128)} %get-tuple-element.32), channel_id=1, source_target_pairs={{1,0},{2,1},{3,2},{0,3},{5,4},{6,5},{7,6},{4,7},{9,8},{10,9},{11,1... | collective-permute-start | bytes 3145736 | tf_op jit(solution)/shard_map/ppermute | solution.py:20
  12.7 28.2 %collective-permute-start.5 = (f32[1,2,256,256]{3,2,1,0:T(8,128)S(1)}, f32[1,2,256,256]{3,2,1,0:T(8,128)S(1)}, u32[]{:S(2)}, u32[]{:S(2)}) collective-permute-start(f32[1,2,256,256]{3,2,1,0:T(8,128)S(1)} %get-tuple-element.33), channel_id=1, source_target_pairs={{4,0},{8,4},{12,8},{16,12},{20,16},{24,20},{28,24},{0,28},{5,1},{9... | collective-permute-start | bytes 1572872 | tf_op jit(solution)/shard_map/ppermute | solution.py:20
  19.6 36.6 %collective-permute-start.6 = (f32[1,2,256,256]{3,2,1,0:T(8,128)}, f32[1,2,256,256]{3,2,1,0:T(8,128)}, u32[]{:S(2)}, u32[]{:S(2)}) collective-permute-start(f32[1,2,256,256]{3,2,1,0:T(8,128)} %collective-permute-done.4.near_ref), channel_id=1, source_target_pairs={{1,0},{2,1},{3,2},{0,3},{5,4},{6,5},{7,6},{4,7},{9,8},{10,9},{11,1... | collective-permute-start | bytes 1572872 | tf_op jit(solution)/shard_map/ppermute | solution.py:20
  30.8 29.4 %collective-permute-start.2 = (f32[1,2,256,256]{3,2,1,0:T(8,128)}, f32[1,2,256,256]{3,2,1,0:T(8,128)}, u32[]{:S(2)}, u32[]{:S(2)}) collective-permute-start(f32[1,2,256,256]{3,2,1,0:T(8,128)} %collective-permute-done.1.near_ref), channel_id=1, source_target_pairs={{1,0},{2,1},{3,2},{0,3},{5,4},{6,5},{7,6},{4,7},{9,8},{10,9},{11,1... | collective-permute-start | bytes 1572872 | tf_op jit(solution)/shard_map/ppermute | solution.py:20
  40.9 0.8 copy-start.4
  41.7 19.8 %collective-permute-start = (f32[1,2,256,256]{3,2,1,0:T(8,128)}, f32[1,2,256,256]{3,2,1,0:T(8,128)}, u32[]{:S(2)}, u32[]{:S(2)}) collective-permute-start(f32[1,2,256,256]{3,2,1,0:T(8,128)} %get-tuple-element.30), channel_id=1, source_target_pairs={{4,0},{8,4},{12,8},{16,12},{20,16},{24,20},{28,24},{0,28},{5,1},{9... | collective-permute-start | bytes 1572872 | tf_op jit(solution)/shard_map/ppermute | solution.py:20
  47.8 8.4 %copy-start.5 = (f32[1,2,256,256]{3,2,1,0:T(8,128)S(1)}, f32[1,2,256,256]{3,2,1,0:T(8,128)}, u32[]{:S(2)}) copy-start(f32[1,2,256,256]{3,2,1,0:T(8,128)} %copy-done.4) | copy-start | bytes 1572868
  69.5 50.6 %collective-permute-start.11 = (f32[2,2,512,256]{3,2,1,0:T(8,128)S(1)}, f32[2,2,512,256]{3,2,1,0:T(8,128)S(1)}, u32[]{:S(2)}, u32[]{:S(2)}) collective-permute-start(f32[2,2,512,256]{3,2,1,0:T(8,128)S(1)} %get-tuple-element.51), channel_id=1, source_target_pairs={{3,0},{0,1},{1,2},{2,3},{7,4},{4,5},{5,6},{6,7},{11,8},{8,9},{9,10... | collective-permute-start | bytes 6291464 | tf_op jit(solution)/shard_map/ppermute | solution.py:20
  69.6 31.1 %collective-permute-start.9 = (f32[1,2,256,256]{3,2,1,0:T(8,128)S(1)}, f32[1,2,256,256]{3,2,1,0:T(8,128)S(1)}, u32[]{:S(2)}, u32[]{:S(2)}) collective-permute-start(f32[1,2,256,256]{3,2,1,0:T(8,128)S(1)} %get-tuple-element.50), channel_id=1, source_target_pairs={{3,0},{0,1},{1,2},{2,3},{7,4},{4,5},{5,6},{6,7},{11,8},{8,9},{9,10... | collective-permute-start | bytes 1572872 | tf_op jit(solution)/shard_map/ppermute | solution.py:20
  69.6 36.6 %collective-permute-start.13 = (f32[1,2,256,256]{3,2,1,0:T(8,128)S(1)}, f32[1,2,256,256]{3,2,1,0:T(8,128)S(1)}, u32[]{:S(2)}, u32[]{:S(2)}) collective-permute-start(f32[1,2,256,256]{3,2,1,0:T(8,128)S(1)} %get-tuple-element.54), channel_id=1, source_target_pairs={{3,0},{0,1},{1,2},{2,3},{7,4},{4,5},{5,6},{6,7},{11,8},{8,9},{9,10... | collective-permute-start | bytes 1572872 | tf_op jit(solution)/shard_map/ppermute | solution.py:20
  69.7 38.7 %collective-permute-start.8 = (f32[1,2,256,256]{3,2,1,0:T(8,128)S(1)}, f32[1,2,256,256]{3,2,1,0:T(8,128)S(1)}, u32[]{:S(2)}, u32[]{:S(2)}) collective-permute-start(f32[1,2,256,256]{3,2,1,0:T(8,128)S(1)} %get-tuple-element.48), channel_id=1, source_target_pairs={{28,0},{0,4},{4,8},{8,12},{12,16},{16,20},{20,24},{24,28},{29,1},{... | collective-permute-start | bytes 1572872 | tf_op jit(solution)/shard_map/ppermute | solution.py:20
  100.7 17.5 %collective-permute-start.10 = (f32[1,2,256,256]{3,2,1,0:T(8,128)S(1)}, f32[1,2,256,256]{3,2,1,0:T(8,128)S(1)}, u32[]{:S(2)}, u32[]{:S(2)}) collective-permute-start(f32[1,2,256,256]{3,2,1,0:T(8,128)S(1)} %add.6), channel_id=1, source_target_pairs={{28,0},{0,4},{4,8},{8,12},{12,16},{16,20},{20,24},{24,28},{29,1},{... | collective-permute-start | bytes 1572872 | tf_op jit(solution)/shard_map/ppermute | solution.py:20
  100.8 27.1 %collective-permute-start.12 = (f32[1,2,256,256]{3,2,1,0:T(8,128)S(1)}, f32[1,2,256,256]{3,2,1,0:T(8,128)S(1)}, u32[]{:S(2)}, u32[]{:S(2)}) collective-permute-start(f32[1,2,256,256]{3,2,1,0:T(8,128)S(1)} %get-tuple-element.52), channel_id=1, source_target_pairs={{28,0},{0,4},{4,8},{8,12},{12,16},{16,20},{20,24},{24,28},{29,1},{... | collective-permute-start | bytes 1572872 | tf_op jit(solution)/shard_map/ppermute | solution.py:20
  106.3 27.2 %collective-permute-start.14 = (f32[1,2,256,256]{3,2,1,0:T(8,128)S(1)}, f32[1,2,256,256]{3,2,1,0:T(8,128)S(1)}, u32[]{:S(2)}, u32[]{:S(2)}) collective-permute-start(f32[1,2,256,256]{3,2,1,0:T(8,128)S(1)} %add.7), channel_id=1, source_target_pairs={{28,0},{0,4},{4,8},{8,12},{12,16},{16,20},{20,24},{24,28},{29,1},{... | collective-permute-start | bytes 1572872 | tf_op jit(solution)/shard_map/ppermute | solution.py:20

commit v5 on v4

--- a/solution.py
+++ b/solution.py
@@ -174,12 +174,11 @@
         accumulate(gradient, 0, patch_spot(places, slot), grad, length)
 
 
-def visit_slots(places, count, slots, limit, inside, todo, exact, visit):
+def visit_slots(places, count, slots, wanted, todo, threes, visit):
     def pick(slot, found):
-        within = jnp.logical_and(places[2 * slot] <= limit, places[2 * slot + 1] <= limit)
-        chosen = slot < count[0]
-        if inside is not None:
-            chosen = jnp.logical_and(chosen, within == inside)
+        chosen = jnp.logical_and(
+            slot < count[0], wanted(places[2 * slot], places[2 * slot + 1])
+        )
 
         @pl.when(chosen)
         def _():
@@ -188,24 +187,41 @@
         return found + chosen.astype(jnp.int32)
 
     found = lax.fori_loop(0, slots, pick, jnp.int32(0))
-    if exact:
-        for size in range(1, slots + 1):
-
-            @pl.when(found == size)
-            def _():
-                visit([todo[i] for i in range(size)])
-
-        return
+    odd = lax.rem(found, 2) == 1
+    three = jnp.logical_and(odd, found >= 3) if threes else jnp.bool_(False)
 
     def pair(index, carry):
         visit([todo[2 * index], todo[2 * index + 1]])
         return carry
 
-    lax.fori_loop(0, found // 2, pair, 0)
-
-    @pl.when(lax.rem(found, 2) == 1)
+    lax.fori_loop(0, (found - 3 * three.astype(jnp.int32)) // 2, pair, 0)
+    if threes:
+
+        @pl.when(three)
+        def _():
+            visit([todo[found - 3], todo[found - 2], todo[found - 1]])
+
+    @pl.when(jnp.logical_and(odd, jnp.logical_not(three)))
     def _():
         visit([todo[found - 1]])
+
+
+def slot_groups(tile, length, split):
+    limit = tile - length
+
+    def inside(row, column):
+        return jnp.logical_and(row <= limit, column <= limit)
+
+    def outside(row, column):
+        return jnp.logical_not(inside(row, column))
+
+    def upper(row, column):
+        return jnp.logical_and(outside(row, column), row <= limit + split)
+
+    def lower(row, column):
+        return row > limit + split
+
+    return inside, outside, upper, lower
 
 
 def sizes(tile, length):
@@ -279,9 +295,8 @@
         spread_slots(places, window, constants, spreads, slots)
         back_slots(places, window, gradient, constants, spreads, inners, slots)
 
-    visit_slots(
-        places, count, inners.shape[0], tile - length, True, todo, False, visit
-    )
+    inside, _, _, _ = slot_groups(tile, length, length // 2)
+    visit_slots(places, count, inners.shape[0], inside, todo, False, visit)
 
 
 def spread_kernel(places, count, near_ref, far_ref, corner_ref, right_ref, *rest):
@@ -303,25 +318,32 @@
     def visit(slots):
         spread_slots(places, window, constants, spreads, slots)
 
-    visit_slots(
-        places, count, inners.shape[0], tile - length, False, todo, False, visit
-    )
-
-
-def load_kernel(near_ref, corner_ref, right_ref, window_in, window, sem):
-    del window_in
-    length = near_ref.shape[3]
+    _, outside, _, _ = slot_groups(tile, length, length // 2)
+    visit_slots(places, count, inners.shape[0], outside, todo, False, visit)
+
+
+def upper_kernel(places, count, near_ref, corner_ref, right_ref, far_ref, *rest):
+    constants, (window, gradient, spreads, inners, todo, sem) = rest[:5], rest[9:]
+    length = constants[0].shape[-1]
     tile = right_ref.shape[2]
-    _, near, _, past = sizes(tile, length)
+    split = far_ref.shape[2]
+    _, near, far, past = sizes(tile, length)
     finish(
         run_copies(
             [
                 strip_copies(near_ref, near, tile, window, 1, sem, False),
                 strip_copies(corner_ref, past, tile, window, 1, sem, False),
                 strip_copies(right_ref, past, 0, window, 1, sem, False),
+                strip_copies(far_ref, far, tile, window, 1, sem, False),
             ]
         )
     )
+
+    def visit(slots):
+        back_slots(places, window, gradient, constants, spreads, inners, slots)
+
+    _, _, upper, _ = slot_groups(tile, length, split)
+    visit_slots(places, count, inners.shape[0], upper, todo, False, visit)
 
 
 def back_kernel(places, count, far_ref, *rest):
@@ -330,14 +352,14 @@
     length = constants[0].shape[-1]
     tile = length + far_ref.shape[3]
     _, near, far, past = sizes(tile, length)
-    into_strips(far_ref, far, tile, window, 1)
+    split = length - far_ref.shape[2]
+    into_strips(far_ref, far, tile + split, window, 1)
 
     def visit(slots):
         back_slots(places, window, gradient, constants, spreads, inners, slots)
 
-    visit_slots(
-        places, count, inners.shape[0], tile - length, False, todo, True, visit
-    )
+    _, _, _, lower = slot_groups(tile, length, split)
+    visit_slots(places, count, inners.shape[0], lower, todo, True, visit)
     from_strips(corner_out, past, tile, gradient, 1)
     from_strips(far_out, far, tile, gradient, 1)
     from_strips(near_out, near, tile, gradient, 1)
@@ -354,9 +376,10 @@
     def visit(slots):
         first_slots(places, gradient, constants, inners, slots)
 
-    visit_slots(
-        places, count, inners.shape[0], tile - length, None, todo, False, visit
-    )
+    def all_slots(row, column):
+        return row >= 0
+
+    visit_slots(places, count, inners.shape[0], all_slots, todo, False, visit)
     from_strips(corner_out, past, tile, gradient, 0)
     from_strips(far_out, far, tile, gradient, 0)
     from_strips(near_out, near, tile, gradient, 0)
@@ -482,21 +505,24 @@
         input_output_aliases={1: 0},
         compiler_params=pltpu.CompilerParams(vmem_limit_bytes=1024 * 1024),
     )(in_hbm(object_field), in_vmem(jnp.zeros((1, parts, length, length), jnp.float32)))
-    right0, far0, near1, far1, right1 = pack(
+    split = length // 2
+    right0, near1, far0, upper1, lower1, right1 = pack(
         object_field,
         [
             (0, 0, 0, tile, length),
+            (1, 0, 0, length, length),
             (0, 0, length, length, rest),
-            (1, 0, 0, length, length),
-            (1, 0, length, length, rest),
+            (1, 0, length, split, rest),
+            (1, split, length, length - split, rest),
             (1, 0, 0, tile, length),
         ],
     )
     near0 = shifted(near0, "row", -1)
     right0 = shifted(right0, "col", -1)
+    near1 = shifted(near1, "row", -1)
     far0 = shifted(far0, "row", -1)
-    near1 = shifted(near1, "row", -1)
-    far1 = shifted(far1, "row", -1)
+    upper1 = shifted(upper1, "row", -1)
+    lower1 = shifted(lower1, "row", -1)
     right1 = shifted(right1, "col", -1)
     corner0 = shifted(near0, "col", -1)
     corner1 = shifted(near1, "col", -1)
@@ -522,18 +548,8 @@
 
     state = call(own_slots_kernel, (in_hbm(object_field),), (), ())
     state = call(spread_kernel, (near0, far0, corner0, right0), state, ())
-    window, *others = state
-    window = pl.pallas_call(
-        load_kernel,
-        name="load",
-        out_shape=state_types[0],
-        in_specs=[any_space] * 3 + [vmem_space],
-        out_specs=vmem_space,
-        scratch_shapes=[pltpu.SemaphoreType.DMA],
-        input_output_aliases={3: 0},
-        compiler_params=pltpu.CompilerParams(vmem_limit_bytes=4 * 1024 * 1024),
-    )(near1, corner1, right1, in_vmem(window))
-    near1, far1, corner1, *state = call(back_kernel, (far1,), (window, *others), piece_shapes)
+    state = call(upper_kernel, (near1, corner1, right1, upper1), state, ())
+    near1, far1, corner1, *state = call(back_kernel, (lower1,), state, piece_shapes)
     corner1 = shifted(corner1, "col", 1)
     far1 = shifted(far1, "row", 1)
     near0, far0, corner0, right, window, gradient, *_ = call(

time: 135 us -> 135 us (level)
  waiting for transfers between devices: 79.1 us -> 76 us
  starting transfers between devices: 15 us -> 17.7 us
    ppermute x15 -> x16, waiting for transfers between devices: 79.1 us -> 76 us  [shifted(): return lax.ppermute(block, axis, route)]
    ppermute x15 -> x16, starting transfers between devices: 15 us -> 17.7 us  [shifted(): return lax.ppermute(block, axis, route)]
    pallas_call x4 -> x5, Pallas kernels: 19.3 us -> 20.3 us  [slots_call(): pl.pallas_call(body, out_shape=[pltpu.VMEM(s, jnp.float32) for s in out_s...]
  transfers between devices with their start and end apart: 15 -> 16, of which waited for: 8 -> 8; matrix products, arithmetic and copies ran while one was open for 1% -> 2% of each run, Pallas kernels for 20% -> 22%
where the time goes in v5:
time: 135 us
  waiting for transfers between devices  76 us (56%)
  Pallas kernels  36.7 us (27%)
  starting transfers between devices  17.7 us (13%)
  local copies, waits for them, and re-layouts  2.82 us (2%)
    ppermute x16, waiting for transfers between devices, shifted(): return lax.ppermute(block, axis, route)  76 us
    pallas_call x5, Pallas kernels, slots_call(): pl.pallas_call(body, out_shape=[pltpu.VMEM(s, jnp.float32) for s in out_s...  20.3 us
    ppermute x16, starting transfers between devices, shifted(): return lax.ppermute(block, axis, route)  17.7 us
    pallas_call x4, Pallas kernels, add_piece(): pl.pallas_call(functools.partial(add_kernel, plane, column), out_shape=ja...  7.98 us
    pallas_call x1, Pallas kernels, pack(): pl.pallas_call(functools.partial(pack_kernel, [piece[:3] for piece in pie...  3.52 us
  transfers between devices with their start and end apart: 16, of which 8 were waited for; matrix products, arithmetic and copies ran while one was open for 2% of the time, Pallas kernels for 22%

profile of v5, /device:TPU:0, one launch (start us, length us, event | category | flops | bytes accessed | tf_op | source)
XLA Modules:
  0.0 134.5 jit_solution(3703082867500199090)
XLA Ops:
  0.1 1.0 pack0.1
  1.2 6.1 %collective-permute-start.5 = (f32[1,2,256,256]{3,2,1,0:T(8,128)S(1)}, f32[1,2,256,256]{3,2,1,0:T(8,128)}, u32[]{:S(2)}, u32[]{:S(2)}) collective-permute-start(f32[1,2,256,256]{3,2,1,0:T(8,128)S(1)} %pack0.1), channel_id=1, source_target_pairs={{4,0},{8,4},{12,8},{16,12},{20,16},{24,20},{28,24},{0,28},{5,1},{9... | collective-permute-start | bytes 1572872 | tf_op jit(solution)/shard_map/ppermute | solution.py:20
  7.2 3.5 %shard_map.82 = (f32[1,2,512,256]{3,2,1,0:T(8,128)}, f32[1,2,256,256]{3,2,1,0:T(8,128)S(1)}, f32[1,2,256,256]{3,2,1,0:T(8,128)}, f32[1,2,128,256]{3,2,1,0:T(8,12...) custom-call(f32[2,2,512,512]{3,2,1,0:T(8,128)} %object_ref.5), custom_call_target="tpu_custom_call" | custom-call | tf_op jit(solution)/shard_map/pallas_call | solution.py:272
  10.7 0.7 copy-done.4
  11.5 0.7 collective-permute-start.8
  12.1 0.7 collective-permute-start.1
  12.8 0.5 collective-permute-start.3
  13.4 1.4 %collective-permute-start.6 = (f32[1,2,256,256]{3,2,1,0:T(8,128)}, f32[1,2,256,256]{3,2,1,0:T(8,128)}, u32[]{:S(2)}, u32[]{:S(2)}) collective-permute-start(f32[1,2,256,256]{3,2,1,0:T(8,128)} %get-tuple-element.39), channel_id=1, source_target_pairs={{4,0},{8,4},{12,8},{16,12},{20,16},{24,20},{28,24},{0,28},{5,1},{9... | collective-permute-start | bytes 1572872 | tf_op jit(solution)/shard_map/ppermute | solution.py:20
  14.7 4.8 %collective-permute-done.5.near_ref = f32[1,2,256,256]{3,2,1,0:T(8,128)} collective-permute-done((f32[1,2,256,256]{3,2,1,0:T(8,128)S(1)}, f32[1,2,256,256]{3,2,1,0:T(8,128)}, u32[]{:S(2)}, u32[]{:S(2)}) %collective-permute-start.5) | collective-permute-done | bytes 524320 | tf_op jit(solution)/shard_map/ppermute | solution.py:20
  19.5 11.2 %collective-permute-done.1.near_ref = f32[1,2,256,256]{3,2,1,0:T(8,128)} collective-permute-done((f32[1,2,256,256]{3,2,1,0:T(8,128)S(1)}, f32[1,2,256,256]{3,2,1,0:T(8,128)}, u32[]{:S(2)}, u32[]{:S(2)}) %collective-permute-start.1) | collective-permute-done | bytes 524320 | tf_op jit(solution)/shard_map/ppermute | solution.py:20
  31.6 9.4 %collective-permute-done.6.far_ref = f32[1,2,256,256]{3,2,1,0:T(8,128)} collective-permute-done((f32[1,2,256,256]{3,2,1,0:T(8,128)}, f32[1,2,256,256]{3,2,1,0:T(8,128)}, u32[]{:S(2)}, u32[]{:S(2)}) %collective-permute-start.6) | collective-permute-done | bytes 524320 | tf_op jit(solution)/shard_map/ppermute | solution.py:20
  41.0 5.2 %collective-permute-start = (f32[1,2,128,256]{3,2,1,0:T(8,128)S(1)}, f32[1,2,128,256]{3,2,1,0:T(8,128)S(1)}, u32[]{:S(2)}, u32[]{:S(2)}) collective-permute-start(f32[1,2,128,256]{3,2,1,0:T(8,128)S(1)} %get-tuple-element.35), channel_id=1, source_target_pairs={{4,0},{8,4},{12,8},{16,12},{20,16},{24,20},{28,24},{0,28},{5,1},{9... | collective-permute-start | bytes 786440 | tf_op jit(solution)/shard_map/ppermute | solution.py:20
  46.2 1.9 %cosine_bitcast_fusion = (f32[1,256,256]{2,1,0:T(8,128)S(1)}, f32[1,256,256]{2,1,0:T(8,128)S(1)}) fusion(f32[256,256]{1,0:T(8,128)} %param.10), kind=kLoop, calls=%fused_computation.2 | loop fusion | bytes 786432 | tf_op jit(solution)/shard_map/stack | solution.py:530
  48.1 7.2 %shard_map.83 = (f32[2,2,6,768,128]{4,3,2,1,0:T(8,128)S(1)}, f32[2,2,6,768,128]{4,3,2,1,0:T(8,128)S(1)}, f32[4,2,256,256]{3,2,1,0:T(8,128)S(1)}, bf16[4,512,256]{2,1,0:T(8,128)(2,1)S(1)}) custom-call(s32[8]{0:T(128)S(1)} %reshape.6.places, s32[1]{0:T(128)} %bitcast.6.count, f32[2,2,512,512]{3,2,1,0:T(8,128)} %object_ref.5, f32[2,256,256]{2,1,0:T(8,128)S(1)} %copy-done, ...), custom_call_target="tpu_custom_call" | custom-call | tf_op jit(solution)/shard_map/pallas_call | solution.py:475
  55.3 4.2 %shard_map.84 = (f32[2,2,6,768,128]{4,3,2,1,0:T(8,128)S(1)}, f32[2,2,6,768,128]{4,3,2,1,0:T(8,128)S(1)}, f32[4,2,256,256]{3,2,1,0:T(8,128)S(1)}, bf16[4,512,256]{2,1,0:T(8,128)(2,1)S(1)}) custom-call(s32[8]{0:T(128)S(1)} %reshape.6.places, s32[1]{0:T(128)} %bitcast.7.count, ...), custom_call_target="tpu_custom_call", output_to_operand_aliasing={{0}: (11, {}), {1}: (12, {}), {2}: (13, {}), {3}: (14, {})} | custom-call | tf_op jit(solution)/shard_map/pallas_call | solution.py:475
  59.5 4.1 %shard_map.85 = (f32[2,2,6,768,128]{4,3,2,1,0:T(8,128)S(1)}, f32[2,2,6,768,128]{4,3,2,1,0:T(8,128)S(1)}, f32[4,2,256,256]{3,2,1,0:T(8,128)S(1)}, bf16[4,512,256]{2,1,0:T(8,128)(2,1)S(1)}) custom-call(s32[8]{0:T(128)S(1)} %reshape.6.places, s32[1]{0:T(128)} %bitcast.8.count, ...), custom_call_target="tpu_custom_call", output_to_operand_aliasing={{0}: (11, {}), {1}: (12, {}), {2}: (13, {}), {3}: (14, {})} | custom-call | tf_op jit(solution)/shard_map/pallas_call | solution.py:475
  63.7 0.8 shard_map.86
  64.5 4.1 %shard_map.87 = (f32[1,2,256,256]{3,2,1,0:T(8,128)S(1)}, f32[1,2,256,256]{3,2,1,0:T(8,128)S(1)}, f32[1,2,256,256]{3,2,1,0:T(8,128)S(1)}, f32[2,2,512,256]{3,2,1,...) custom-call(s32[8]{0:T(128)S(1)} %reshape.6.places, ...), custom_call_target="tpu_custom_call", output_to_operand_aliasing={{4}: (7, {}), {5}: (8, {}), {6}: (9, {}), {7}: (10, {})} | custom-call | tf_op jit(solution)/shard_map/pallas_call | solution.py:475
  68.7 2.3 %collective-permute-start.9 = (f32[1,2,256,256]{3,2,1,0:T(8,128)S(1)}, f32[1,2,256,256]{3,2,1,0:T(8,128)S(1)}, u32[]{:S(2)}, u32[]{:S(2)}) collective-permute-start(f32[1,2,256,256]{3,2,1,0:T(8,128)S(1)} %get-tuple-element.58), channel_id=1, source_target_pairs={{28,0},{0,4},{4,8},{8,12},{12,16},{16,20},{20,24},{24,28},{29,1},{... | collective-permute-start | bytes 1572872 | tf_op jit(solution)/shard_map/ppermute | solution.py:20
  71.1 28.6 %collective-permute-done.10 = f32[1,2,256,256]{3,2,1,0:T(8,128)S(1)} collective-permute-done((f32[1,2,256,256]{3,2,1,0:T(8,128)S(1)}, f32[1,2,256,256]{3,2,1,0:T(8,128)S(1)}, u32[]{:S(2)}, u32[]{:S(2)}) %collective-permute-start.10) | collective-permute-done | bytes 524320 | tf_op jit(solution)/shard_map/ppermute | solution.py:20
  99.7 0.3 collective-permute-start.11
  100.1 5.2 %collective-permute-done.14 = f32[1,2,256,256]{3,2,1,0:T(8,128)S(1)} collective-permute-done((f32[1,2,256,256]{3,2,1,0:T(8,128)S(1)}, f32[1,2,256,256]{3,2,1,0:T(8,128)S(1)}, u32[]{:S(2)}, u32[]{:S(2)}) %collective-permute-start.14) | collective-permute-done | bytes 524320 | tf_op jit(solution)/shard_map/ppermute | solution.py:20
  105.6 2.0 %store.1.gradient_in = f32[2,2,512,512]{3,2,1,0:T(8,128)} custom-call(f32[2,2,6,768,128]{4,3,2,1,0:T(8,128)S(1)} %get-tuple-element.57.gradient), custom_call_target="tpu_custom_call" | custom-call | tf_op jit(solution)/shard_map/store/pallas_call | solution.py:562
  107.6 1.8 %shard_map.88.gradient_in = f32[2,2,512,512]{3,2,1,0:T(8,128)} custom-call(f32[2,2,512,512]{3,2,1,0:T(8,128)} %store.1.gradient_in, f32[1,2,256,256]{3,2,1,0:T(8,128)S(1)} %collective-permute-done.9.piece_ref), custom_call_target="tpu_custom_call", output_to_operand_aliasing={{}: (0, {})} | custom-call | tf_op jit(solution)/shard_map/pallas_call | solution.py:420
  109.5 7.8 %collective-permute-done.11.piece_ref = f32[1,2,256,256]{3,2,1,0:T(8,128)S(1)} collective-permute-done((f32[1,2,256,256]{3,2,1,0:T(8,128)S(1)}, f32[1,2,256,256]{3,2,1,0:T(8,128)S(1)}, u32[]{:S(2)}, u32[]{:S(2)}) %collective-permute-start.11) | collective-permute-done | bytes 524320 | tf_op jit(solution)/shard_map/ppermute | solution.py:20
  117.3 1.8 %shard_map.89.gradient_in = f32[2,2,512,512]{3,2,1,0:T(8,128)} custom-call(f32[2,2,512,512]{3,2,1,0:T(8,128)} %shard_map.88.gradient_in, f32[1,2,256,256]{3,2,1,0:T(8,128)S(1)} %collective-permute-done.11.piece_ref), custom_call_target="tpu_custom_call", output_to_operand_aliasing={{}: (0, {})} | custom-call | tf_op jit(solution)/shard_map/pallas_call | solution.py:420
  119.1 2.5 %shard_map.90.gradient_in = f32[2,2,512,512]{3,2,1,0:T(8,128)} custom-call(f32[2,2,512,512]{3,2,1,0:T(8,128)} %shard_map.89.gradient_in, f32[2,2,512,256]{3,2,1,0:T(8,128)S(1)} %collective-permute-done.12.piece_ref), custom_call_target="tpu_custom_call", output_to_operand_aliasing={{}: (0, {})} | custom-call | tf_op jit(solution)/shard_map/pallas_call | solution.py:420
  121.6 6.3 %collective-permute-done.13.piece_ref = f32[1,2,256,256]{3,2,1,0:T(8,128)S(1)} collective-permute-done((f32[1,2,256,256]{3,2,1,0:T(8,128)S(1)}, f32[1,2,256,256]{3,2,1,0:T(8,128)S(1)}, u32[]{:S(2)}, u32[]{:S(2)}) %collective-permute-start.13) | collective-permute-done | bytes 524320 | tf_op jit(solution)/shard_map/ppermute | solution.py:20
  127.9 1.8 %shard_map.91.gradient.gradient_in = f32[2,2,512,512]{3,2,1,0:T(8,128)} custom-call(f32[2,2,512,512]{3,2,1,0:T(8,128)} %shard_map.90.gradient_in, f32[1,2,256,256]{3,2,1,0:T(8,128)S(1)} %collective-permute-done.13.piece_ref), custom_call_target="tpu_custom_call", output_to_operand_aliasing={{}: (0, {})} | custom-call | tf_op jit(solution)/shard_map/pallas_call | solution.py:420
  129.7 1.0 hold.1.held
  130.8 2.7 %collective-permute-done.15.piece = f32[1,2,256,256]{3,2,1,0:T(8,128)S(1)} collective-permute-done((f32[1,2,256,256]{3,2,1,0:T(8,128)S(1)}, f32[1,2,256,256]{3,2,1,0:T(8,128)S(1)}, u32[]{:S(2)}, u32[]{:S(2)}) %collective-permute-start.15) | collective-permute-done | bytes 524320 | tf_op jit(solution)/shard_map/ppermute | solution.py:20
  133.5 0.8 addn0.1
  (33 shorter events, 1.0 us)
Async XLA Ops:
  0.0 31.4 %copy-start.5 = (s32[1,1,4,2]{2,3,1,0:T(2,128)S(1)}, s32[1,1,4,2]{2,3,1,0:T(2,128)}, u32[]{:S(2)}) copy-start(s32[1,1,4,2]{2,3,1,0:T(2,128)} %param.11) | copy-start | bytes 100
  1.1 47.0 %copy-start = (f32[2,256,256]{2,1,0:T(8,128)S(1)}, f32[2,256,256]{2,1,0:T(8,128)}, u32[]{:S(2)}) copy-start(f32[2,256,256]{2,1,0:T(8,128)} %rest_0_.9) | copy-start | bytes 1572868
  1.1 47.0 %copy-start.1 = (bf16[1,1,4,256,256]{4,3,2,1,0:T(8,128)(2,1)S(1)}, bf16[1,1,4,256,256]{4,3,2,1,0:T(8,128)(2,1)}, u32[]{:S(2)}) copy-start(bf16[1,1,4,256,256]{4,3,2,1,0:T(8,128)(2,1)} %param.13) | copy-start | bytes 1572868
  1.1 47.0 %copy-start.2 = (bf16[512,512]{1,0:T(8,128)(2,1)S(1)}, bf16[512,512]{1,0:T(8,128)(2,1)}, u32[]{:S(2)}) copy-start(bf16[512,512]{1,0:T(8,128)(2,1)} %constant.7.clone.rest_4_) | copy-start | bytes 1572868
  1.1 47.0 %copy-start.3 = (bf16[512,512]{1,0:T(8,128)(2,1)S(1)}, bf16[512,512]{1,0:T(8,128)(2,1)}, u32[]{:S(2)}) copy-start(bf16[512,512]{1,0:T(8,128)(2,1)} %constant.6.clone.rest_3_) | copy-start | bytes 1572868
  1.2 18.4 %collective-permute-start.5 = (f32[1,2,256,256]{3,2,1,0:T(8,128)S(1)}, f32[1,2,256,256]{3,2,1,0:T(8,128)}, u32[]{:S(2)}, u32[]{:S(2)}) collective-permute-start(f32[1,2,256,256]{3,2,1,0:T(8,128)S(1)} %pack0.1), channel_id=1, source_target_pairs={{4,0},{8,4},{12,8},{16,12},{20,16},{24,20},{28,24},{0,28},{5,1},{9... | collective-permute-start | bytes 1572872 | tf_op jit(solution)/shard_map/ppermute | solution.py:20
  10.7 0.7 copy-start.4
  11.5 43.9 %collective-permute-start.8 = (f32[1,2,512,256]{3,2,1,0:T(8,128)}, f32[1,2,512,256]{3,2,1,0:T(8,128)}, u32[]{:S(2)}, u32[]{:S(2)}) collective-permute-start(f32[1,2,512,256]{3,2,1,0:T(8,128)} %get-tuple-element.40), channel_id=1, source_target_pairs={{1,0},{2,1},{3,2},{0,3},{5,4},{6,5},{7,6},{4,7},{9,8},{10,9},{11,1... | collective-permute-start | bytes 3145736 | tf_op jit(solution)/shard_map/ppermute | solution.py:20
  12.1 18.6 %collective-permute-start.1 = (f32[1,2,256,256]{3,2,1,0:T(8,128)S(1)}, f32[1,2,256,256]{3,2,1,0:T(8,128)}, u32[]{:S(2)}, u32[]{:S(2)}) collective-permute-start(f32[1,2,256,256]{3,2,1,0:T(8,128)S(1)} %get-tuple-element.36), channel_id=1, source_target_pairs={{4,0},{8,4},{12,8},{16,12},{20,16},{24,20},{28,24},{0,28},{5,1},{9... | collective-permute-start | bytes 1572872 | tf_op jit(solution)/shard_map/ppermute | solution.py:20
  12.8 46.7 %collective-permute-start.3 = (f32[1,2,512,256]{3,2,1,0:T(8,128)}, f32[1,2,512,256]{3,2,1,0:T(8,128)S(1)}, u32[]{:S(2)}, u32[]{:S(2)}) collective-permute-start(f32[1,2,512,256]{3,2,1,0:T(8,128)} %get-tuple-element.37), channel_id=1, source_target_pairs={{1,0},{2,1},{3,2},{0,3},{5,4},{6,5},{7,6},{4,7},{9,8},{10,9},{11,1... | collective-permute-start | bytes 3145736 | tf_op jit(solution)/shard_map/ppermute | solution.py:20
  13.4 27.6 %collective-permute-start.6 = (f32[1,2,256,256]{3,2,1,0:T(8,128)}, f32[1,2,256,256]{3,2,1,0:T(8,128)}, u32[]{:S(2)}, u32[]{:S(2)}) collective-permute-start(f32[1,2,256,256]{3,2,1,0:T(8,128)} %get-tuple-element.39), channel_id=1, source_target_pairs={{4,0},{8,4},{12,8},{16,12},{20,16},{24,20},{28,24},{0,28},{5,1},{9... | collective-permute-start | bytes 1572872 | tf_op jit(solution)/shard_map/ppermute | solution.py:20
  19.5 26.6 %collective-permute-start.7 = (f32[1,2,256,256]{3,2,1,0:T(8,128)}, f32[1,2,256,256]{3,2,1,0:T(8,128)}, u32[]{:S(2)}, u32[]{:S(2)}) collective-permute-start(f32[1,2,256,256]{3,2,1,0:T(8,128)} %collective-permute-done.5.near_ref), channel_id=1, source_target_pairs={{1,0},{2,1},{3,2},{0,3},{5,4},{6,5},{7,6},{4,7},{9,8},{10,9},{11,1... | collective-permute-start | bytes 1572872 | tf_op jit(solution)/shard_map/ppermute | solution.py:20
  30.8 28.8 %collective-permute-start.2 = (f32[1,2,256,256]{3,2,1,0:T(8,128)}, f32[1,2,256,256]{3,2,1,0:T(8,128)}, u32[]{:S(2)}, u32[]{:S(2)}) collective-permute-start(f32[1,2,256,256]{3,2,1,0:T(8,128)} %collective-permute-done.1.near_ref), channel_id=1, source_target_pairs={{1,0},{2,1},{3,2},{0,3},{5,4},{6,5},{7,6},{4,7},{9,8},{10,9},{11,1... | collective-permute-start | bytes 1572872 | tf_op jit(solution)/shard_map/ppermute | solution.py:20
  41.0 22.7 %collective-permute-start = (f32[1,2,128,256]{3,2,1,0:T(8,128)S(1)}, f32[1,2,128,256]{3,2,1,0:T(8,128)S(1)}, u32[]{:S(2)}, u32[]{:S(2)}) collective-permute-start(f32[1,2,128,256]{3,2,1,0:T(8,128)S(1)} %get-tuple-element.35), channel_id=1, source_target_pairs={{4,0},{8,4},{12,8},{16,12},{20,16},{24,20},{28,24},{0,28},{5,1},{9... | collective-permute-start | bytes 786440 | tf_op jit(solution)/shard_map/ppermute | solution.py:20
  46.1 13.4 %collective-permute-start.4 = (f32[1,2,128,256]{3,2,1,0:T(8,128)}, f32[1,2,128,256]{3,2,1,0:T(8,128)S(1)}, u32[]{:S(2)}, u32[]{:S(2)}) collective-permute-start(f32[1,2,128,256]{3,2,1,0:T(8,128)} %copy-done.4), channel_id=1, source_target_pairs={{4,0},{8,4},{12,8},{16,12},{20,16},{24,20},{28,24},{0,28},{5,1},{9... | collective-permute-start | bytes 786440 | tf_op jit(solution)/shard_map/ppermute | solution.py:20
  68.5 50.6 %collective-permute-start.12 = (f32[2,2,512,256]{3,2,1,0:T(8,128)S(1)}, f32[2,2,512,256]{3,2,1,0:T(8,128)S(1)}, u32[]{:S(2)}, u32[]{:S(2)}) collective-permute-start(f32[2,2,512,256]{3,2,1,0:T(8,128)S(1)} %get-tuple-element.61), channel_id=1, source_target_pairs={{3,0},{0,1},{1,2},{2,3},{7,4},{4,5},{5,6},{6,7},{11,8},{8,9},{9,10... | collective-permute-start | bytes 6291464 | tf_op jit(solution)/shard_map/ppermute | solution.py:20
  68.6 31.1 %collective-permute-start.10 = (f32[1,2,256,256]{3,2,1,0:T(8,128)S(1)}, f32[1,2,256,256]{3,2,1,0:T(8,128)S(1)}, u32[]{:S(2)}, u32[]{:S(2)}) collective-permute-start(f32[1,2,256,256]{3,2,1,0:T(8,128)S(1)} %get-tuple-element.60), channel_id=1, source_target_pairs={{3,0},{0,1},{1,2},{2,3},{7,4},{4,5},{5,6},{6,7},{11,8},{8,9},{9,10... | collective-permute-start | bytes 1572872 | tf_op jit(solution)/shard_map/ppermute | solution.py:20
  68.7 36.6 %collective-permute-start.14 = (f32[1,2,256,256]{3,2,1,0:T(8,128)S(1)}, f32[1,2,256,256]{3,2,1,0:T(8,128)S(1)}, u32[]{:S(2)}, u32[]{:S(2)}) collective-permute-start(f32[1,2,256,256]{3,2,1,0:T(8,128)S(1)} %get-tuple-element.64), channel_id=1, source_target_pairs={{3,0},{0,1},{1,2},{2,3},{7,4},{4,5},{5,6},{6,7},{11,8},{8,9},{9,10... | collective-permute-start | bytes 1572872 | tf_op jit(solution)/shard_map/ppermute | solution.py:20
  68.7 38.9 %collective-permute-start.9 = (f32[1,2,256,256]{3,2,1,0:T(8,128)S(1)}, f32[1,2,256,256]{3,2,1,0:T(8,128)S(1)}, u32[]{:S(2)}, u32[]{:S(2)}) collective-permute-start(f32[1,2,256,256]{3,2,1,0:T(8,128)S(1)} %get-tuple-element.58), channel_id=1, source_target_pairs={{28,0},{0,4},{4,8},{8,12},{12,16},{16,20},{20,24},{24,28},{29,1},{... | collective-permute-start | bytes 1572872 | tf_op jit(solution)/shard_map/ppermute | solution.py:20
  99.7 17.5 %collective-permute-start.11 = (f32[1,2,256,256]{3,2,1,0:T(8,128)S(1)}, f32[1,2,256,256]{3,2,1,0:T(8,128)S(1)}, u32[]{:S(2)}, u32[]{:S(2)}) collective-permute-start(f32[1,2,256,256]{3,2,1,0:T(8,128)S(1)} %add.6), channel_id=1, source_target_pairs={{28,0},{0,4},{4,8},{8,12},{12,16},{16,20},{20,24},{24,28},{29,1},{... | collective-permute-start | bytes 1572872 | tf_op jit(solution)/shard_map/ppermute | solution.py:20
  100.0 27.9 %collective-permute-start.13 = (f32[1,2,256,256]{3,2,1,0:T(8,128)S(1)}, f32[1,2,256,256]{3,2,1,0:T(8,128)S(1)}, u32[]{:S(2)}, u32[]{:S(2)}) collective-permute-start(f32[1,2,256,256]{3,2,1,0:T(8,128)S(1)} %get-tuple-element.62), channel_id=1, source_target_pairs={{28,0},{0,4},{4,8},{8,12},{12,16},{16,20},{20,24},{24,28},{29,1},{... | collective-permute-start | bytes 1572872 | tf_op jit(solution)/shard_map/ppermute | solution.py:20
  105.3 28.2 %collective-permute-start.15 = (f32[1,2,256,256]{3,2,1,0:T(8,128)S(1)}, f32[1,2,256,256]{3,2,1,0:T(8,128)S(1)}, u32[]{:S(2)}, u32[]{:S(2)}) collective-permute-start(f32[1,2,256,256]{3,2,1,0:T(8,128)S(1)} %add.7), channel_id=1, source_target_pairs={{28,0},{0,4},{4,8},{8,12},{12,16},{16,20},{20,24},{24,28},{29,1},{... | collective-permute-start | bytes 1572872 | tf_op jit(solution)/shard_map/ppermute | solution.py:20
